TPU v7x, 256 devices: a whole 4x4x8 slice. The times are simulated.
256 devices in a mesh: rows: 8 (over y, core), cols: 16 (over z_hi, x), hub: 2 (over z_lo).
Axes of the slice: x: 4, y: 4, z: 8 (z_hi: 4, z_lo: 2; z = z_hi * 2 + z_lo), core: 2. Of those that a mesh axis runs over, the one named last changes fastest.
Arguments:
- light_bits: int32 [384, 12288], P('rows', 'cols'), may hold values from -2147483648 to 2147483647, as said below
- hub_bits: int32 [8, 12288], P('hub', 'cols'), may hold values from -2147483648 to 2147483647, as said below
- hub_ids: int32 [256], replicated, may hold values from 0 to 12287, as said below
Outputs:
- clustering: float32 [12288], P(('rows', 'cols'))
Inputs may be any that keep to these rules, and one draw needn't show every extreme that they name: Every word holds 32 bits; the matrix of light_bits is symmetric with a zero diagonal. `hub_bits`: every word holds 32 bits. `hub_ids`: 256 distinct vertex numbers.
All inputs are finite; a program needn't handle non-finite values.
Results may differ from a plain program's by a relative error of at most 0.0003.
Values sent between devices are 32-bit elements; how exact they have to be, the bound alone decides.
No kernel may reach another device: no remote copies, remote signals or barrier semaphores. Data moves between devices by JAX's collectives and lax.ppermute only.
A program may use at most 128 MiB of HBM per device.

v0:
```python
import jax
import jax.numpy as jnp
from jax import lax
from jax.sharding import Mesh
from jax.sharding import PartitionSpec as P

ROWS = ("rows_0", "rows_1")
COLS = ("cols_0", "cols_1")
ROWS_COLS_HUB = ("rows_0", "rows_1", "cols_0", "cols_1", "hub")
COLS_HUB = ("cols_0", "cols_1", "hub")
ROWS_COLS = ("rows_0", "rows_1", "cols_0", "cols_1")


def in_order(pieces, dim):
    pieces = jnp.moveaxis(pieces, 0, dim)
    shape = pieces.shape
    return pieces.reshape(*shape[:dim], shape[dim] * shape[dim + 1], *shape[dim + 2 :])


def from_everyone(value, axis):
    copies = jnp.broadcast_to(value, (lax.axis_size(axis), *value.shape))
    return lax.all_to_all(copies, axis, split_axis=0, concat_axis=0, tiled=True)


def gathered_copies(value, axis, dim):
    return in_order(from_everyone(value, axis), dim)


def by_axis(value, axes):
    for axis in axes:
        value = lax.psum(value, axis)
    return value


def of_everyone(value, axis):
    everything = from_everyone(value, axis)
    return jnp.sum(everything, axis=0)


def together(arrays, axis):
    vector, at, done = (jnp.concatenate([a.reshape(-1) for a in arrays]), 0, [])
    running = of_everyone(vector, axis)
    for a in arrays:
        done.append(running[at : at + a.size].reshape(a.shape))
        at += a.size
    return tuple(done)


def unpack(packed):
    shifts = jnp.arange(32, dtype=jnp.int32)
    bit_grid = jnp.bitwise_and(jnp.right_shift(packed[:, None, :], shifts[None, :, None]), 1)
    return bit_grid.reshape(packed.shape[0] * 32, packed.shape[1]).astype(jnp.bfloat16)


def light_flags(anchor, amount, hub_ids):
    vertex_ids = anchor + lax.iota(jnp.int32, amount)
    is_hub = jnp.any(vertex_ids[:, None] == hub_ids[None, :], axis=1)
    return jnp.where(is_hub, 0.0, 1.0).astype(jnp.bfloat16)


def body(light_bits, hub_bits, hub_ids):
    row_idx = lax.axis_index(ROWS)
    col_idx = lax.axis_index(COLS)
    group_idx = lax.axis_index("hub")
    groups = lax.axis_size("hub")
    col_devices = lax.axis_size(COLS)
    block_words = light_bits.shape[0]
    block_rows = 32 * block_words
    block_cols = light_bits.shape[1]
    row_base = row_idx * block_rows
    col_base = col_idx * block_cols
    row_keep = light_flags(row_base, block_rows, hub_ids)
    col_keep = light_flags(col_base, block_cols, hub_ids)
    adjacent = unpack(light_bits) * row_keep[:, None] * col_keep[None, :]
    part_words = block_words // groups
    part_rows = 32 * part_words
    row_start = group_idx * part_rows
    row_words = lax.dynamic_slice_in_dim(light_bits, group_idx * part_words, part_words, 0)
    col_start = 0
    row_keep_part = lax.dynamic_slice_in_dim(row_keep, row_start, part_rows, 0)
    row_packed = lax.all_gather(row_words, COLS, axis=1, tiled=True)
    section = gathered_copies(light_bits, ROWS, 0)
    vertex_start = 32 * jnp.int32(0)
    section_rows = 32 * section.shape[0]
    keep_mid = light_flags(vertex_start, section_rows, hub_ids)
    column_bits = unpack(section) * keep_mid[:, None]
    row_slice = unpack(row_packed)
    two_paths = jnp.dot(row_slice, column_bits, preferred_element_type=jnp.float32)
    two_paths = two_paths * row_keep_part.astype(jnp.float32)[:, None]
    own_part = lax.dynamic_slice(adjacent, (row_start, col_start), (part_rows, block_cols)).astype(
        jnp.float32
    )
    light_tri = 0.5 * jnp.sum(own_part * two_paths, axis=1)
    light_deg = jnp.sum(own_part, axis=1)
    tri_vec = lax.dynamic_update_slice_in_dim(
        jnp.zeros((block_rows,), jnp.float32), light_tri, row_start, 0
    )
    deg_vec = lax.dynamic_update_slice_in_dim(
        jnp.zeros((block_rows,), jnp.float32), light_deg, row_start, 0
    )
    group_hubs = 32 * hub_bits.shape[0]
    hub_cols = unpack(hub_bits) * col_keep[None, :]
    hub_whole = gathered_copies(hub_bits, COLS, 1)
    hub_here = (
        unpack(lax.dynamic_slice_in_dim(hub_whole, row_base, block_rows, 1)) * row_keep[None, :]
    )
    reach_hub = lax.dot_general(
        hub_cols, adjacent, (((1,), (1,)), ((), ())), preferred_element_type=jnp.float32
    )
    intersect = hub_here.astype(jnp.float32) * reach_hub
    first_col = (col_idx == 0).astype(jnp.float32)
    first_row = (row_idx == 0).astype(jnp.float32)
    tri_vec = tri_vec + jnp.sum(intersect, axis=0)
    deg_vec = deg_vec + first_col * jnp.sum(hub_here.astype(jnp.float32), axis=0)
    hub_tri = 0.5 * jnp.sum(intersect, axis=1)
    hub_deg = first_row * jnp.sum(hub_cols.astype(jnp.float32), axis=1)
    all_hubs = hub_ids.shape[0]
    hub_tri_full = lax.dynamic_update_slice_in_dim(
        jnp.zeros((all_hubs,), jnp.float32), hub_tri, group_idx * group_hubs, 0
    )
    hub_deg_full = lax.dynamic_update_slice_in_dim(
        jnp.zeros((all_hubs,), jnp.float32), hub_deg, group_idx * group_hubs, 0
    )
    hub_tri_full, hub_deg_full = (
        by_axis(hub_tri_full, ROWS_COLS_HUB),
        by_axis(hub_deg_full, ROWS_COLS_HUB),
    )
    per_device = block_rows // col_devices
    tri_whole, deg_whole = together((tri_vec, deg_vec), COLS_HUB)
    tri_mine = lax.dynamic_slice_in_dim(tri_whole, col_idx * per_device, per_device, 0)
    deg_mine = lax.dynamic_slice_in_dim(deg_whole, col_idx * per_device, per_device, 0)
    vertex_ids = row_base + col_idx * per_device + lax.iota(jnp.int32, per_device)
    owners = (vertex_ids[:, None] == hub_ids[None, :]).astype(jnp.float32)
    tri_mine = tri_mine + jnp.sum(owners * hub_tri_full[None, :], axis=1)
    deg_mine = deg_mine + jnp.sum(owners * hub_deg_full[None, :], axis=1)
    return tri_mine / (1.0 + deg_mine)


def solution(mesh):
    finer = Mesh(
        mesh.devices.reshape(4, 2, 4, 4, mesh.shape["hub"]),
        ("rows_0", "rows_1", "cols_0", "cols_1", "hub"),
    )
    placed = (P(ROWS, COLS), P("hub", COLS), P())
    return jax.shard_map(body, mesh=finer, in_specs=placed, out_specs=P(ROWS_COLS), check_vma=False)
```

profile of v0, /device:TPU:8, one launch (start us, length us, event | category | flops | bytes accessed | tf_op | source)
XLA Modules:
  0.0 156.2 jit_solution(6811426682850002151)
XLA Ops:
  6.5 1.5 constant_dynamic-slice_fusion
  8.1 0.0 all-gather.2.cloned.1.call-update
  8.1 1.4 broadcast_in_dim.28
  9.5 11.0 %all-to-all-start = ((s32[16,4,768]{2,1,0:T(4,128)}), s32[16,4,768]{2,1,0:T(4,128)S(1)}, u32[]{:S(2)}, u32[]{:S(2)}) async-start(s32[16,4,768]{2,1,0:T(4,128)} %broadcast_in_dim.28), calls=%async_computation | async-start | bytes 393216 | tf_op jit(solution)/shard_map/all_to_all | solution.py:22
  20.5 2.6 %fusion.1 = pred[12288]{0:T(1024)(128)(4,1)S(1)} fusion(s32[256]{0:T(256)} %param.5), kind=kLoop, calls=%fused_computation.4 | loop fusion | flops 6279168 | bytes 13312 | tf_op jit(solution)/shard_map/reduce_or | solution.py:57
  23.1 1.0 compare_reduce_fusion.1
  24.1 1.2 compare_reduce_fusion
  25.3 0.1 shift_right_arithmetic.136
  25.4 0.7 fusion.15
  26.1 0.1 dynamic-slice.2
  26.2 1.3 shift_right_arithmetic.131
  27.5 1.6 %constant_dynamic-slice_fusion.1 = s32[768,768]{1,0:T(8,128)} fusion(s32[1536,768]{1,0:T(8,128)S(1)} %bitcast.23, s32[]{:T(128)S(6)} %select_n.54), kind=kLoop, calls=%fused_computation.42 | loop fusion | bytes 4718596 | tf_op jit(solution)/shard_map/dynamic_slice | solution.py:90
  29.0 2.0 %copy.15 = s32[768,768]{0,1:T(8,128)S(1)} copy(s32[768,768]{1,0:T(8,128)} %constant_dynamic-slice_fusion.1) | data formatting | bytes 4718592
  31.1 1.1 convert_reduce_fusion
  32.2 0.7 fusion.11
  32.9 0.1 convert_element_type.113
  33.0 0.6 shift_right_arithmetic.125
  33.6 0.7 convert_element_type.120
  34.3 2.3 %fusion.4 = bf16[48,32,768]{2,1,0:T(8,128)(2,1)} fusion(s32[48,768]{1,0:T(8,128)S(1)} %copy-done, bf16[768]{0:T(1024)(128)(2,1)S(1)} %select_convert_fusion.2, bf16[48,32]{1,0:T(8,128)(2,1)S(1)} %convert_element_type.113), kind=kLoop, calls=%fused_computation.11 | loop fusion | flops 10616832 | bytes 2511360 | tf_op jit(solution)/shard_map/mul | solution.py:74
  36.6 1.1 broadcast_in_dim.32
  37.8 4.9 %all-to-all-start.1 = ((s32[8,48,768]{2,1,0:T(8,128)}), s32[8,48,768]{2,1,0:T(8,128)S(1)}, u32[]{:S(2)}, u32[]{:S(2)}) async-start(s32[8,48,768]{2,1,0:T(8,128)} %broadcast_in_dim.32), calls=%async_computation.1 | async-start | bytes 2359296 | tf_op jit(solution)/shard_map/all_to_all | solution.py:22
  42.7 0.7 constant_dynamic-slice_fusion.2
  43.4 0.8 fusion.10
  44.3 0.1 convert_reduce_fusion.1
  44.4 0.6 broadcast_multiply_fusion
  45.0 1.5 add_dynamic-update-slice_fusion
  46.5 3.4 %fusion.14 = (f32[128]{0:T(128)S(1)}, f32[1536]{0:T(1024)}) fusion(bf16[128,768]{1,0:T(8,128)(2,1)} %bitcast.26, bf16[1536,768]{1,0:T(8,128)(2,1)} %bitcast.24, bf16[128,1536]{1,0:T(8,128)(2,1)S(1)} %fusion.10), kind=kOutput, calls=%fused_computation.47 | convolution fusion | flops 302774656 | bytes 2955776 | tf_op jit(solution)/shard_map/dot_general | solution.py:107
  49.9 8.7 %all-to-all-done.1 = s32[8,48,768]{2,1,0:T(8,128)S(1)} async-done(((s32[8,48,768]{2,1,0:T(8,128)}), s32[8,48,768]{2,1,0:T(8,128)S(1)}, u32[]{:S(2)}, u32[]{:S(2)}) %all-to-all-start.1) | async-done | bytes 1179680 | tf_op jit(solution)/shard_map/all_to_all | solution.py:22
  58.6 9.2 %fusion = bf16[384,32,768]{2,1,0:T(8,128)(2,1)} fusion(s32[384,768]{1,0:T(8,128)S(1)} %bitcast.25, bf16[384,32]{1,0:T(8,128)(2,1)} %convert_element_type.120), kind=kLoop, calls=%fused_computation.2 | loop fusion | flops 66060288 | bytes 20078592 | tf_op jit(solution)/shard_map/mul | solution.py:86
  67.8 0.0 all-gather.2.cloned.1.call-done
  67.8 8.0 %and_convert_fusion.1 = bf16[24,32,12288]{2,1,0:T(8,128)(2,1)} fusion(s32[24,12288]{1,0:T(8,128)} %all-gather.2.cloned.1.call-done), kind=kLoop, calls=%fused_computation.1 | loop fusion | flops 28311552 | bytes 20054016 | tf_op jit(solution)/shard_map/convert_element_type | solution.py:52
  75.8 20.7 %fusion.2 = f32[768]{0:T(1024)S(1)} fusion(bf16[768,12288]{1,0:T(8,128)(2,1)} %bitcast.22, bf16[12288,768]{1,0:T(8,128)(2,1)} %bitcast.21, f32[768]{0:T(1024)S(1)} %copy-done.11, bf16[768]{0:T(1024)(128)(2,1)S(1)} %copy-done.5, bf16[768]{0:T(1024)(128)(2,1)S(1)} %copy-done.10, s32[768,768]{0,1:T(8,128)S(1)} %copy.15, s32[768]{0:T(1024)S(1)} %copy-done.7), kind=kOutput, calls=%fused_computation.9 | convolution fusion | flops 14502591488 | bytes 40120320 | tf_op jit(solution)/shard_map/dot_general | solution.py:88
  96.5 0.2 add_dynamic-update-slice_fusion.1
  96.7 0.7 pad_maximum_fusion
  97.4 0.9 broadcast_in_dim.35
  98.3 9.9 %all-to-all-start.2 = ((f32[32,1,3072]{2,1,0:T(1,128)}), f32[32,1,3072]{2,1,0:T(1,128)S(1)}, u32[]{:S(2)}, u32[]{:S(2)}) async-start(f32[32,1,3072]{2,1,0:T(1,128)} %broadcast_in_dim.35), calls=%async_computation.2 | async-start | bytes 786432 | tf_op jit(solution)/shard_map/all_to_all | solution.py:22
  108.2 0.1 convert_reduce_fusion.2
  108.4 0.1 mul.216
  108.5 0.2 dynamic_update_slice.15
  108.7 0.1 multiply_dynamic-update-slice_fusion
  108.8 9.2 %all-reduce.2 = (f32[256]{0:T(256)S(1)}, f32[256]{0:T(256)S(1)}) all-reduce(f32[256]{0:T(256)S(1)} %multiply_dynamic-update-slice_fusion, f32[256]{0:T(256)S(1)} %dynamic_update_slice.15), channel_id=1, replica_groups=mesh['rows_0'=4,'rows_1'=2,'cols_0'=4,'cols_1'=4,'hub'=2] {'rows_0'}, use_global_device_ids=true, to_apply=%region_9.10 | all-reduce | flops 512 | bytes 4096 | tf_op jit(solution)/shard_map/psum | solution.py:31
  117.9 2.5 %all-reduce.4 = (f32[256]{0:T(256)S(1)}, f32[256]{0:T(256)S(1)}) all-reduce(f32[256]{0:T(256)S(1)} %get-tuple-element.13, f32[256]{0:T(256)S(1)} %get-tuple-element.14), channel_id=1, replica_groups=mesh['rows_0'=4,'rows_1'=2,'cols_0'=4,'cols_1'=4,'hub'=2] {'rows_1'}, use_global_device_ids=true, to_apply=%region_10.11 | all-reduce | flops 512 | bytes 4096 | tf_op jit(solution)/shard_map/psum | solution.py:31
  120.4 12.6 %all-reduce.1 = (f32[256]{0:T(256)S(1)}, f32[256]{0:T(256)S(1)}) all-reduce(f32[256]{0:T(256)S(1)} %get-tuple-element.17, f32[256]{0:T(256)S(1)} %get-tuple-element.18), channel_id=1, replica_groups=mesh['rows_0'=4,'rows_1'=2,'cols_0'=4,'cols_1'=4,'hub'=2] {'cols_0'}, use_global_device_ids=true, to_apply=%region_11.12 | all-reduce | flops 512 | bytes 4096 | tf_op jit(solution)/shard_map/psum | solution.py:31
  133.0 10.4 %all-reduce = (f32[256]{0:T(256)S(1)}, f32[256]{0:T(256)S(1)}) all-reduce(f32[256]{0:T(256)S(1)} %get-tuple-element.11, f32[256]{0:T(256)S(1)} %get-tuple-element.12), channel_id=1, replica_groups=mesh['rows_0'=4,'rows_1'=2,'cols_0'=4,'cols_1'=4,'hub'=2] {'cols_1'}, use_global_device_ids=true, to_apply=%region_12.13 | all-reduce | flops 512 | bytes 4096 | tf_op jit(solution)/shard_map/psum | solution.py:31
  143.4 4.9 %all-reduce.3 = (f32[256]{0:T(256)S(1)}, f32[256]{0:T(256)S(1)}) all-reduce(f32[256]{0:T(256)S(1)} %get-tuple-element.9, f32[256]{0:T(256)S(1)} %get-tuple-element.10), channel_id=1, replica_groups=mesh['rows_0'=4,'rows_1'=2,'cols_0'=4,'cols_1'=4,'hub'=2] {'hub'}, use_global_device_ids=true, to_apply=%region_13.14 | all-reduce | flops 512 | bytes 4096 | tf_op jit(solution)/shard_map/psum | solution.py:31
  148.3 0.2 fusion.12
  148.5 0.2 reduce_sum.88
  148.7 0.6 add_divide_fusion
  (39 shorter events, 0.1 us)
Async XLA Ops:
  6.5 61.2 %all-gather.2.cloned.1.call-start = ((), (), s32[]{:S(2)}) async-start(), calls=%async_computation.3 | async-start | bytes 1253376 | tf_op jit(solution)/shard_map/all_gather | solution.py:81
  9.5 27.2 %all-to-all-start = ((s32[16,4,768]{2,1,0:T(4,128)}), s32[16,4,768]{2,1,0:T(4,128)S(1)}, u32[]{:S(2)}, u32[]{:S(2)}) async-start(s32[16,4,768]{2,1,0:T(4,128)} %broadcast_in_dim.28), calls=%async_computation | async-start | bytes 393216 | tf_op jit(solution)/shard_map/all_to_all | solution.py:22
  24.1 10.2 %copy-start.4 = (bf16[768]{0:T(1024)(128)(2,1)}, bf16[768]{0:T(1024)(128)(2,1)S(1)}, u32[]{:S(2)}) copy-start(bf16[768]{0:T(1024)(128)(2,1)S(1)} %select_convert_fusion.2) | copy-start | bytes 4612
  26.1 5.0 %copy-start.9 = (bf16[768]{0:T(1024)(128)(2,1)}, bf16[768]{0:T(1024)(128)(2,1)S(1)}, u32[]{:S(2)}) copy-start(bf16[768]{0:T(1024)(128)(2,1)S(1)} %get-tuple-element.20) | copy-start | bytes 4612
  26.2 4.9 %copy-start.6 = (s32[768]{0:T(1024)}, s32[768]{0:T(1024)S(1)}, u32[]{:S(2)}) copy-start(s32[768]{0:T(1024)S(1)} %dynamic-slice.2) | copy-start | bytes 9220
  31.1 1.1 copy-start.2
  31.1 3.3 %copy-start = (s32[48,768]{1,0:T(8,128)S(1)}, s32[48,768]{1,0:T(8,128)}, u32[]{:S(2)}) copy-start(s32[48,768]{1,0:T(8,128)} %param.3) | copy-start | bytes 442372
  36.6 1.1 copy-start.1
  37.8 20.8 %all-to-all-start.1 = ((s32[8,48,768]{2,1,0:T(8,128)}), s32[8,48,768]{2,1,0:T(8,128)S(1)}, u32[]{:S(2)}, u32[]{:S(2)}) async-start(s32[8,48,768]{2,1,0:T(8,128)} %broadcast_in_dim.32), calls=%async_computation.1 | async-start | bytes 2359296 | tf_op jit(solution)/shard_map/all_to_all | solution.py:22
  67.7 8.0 %copy-start.5 = (bf16[768]{0:T(1024)(128)(2,1)S(1)}, bf16[768]{0:T(1024)(128)(2,1)}, u32[]{:S(2)}) copy-start(bf16[768]{0:T(1024)(128)(2,1)} %copy-done.4) | copy-start | bytes 4612
  67.7 8.0 %copy-start.7 = (s32[768]{0:T(1024)S(1)}, s32[768]{0:T(1024)}, u32[]{:S(2)}) copy-start(s32[768]{0:T(1024)} %copy-done.6) | copy-start | bytes 9220
  67.7 8.0 %copy-start.10 = (bf16[768]{0:T(1024)(128)(2,1)S(1)}, bf16[768]{0:T(1024)(128)(2,1)}, u32[]{:S(2)}) copy-start(bf16[768]{0:T(1024)(128)(2,1)} %copy-done.9) | copy-start | bytes 4612
  67.8 8.0 %copy-start.11 = (f32[768]{0:T(1024)S(1)}, f32[768]{0:T(1024)}, u32[]{:S(2)}) copy-start(f32[768]{0:T(1024)} %get-tuple-element.19) | copy-start | bytes 9220
  75.8 20.7 %copy-start.3 = (f32[1536]{0:T(1024)S(1)}, f32[1536]{0:T(1024)}, u32[]{:S(2)}) copy-start(f32[1536]{0:T(1024)} %get-tuple-element.6) | copy-start | bytes 18436
  75.8 72.5 %copy-start.8 = (s32[256]{0:T(256)S(1)}, s32[256]{0:T(256)}, u32[]{:S(2)}) copy-start(s32[256]{0:T(256)} %param.5) | copy-start | bytes 3076
  98.3 50.1 %all-to-all-start.2 = ((f32[32,1,3072]{2,1,0:T(1,128)}), f32[32,1,3072]{2,1,0:T(1,128)S(1)}, u32[]{:S(2)}, u32[]{:S(2)}) async-start(f32[32,1,3072]{2,1,0:T(1,128)} %broadcast_in_dim.35), calls=%async_computation.2 | async-start | bytes 786432 | tf_op jit(solution)/shard_map/all_to_all | solution.py:22
Sparse Core Ops, SparseCore 0:
  9.8 56.5 all-gather.1
where the time goes:
time: 157 us; the launch traced here: 156 us
  blocking collectives  39.5 us (25%)
  other arithmetic  31.9 us (20%)
  starting transfers between devices  25.8 us (16%)
  matrix products  24 us (15%)
  between operations  13.7 us (9%)
  local copies, waits for them, and re-layouts  12.5 us (8%)
  waiting for transfers between devices  8.73 us (6%)
    psum x5, blocking collectives, by_axis(): value = lax.psum(value, axis)  39.5 us
    all_to_all x3, starting transfers between devices, from_everyone(): return lax.all_to_all(copies, axis, split_axis=0, concat_axis=0, tiled=True)  25.8 us
    dot_general x1, matrix products, body(): jnp.dot(row_slice, column_bits, preferred_element_type=jnp.float32)  20.7 us
    mul x1, other arithmetic, body(): column_bits = unpack(section) * keep_mid[:, None]  9.19 us
    all_to_all x3, waiting for transfers between devices, from_everyone(): return lax.all_to_all(copies, axis, split_axis=0, concat_axis=0, tiled=True)  8.7 us
    convert_element_type x1, other arithmetic, unpack(): bit_grid.reshape(packed.shape[0] * 32, packed.shape[1]).astype(jnp.bfloat16)  7.98 us
    reduce_or x3, other arithmetic, light_flags(): is_hub = jnp.any(vertex_ids[:, None] == hub_ids[None, :], axis=1)  4.72 us
    broadcast_in_dim x3, local copies, waits for them, and re-layouts, from_everyone(): copies = jnp.broadcast_to(value, (lax.axis_size(axis), *value.shape))  3.46 us
  transfers between devices with their start and end apart: 4, of which 1 were waited for; matrix products, arithmetic and copies ran while one was open for 23% of the time, Pallas kernels for 0%

commit v1 on v0

v1 whole, which is shorter than its diff:
```python
import functools

import jax
import jax.numpy as jnp
from jax import lax
from jax.experimental import pallas as pl
from jax.experimental.pallas import tpu as pltpu
from jax.sharding import Mesh
from jax.sharding import PartitionSpec as P

AXES = ("y", "core", "zh", "x", "zl")
ROWS = ("y", "core")
COLS = ("zh", "x")
SIZES = (4, 2, 4, 4, 2)
F8 = jnp.float8_e4m3fn
F32 = jnp.float32
I32 = jnp.int32
BITS = 8
OUT = 96


def flat(y, core, zh, x, zl):
    return (((y * 2 + core) * 4 + zh) * 4 + x) * 2 + zl


def permutation(source_of):
    pairs = []
    for y in range(4):
        for core in range(2):
            for zh in range(4):
                for x in range(4):
                    for zl in range(2):
                        s = source_of(y, core, zh, x, zl)
                        if s is not None:
                            pairs.append((flat(*s), flat(y, core, zh, x, zl)))
    return pairs


def slots(zh, zl):
    return ((zh + zl) % 4, (zh + 3 + 3 * zl) % 4)


def z_near(y, core, zh, x, zl):
    return (y, core, (zh + 3) % 4, x, 1) if zl == 0 else (y, core, (zh + 1) % 4, x, 0)


def z_far(y, core, zh, x, zl):
    return None if zl == 0 else (y, core, (zh + 2) % 4, x, 0)


def y_out(y, core, zh, x, zl):
    a, b = slots(zh, zl)
    away = 1 if zl == 0 else 3
    if y == (a + away) % 4:
        return (a, core, zh, x, zl)
    if y == (b - away) % 4:
        return (b, core, zh, x, zl)
    return None


def y_swap(y, core, zh, x, zl):
    a, b = slots(zh, zl)
    away = 1 if zl == 0 else 3
    oa, ob = (a + away) % 4, (b - away) % 4
    return ({a: b, b: a, oa: ob, ob: oa}[y], core, zh, x, zl)


def hub_source(second):
    def source(y, core, zh, x, zl):
        row, col = 2 * y + core, 4 * zh + x
        side = (col // 8) ^ second
        c = 2 * row + side
        r = col % 8
        return (r // 2, r % 2, c // 4, c % 4, zl)

    return source


def unpack(words, dtype):
    n = words.shape[1]
    shifts = lax.broadcasted_iota(I32, (32, n), 0)
    rows = [
        jnp.right_shift(jnp.broadcast_to(words[i : i + 1, :], (32, n)), shifts) & 1
        for i in range(words.shape[0])
    ]
    return jnp.concatenate(rows, 0).astype(F32).astype(dtype)


def find_keep(idc, idr, keep):
    q = (lax.broadcasted_iota(I32, (16, 256), 0) == idr[...] // 768).astype(jnp.bfloat16)
    r = (lax.broadcasted_iota(I32, (256, 768), 1) == idc[...] % 768).astype(jnp.bfloat16)
    count = jnp.dot(q, r, preferred_element_type=F32)
    keep[...] = jnp.where(count > 0.5, 0, -1)


def place():
    y, core = lax.axis_index("y"), lax.axis_index("core")
    zh, x, zl = lax.axis_index("zh"), lax.axis_index("x"), lax.axis_index("zl")
    return y, core, zh, x, zl


def light_kernel(idc, idr, own, r0, rp, rm, r2, yy, yc, tri, deg, keep, lhs, rhs):
    y, core, zh, x, zl = place()
    row, col = 2 * y + core, 4 * zh + x
    groups = (lax.rem(zh + zl, 4), lax.rem(zh + 3 + 3 * zl, 4))
    find_keep(idc, idr, keep)
    w = (lax.broadcasted_iota(I32, (48, 256), 0) + 48 * row == idr[...] // 32).astype(jnp.bfloat16)
    b = (lax.broadcasted_iota(I32, (256, 32), 1) == idc[...] % 32).astype(jnp.bfloat16)
    light = 1.0 - jnp.dot(w, b, preferred_element_type=F32)
    sources = ((r0, 0), (rp, 1), (rm, 3), (r2, 2))
    for n, (ref, rel) in enumerate(sources):
        xs = lax.rem(x + rel, 4)
        other = (xs // 2) != core
        for s in range(2):
            at = pl.multiple_of(48 * s + 24 * lax.rem(xs, 2), 8)
            words = jnp.where(other, yc[pl.ds(at, 24), :], yy[pl.ds(at, 24), :])
            base = (2 * n + s) * 768
            for part in range(3):
                rhs[base + 256 * part : base + 256 * part + 256, :] = unpack(
                    words[8 * part : 8 * part + 8, :], F8
                )
    mine = own[...] & keep[pl.ds(col, 1), :]
    for t in range(32 // BITS):
        for n, (ref, rel) in enumerate(sources):
            xs = lax.rem(x + rel, 4)
            for s in range(2):
                words = ref[48 * s : 48 * s + 48, :] & keep[pl.ds(4 * groups[s] + xs, 1), :]
                bits = jnp.concatenate(
                    [jnp.right_shift(words, t * BITS + b) & 1 for b in range(BITS)], 0
                )
                base = (2 * n + s) * 768
                lhs[t % 2, :, base : base + 768] = bits.astype(F32).astype(F8)
        paths = jnp.dot(lhs[t % 2], rhs[...], preferred_element_type=F32)
        for b in range(BITS):
            at = t * BITS + b
            edge = (jnp.right_shift(mine, at) & 1).astype(F32)
            closed = paths[48 * b : 48 * b + 48, :] * edge
            tri[:, at : at + 1] = jnp.sum(closed, axis=1, keepdims=True)
            deg[:, at : at + 1] = jnp.sum(edge, axis=1, keepdims=True)
    first = (zl == 0).astype(F32)
    tri[...] = 0.5 * tri[...] * light
    deg[...] = first * deg[...] * light


def hub_kernel(idc, idr, own, hub, h1, h2, tri, deg, table, keep, near):
    y, core, zh, x, zl = place()
    row, col = 2 * y + core, 4 * zh + x
    find_keep(idc, idr, keep)
    kc = keep[pl.ds(col, 1), :]
    mine = own[...] & kc
    for part in range(6):
        near[256 * part : 256 * part + 256, :] = unpack(mine[8 * part : 8 * part + 8, :], F8)
    swap = col >= 8
    ha = jnp.where(swap, h2[...], h1[...]) & keep[pl.ds(2 * row, 1), :]
    hb = jnp.where(swap, h1[...], h2[...]) & keep[pl.ds(2 * row + 1, 1), :]
    here = unpack(jnp.concatenate([ha, hb], axis=1), F32)
    cols = unpack(hub[...] & kc, F32)
    reach = lax.dot_general(
        cols.astype(F8), near[...], (((1,), (1,)), ((), ())), preferred_element_type=F32
    )
    both = here * reach
    tri[...] = jnp.sum(both, axis=0, keepdims=True)
    deg[...] = (col == 0).astype(F32) * jnp.sum(here, axis=0, keepdims=True)
    hub_tri = 0.5 * jnp.sum(both, axis=1, keepdims=True)
    hub_deg = (row == 0).astype(F32) * jnp.sum(cols, axis=1, keepdims=True)
    at = pl.multiple_of(zl * 128, 128)
    ids = idc[pl.ds(at, 128), :]
    lane = lax.broadcasted_iota(I32, (128, 128), 1)
    inside = lane == ids % OUT
    block = (lax.broadcasted_iota(I32, (128, 128), 1) == ids // OUT).astype(F32)
    for n, value in enumerate((hub_tri, hub_deg)):
        spread = jnp.where(inside, value, 0.0)
        table[:, 128 * n : 128 * n + 128] = lax.dot_general(
            block,
            spread,
            (((0,), (0,)), ((), ())),
            precision=lax.Precision.HIGHEST,
            preferred_element_type=F32,
        )


def call(kernel, outs, scratch, args, flops):
    vmem = pl.BlockSpec(memory_space=pltpu.VMEM)
    return pl.pallas_call(
        kernel,
        out_shape=[jax.ShapeDtypeStruct(s, F32) for s in outs],
        in_specs=[vmem] * len(args),
        out_specs=[vmem] * len(outs),
        scratch_shapes=scratch,
        cost_estimate=pl.CostEstimate(flops=flops, bytes_accessed=1 << 20, transcendentals=0),
        compiler_params=pltpu.CompilerParams(vmem_limit_bytes=56 * 2**20),
    )(*args)


def body(light_bits, hub_bits, hub_ids):
    y, core, zh, x, zl = place()
    row = 2 * y + core
    idc, idr = hub_ids[:, None], hub_ids[None, :]
    send = functools.partial(lax.ppermute, axis_name=AXES)
    near = send(light_bits, perm=permutation(z_near))
    far = send(light_bits, perm=permutation(z_far))
    even = zl == 0
    group = jnp.concatenate([jnp.where(even, light_bits, near), jnp.where(even, near, far)], 0)
    ring = [
        lax.ppermute(group, "x", [((d + r) % 4, d) for d in range(4)]) for r in (1, 3, 2)
    ]
    out = send(light_bits, perm=permutation(y_out))
    ga, gb = (zh + zl) % 4, (zh + 3 + 3 * zl) % 4
    root = (y == ga) | (y == gb)
    have = jnp.where(root, light_bits, out)
    got = send(have, perm=permutation(y_swap))
    first = (y == ga) | (y == (ga + 1 + 2 * zl) % 4)
    yy = jnp.concatenate([jnp.where(first, have, got), jnp.where(first, got, have)], 0)
    yc = lax.ppermute(yy, "core", [(0, 1), (1, 0)])
    h1 = send(hub_bits, perm=permutation(hub_source(0)))
    h2 = send(hub_bits, perm=permutation(hub_source(1)))
    htri, hdeg, table = call(
        hub_kernel,
        [(1, 1536), (1, 1536), (128, 256)],
        [pltpu.VMEM((16, 768), I32), pltpu.VMEM((1536, 768), F8)],
        (idc, idr, light_bits, hub_bits, h1, h2),
        1 << 29,
    )
    tri, deg = call(
        light_kernel,
        [(48, 32), (48, 32)],
        [
            pltpu.VMEM((16, 768), I32),
            pltpu.VMEM((2, 48 * BITS, 6144), F8),
            pltpu.VMEM((6144, 768), F8),
        ],
        (idc, idr, light_bits, group, *ring, yy, yc),
        1 << 33,
    )
    tri = tri.reshape(16, OUT) + htri.reshape(16, OUT)
    deg = deg.reshape(16, OUT) + hdeg.reshape(16, OUT)
    pad = jnp.zeros((16, 128 - OUT), F32)
    mine = jnp.concatenate([tri, pad, deg, pad], 1)
    table = lax.dynamic_update_slice_in_dim(
        table, lax.dynamic_slice_in_dim(table, 16 * row, 16, 0) + mine, 16 * row, 0
    )
    table = jnp.broadcast_to(table[:, None, :], (128, 2, 256)).reshape(256, 256)
    everyone = lax.all_to_all(table, AXES, 0, 0, tiled=True)
    total = jnp.sum(everyone, axis=0)
    return total[:OUT] / (1.0 + total[128 : 128 + OUT])


def solution(mesh):
    finer = Mesh(mesh.devices.reshape(SIZES), AXES)
    placed = (P(ROWS, COLS), P("zl", COLS), P())
    return jax.shard_map(
        body, mesh=finer, in_specs=placed, out_specs=P(ROWS + COLS), check_vma=False
    )
```

time: 157 us -> 97.8 us (0.62)
  the two profiles are of different devices: /device:TPU:8 before, /device:TPU:1 now
where the time goes in v1:
time: 97.8 us; the launch traced here: 97.3 us
  blocking collectives  33 us (34%)
  starting transfers between devices  28.3 us (29%)
  Pallas kernels  16.9 us (17%)
  waiting for transfers between devices  10.4 us (11%)
  local copies, waits for them, and re-layouts  5.85 us (6%)
  other arithmetic  2.65 us (3%)
    all_to_all x1, blocking collectives, body(): everyone = lax.all_to_all(table, AXES, 0, 0, tiled=True)  33 us
    pallas_call x2, Pallas kernels, call(): pl.pallas_call(kernel, out_shape=[jax.ShapeDtypeStruct(s, F32) for s in o...  16.9 us
    ppermute x1, waiting for transfers between devices, body(): h1 = send(hub_bits, perm=permutation(hub_source(0)))  6.92 us
    ppermute x1, starting transfers between devices, body(): near = send(light_bits, perm=permutation(z_near))  6.39 us
    ppermute x3, starting transfers between devices, body(): lax.ppermute(group, 'x', [((d + r) % 4, d) for d in range(4)])  4.29 us
    ppermute x1, starting transfers between devices, body(): h1 = send(hub_bits, perm=permutation(hub_source(0)))  3.87 us
    unnamed x26, local copies, waits for them, and re-layouts  3.54 us
    ppermute x1, starting transfers between devices, body(): far = send(light_bits, perm=permutation(z_far))  3.53 us
  transfers between devices with their start and end apart: 10, of which 4 were waited for; matrix products, arithmetic and copies ran while one was open for 2% of the time, Pallas kernels for 3%

profile of v1, /device:TPU:1, one launch (start us, length us, event | category | flops | bytes accessed | tf_op | source)
XLA Modules:
  0.0 97.3 jit_solution(6498117799656626712)
XLA Ops:
  0.0 6.4 %collective-permute-start.2 = (s32[48,768]{1,0:T(8,128)}, s32[48,768]{1,0:T(8,128)S(1)}, u32[]{:S(2)}, u32[]{:S(2)}) collective-permute-start(s32[48,768]{1,0:T(8,128)} %own.3), channel_id=1, source_target_pairs={{25,0},{8,1},{27,2},{10,3},{29,4},{12,5},{31,6},{14,7},{1,8},{16,9... | collective-permute-start | bytes 442376 | tf_op jit(solution)/shard_map/ppermute | solution.py:200
  6.4 3.5 %collective-permute-start.3 = (s32[48,768]{1,0:T(8,128)}, s32[48,768]{1,0:T(8,128)S(1)}, u32[]{:S(2)}, u32[]{:S(2)}) collective-permute-start(s32[48,768]{1,0:T(8,128)} %own.3), channel_id=1, source_target_pairs={{16,1},{18,3},{20,5},{22,7},{24,9},{26,11},{28,13},{30,15},{0,17},... | collective-permute-start | bytes 442376 | tf_op jit(solution)/shard_map/ppermute | solution.py:201
  9.9 3.2 %collective-permute-start.7 = (s32[48,768]{1,0:T(8,128)}, s32[48,768]{1,0:T(8,128)S(1)}, u32[]{:S(2)}, u32[]{:S(2)}) collective-permute-start(s32[48,768]{1,0:T(8,128)} %own.3), channel_id=1, source_target_pairs={{65,1},{67,3},{69,5},{71,7},{201,9},{203,11},{205,13},{207,15},{80... | collective-permute-start | bytes 442376 | tf_op jit(solution)/shard_map/ppermute | solution.py:207
  13.2 0.0 collective-permute-done.2
  13.2 0.6 collective-permute-done.3
  13.8 1.7 %collective-permute-done.7 = s32[48,768]{1,0:T(8,128)S(1)} collective-permute-done((s32[48,768]{1,0:T(8,128)}, s32[48,768]{1,0:T(8,128)S(1)}, u32[]{:S(2)}, u32[]{:S(2)}) %collective-permute-start.7) | collective-permute-done | bytes 147488 | tf_op jit(solution)/shard_map/ppermute | solution.py:207
  15.5 0.9 broadcast_select_fusion
  16.5 2.0 %collective-permute-start.8 = (s32[48,768]{1,0:T(8,128)S(1)}, s32[48,768]{1,0:T(8,128)S(1)}, u32[]{:S(2)}, u32[]{:S(2)}) collective-permute-start(s32[48,768]{1,0:T(8,128)S(1)} %get-tuple-element.17), channel_id=1, source_target_pairs={{192,0},{193,1},{194,2},{195,3},{196,4},{197,5},{198,6},{199,7},{7... | collective-permute-start | bytes 442376 | tf_op jit(solution)/shard_map/ppermute | solution.py:211
  18.5 0.0 copy-start
  18.5 2.6 %collective-permute-start.4 = (s32[96,768]{1,0:T(8,128)S(1)}, s32[96,768]{1,0:T(8,128)S(1)}, u32[]{:S(2)}, u32[]{:S(2)}) collective-permute-start(s32[96,768]{1,0:T(8,128)S(1)} %pad_add_fusion.r0), channel_id=1, source_target_pairs={{2,0},{4,2},{6,4},{0,6},{3,1},{5,3},{7,5},{1,7},{10,8},{12,10},{14... | collective-permute-start | bytes 884744 | tf_op jit(solution)/shard_map/ppermute | solution.py:205
  21.1 0.0 collective-permute-start.5
  21.1 1.7 %collective-permute-start.6 = (s32[96,768]{1,0:T(8,128)S(1)}, s32[96,768]{1,0:T(8,128)S(1)}, u32[]{:S(2)}, u32[]{:S(2)}) collective-permute-start(s32[96,768]{1,0:T(8,128)S(1)} %pad_add_fusion.r0), channel_id=1, source_target_pairs={{4,0},{6,2},{0,4},{2,6},{5,1},{7,3},{1,5},{3,7},{12,8},{14,10},{8,... | collective-permute-start | bytes 884744 | tf_op jit(solution)/shard_map/ppermute | solution.py:205
  22.8 0.0 collective-permute-done.8
  22.8 0.0 copy-done
  22.8 0.0 copy-start.10
  22.9 0.0 copy-start.1
  22.9 3.3 %collective-permute-start.9 = (s32[96,768]{1,0:T(8,128)S(1)}, s32[96,768]{1,0:T(8,128)S(1)}, u32[]{:S(2)}, u32[]{:S(2)}) collective-permute-start(s32[96,768]{1,0:T(8,128)S(1)} %pad_add_fusion.1.yy), channel_id=1, source_target_pairs={{0,32},{32,0},{1,33},{33,1},{2,34},{34,2},{3,35},{35,3},{4,36},{36... | collective-permute-start | bytes 884744 | tf_op jit(solution)/shard_map/ppermute | solution.py:214
  26.2 0.0 copy-done.10
  26.2 3.9 %collective-permute-start = (s32[4,768]{1,0:T(4,128)S(1)}, s32[4,768]{1,0:T(4,128)S(1)}, u32[]{:S(2)}, u32[]{:S(2)}) collective-permute-start(s32[4,768]{1,0:T(4,128)S(1)} %copy-done.10), channel_id=1, source_target_pairs={{0,0},{1,1},{32,2},{33,3},{64,4},{65,5},{96,6},{97,7},{128,8},{129... | collective-permute-start | bytes 36872 | tf_op jit(solution)/shard_map/ppermute | solution.py:215
  30.1 6.9 %collective-permute-done.h1 = s32[4,768]{1,0:T(4,128)S(1)} collective-permute-done((s32[4,768]{1,0:T(4,128)S(1)}, s32[4,768]{1,0:T(4,128)S(1)}, u32[]{:S(2)}, u32[]{:S(2)}) %collective-permute-start) | collective-permute-done | bytes 12320 | tf_op jit(solution)/shard_map/ppermute | solution.py:215
  37.0 1.7 %collective-permute-start.1 = (s32[4,768]{1,0:T(4,128)S(1)}, s32[4,768]{1,0:T(4,128)S(1)}, u32[]{:S(2)}, u32[]{:S(2)}) collective-permute-start(s32[4,768]{1,0:T(4,128)S(1)} %copy-done.10), channel_id=1, source_target_pairs={{2,0},{3,1},{34,2},{35,3},{66,4},{67,5},{98,6},{99,7},{130,8},{131... | collective-permute-start | bytes 36872 | tf_op jit(solution)/shard_map/ppermute | solution.py:216
  38.7 0.7 copy-done.5
  39.4 0.8 copy.6.idc
  40.2 1.2 %collective-permute-done.1.h2 = s32[4,768]{1,0:T(4,128)S(1)} collective-permute-done((s32[4,768]{1,0:T(4,128)S(1)}, s32[4,768]{1,0:T(4,128)S(1)}, u32[]{:S(2)}, u32[]{:S(2)}) %collective-permute-start.1) | collective-permute-done | bytes 12320 | tf_op jit(solution)/shard_map/ppermute | solution.py:216
  41.3 0.6 copy-done.12
  41.9 3.3 %shard_map.37 = (f32[1,1536]{1,0:T(1,128)}, f32[1,1536]{1,0:T(1,128)}, f32[128,256]{1,0:T(8,128)}) custom-call(s32[256,1]{1,0:T(8,128)} %copy.6.idc, s32[1,256]{1,0:T(1,128)} %bitcast.2, s32[48,768]{1,0:T(8,128)} %own.3, s32[4,768]{1,0:T(4,128)} %hub.1, s32[4,768]{1,0:T(4,128)} %copy-done.11, s32[4,768]{1,0:T(4,128)} %copy-done.12), custom_call_target="tpu_custom_call" | custom-call | flops 536870912 | bytes 1048576 | tf_op jit(solution)/shard_map/pallas_call | solution.py:184
  45.3 0.7 reduce.1
  46.0 0.1 reshape.23
  46.1 0.6 copy-done.4
  46.7 0.1 reshape.25
  46.8 0.0 collective-permute-done.4.rp
  46.8 0.0 collective-permute-done.5.rm
  46.8 0.0 collective-permute-done.6.r2
  46.8 0.0 collective-permute-done.9.yc
  46.8 0.7 copy-done.6
  47.5 0.1 copy-done.7
  47.6 0.1 copy-done.8
  47.7 0.7 copy-done.9
  48.5 13.6 %shard_map.38 = (f32[48,32]{1,0:T(8,128)}, f32[48,32]{1,0:T(8,128)}) custom-call(s32[256,1]{1,0:T(8,128)} %copy.6.idc, s32[1,256]{1,0:T(1,128)} %bitcast.3, s32[48,768]{1,0:T(8,128)} %own.3, s32[96,768]{1,0:T(8,128)} %copy-done, s32[96,768]{1,0:T(8,128)} %copy-done.6, s32[96,768]{1,0:T(8,128)} %copy-done.7, s32[96,768]{1,0:T(8,128)} %copy-done.8, ...), custom_call_target="tpu_custom_call" | custom-call | flops 8589934592 | bytes 1048576 | tf_op jit(solution)/shard_map/pallas_call | solution.py:184
  62.1 0.8 reshape.22
  62.9 0.1 reshape.24
  63.0 0.0 copy-done.2
  63.0 0.1 fusion
  63.0 0.1 broadcast_in_dim.18
  63.1 0.4 all_to_all.6
  63.5 33.0 %all_to_all.9 = f32[256,1,256]{2,1,0:T(1,128)S(1)} all-to-all(f32[256,1,256]{2,1,0:T(1,128)S(1)} %all_to_all.6), channel_id=1, replica_groups=mesh['y'=4,'core'=2,'zh'=4,'x'=4,'zl'=2] {'y','core','zh','x','zl'}, dimensions={0} | all-to-all | bytes 524288 | tf_op jit(solution)/shard_map/all_to_all | solution.py:243
  96.5 0.3 reduce_sum.9
  96.8 0.5 add_divide_fusion
  (20 shorter events, 0.1 us)
Async XLA Ops:
  0.0 13.2 %collective-permute-start.2 = (s32[48,768]{1,0:T(8,128)}, s32[48,768]{1,0:T(8,128)S(1)}, u32[]{:S(2)}, u32[]{:S(2)}) collective-permute-start(s32[48,768]{1,0:T(8,128)} %own.3), channel_id=1, source_target_pairs={{25,0},{8,1},{27,2},{10,3},{29,4},{12,5},{31,6},{14,7},{1,8},{16,9... | collective-permute-start | bytes 442376 | tf_op jit(solution)/shard_map/ppermute | solution.py:200
  6.4 7.4 %collective-permute-start.3 = (s32[48,768]{1,0:T(8,128)}, s32[48,768]{1,0:T(8,128)S(1)}, u32[]{:S(2)}, u32[]{:S(2)}) collective-permute-start(s32[48,768]{1,0:T(8,128)} %own.3), channel_id=1, source_target_pairs={{16,1},{18,3},{20,5},{22,7},{24,9},{26,11},{28,13},{30,15},{0,17},... | collective-permute-start | bytes 442376 | tf_op jit(solution)/shard_map/ppermute | solution.py:201
  9.9 5.6 %collective-permute-start.7 = (s32[48,768]{1,0:T(8,128)}, s32[48,768]{1,0:T(8,128)S(1)}, u32[]{:S(2)}, u32[]{:S(2)}) collective-permute-start(s32[48,768]{1,0:T(8,128)} %own.3), channel_id=1, source_target_pairs={{65,1},{67,3},{69,5},{71,7},{201,9},{203,11},{205,13},{207,15},{80... | collective-permute-start | bytes 442376 | tf_op jit(solution)/shard_map/ppermute | solution.py:207
  16.5 6.3 %collective-permute-start.8 = (s32[48,768]{1,0:T(8,128)S(1)}, s32[48,768]{1,0:T(8,128)S(1)}, u32[]{:S(2)}, u32[]{:S(2)}) collective-permute-start(s32[48,768]{1,0:T(8,128)S(1)} %get-tuple-element.17), channel_id=1, source_target_pairs={{192,0},{193,1},{194,2},{195,3},{196,4},{197,5},{198,6},{199,7},{7... | collective-permute-start | bytes 442376 | tf_op jit(solution)/shard_map/ppermute | solution.py:211
  18.5 4.3 %copy-start = (s32[96,768]{1,0:T(8,128)}, s32[96,768]{1,0:T(8,128)S(1)}, u32[]{:S(2)}) copy-start(s32[96,768]{1,0:T(8,128)S(1)} %pad_add_fusion.r0) | copy-start | bytes 884740
  18.5 28.3 %collective-permute-start.4 = (s32[96,768]{1,0:T(8,128)S(1)}, s32[96,768]{1,0:T(8,128)S(1)}, u32[]{:S(2)}, u32[]{:S(2)}) collective-permute-start(s32[96,768]{1,0:T(8,128)S(1)} %pad_add_fusion.r0), channel_id=1, source_target_pairs={{2,0},{4,2},{6,4},{0,6},{3,1},{5,3},{7,5},{1,7},{10,8},{12,10},{14... | collective-permute-start | bytes 884744 | tf_op jit(solution)/shard_map/ppermute | solution.py:205
  21.1 25.7 %collective-permute-start.5 = (s32[96,768]{1,0:T(8,128)S(1)}, s32[96,768]{1,0:T(8,128)S(1)}, u32[]{:S(2)}, u32[]{:S(2)}) collective-permute-start(s32[96,768]{1,0:T(8,128)S(1)} %pad_add_fusion.r0), channel_id=1, source_target_pairs={{6,0},{0,2},{2,4},{4,6},{7,1},{1,3},{3,5},{5,7},{14,8},{8,10},{10,... | collective-permute-start | bytes 884744 | tf_op jit(solution)/shard_map/ppermute | solution.py:205
  21.1 25.7 %collective-permute-start.6 = (s32[96,768]{1,0:T(8,128)S(1)}, s32[96,768]{1,0:T(8,128)S(1)}, u32[]{:S(2)}, u32[]{:S(2)}) collective-permute-start(s32[96,768]{1,0:T(8,128)S(1)} %pad_add_fusion.r0), channel_id=1, source_target_pairs={{4,0},{6,2},{0,4},{2,6},{5,1},{7,3},{1,5},{3,7},{12,8},{14,10},{8,... | collective-permute-start | bytes 884744 | tf_op jit(solution)/shard_map/ppermute | solution.py:205
  22.8 3.4 %copy-start.10 = (s32[4,768]{1,0:T(4,128)S(1)}, s32[4,768]{1,0:T(4,128)}, u32[]{:S(2)}) copy-start(s32[4,768]{1,0:T(4,128)} %hub.1) | copy-start | bytes 36868
  22.9 22.4 %copy-start.1 = (s32[96,768]{1,0:T(8,128)}, s32[96,768]{1,0:T(8,128)S(1)}, u32[]{:S(2)}) copy-start(s32[96,768]{1,0:T(8,128)S(1)} %pad_add_fusion.1.yy) | copy-start | bytes 884740
  22.9 23.9 %collective-permute-start.9 = (s32[96,768]{1,0:T(8,128)S(1)}, s32[96,768]{1,0:T(8,128)S(1)}, u32[]{:S(2)}, u32[]{:S(2)}) collective-permute-start(s32[96,768]{1,0:T(8,128)S(1)} %pad_add_fusion.1.yy), channel_id=1, source_target_pairs={{0,32},{32,0},{1,33},{33,1},{2,34},{34,2},{3,35},{35,3},{4,36},{36... | collective-permute-start | bytes 884744 | tf_op jit(solution)/shard_map/ppermute | solution.py:214
  26.2 10.8 %collective-permute-start = (s32[4,768]{1,0:T(4,128)S(1)}, s32[4,768]{1,0:T(4,128)S(1)}, u32[]{:S(2)}, u32[]{:S(2)}) collective-permute-start(s32[4,768]{1,0:T(4,128)S(1)} %copy-done.10), channel_id=1, source_target_pairs={{0,0},{1,1},{32,2},{33,3},{64,4},{65,5},{96,6},{97,7},{128,8},{129... | collective-permute-start | bytes 36872 | tf_op jit(solution)/shard_map/ppermute | solution.py:215
  37.0 3.2 %copy-start.11 = (s32[4,768]{1,0:T(4,128)}, s32[4,768]{1,0:T(4,128)S(1)}, u32[]{:S(2)}) copy-start(s32[4,768]{1,0:T(4,128)S(1)} %collective-permute-done.h1) | copy-start | bytes 36868
  37.0 4.3 %collective-permute-start.1 = (s32[4,768]{1,0:T(4,128)S(1)}, s32[4,768]{1,0:T(4,128)S(1)}, u32[]{:S(2)}, u32[]{:S(2)}) collective-permute-start(s32[4,768]{1,0:T(4,128)S(1)} %copy-done.10), channel_id=1, source_target_pairs={{2,0},{3,1},{34,2},{35,3},{66,4},{67,5},{98,6},{99,7},{130,8},{131... | collective-permute-start | bytes 36872 | tf_op jit(solution)/shard_map/ppermute | solution.py:216
  38.7 0.7 copy-start.5
  41.3 0.6 copy-start.12
  46.0 0.7 copy-start.4
  46.8 0.7 copy-start.6
  46.8 0.8 copy-start.7
  46.8 0.9 copy-start.8
  47.7 0.7 copy-start.9
  48.5 14.5 %copy-start.2 = (f32[128,256]{1,0:T(8,128)S(1)}, f32[128,256]{1,0:T(8,128)}, u32[]{:S(2)}) copy-start(f32[128,256]{1,0:T(8,128)} %get-tuple-element.10) | copy-start | bytes 393220
  62.0 0.8 copy-start.3

commit v2 on v1

v2 whole, which is shorter than its diff:
```python
import functools

import jax
import jax.numpy as jnp
from jax import lax
from jax.experimental import pallas as pl
from jax.experimental.pallas import tpu as pltpu
from jax.sharding import Mesh
from jax.sharding import PartitionSpec as P

AXES = ("y", "core", "zh", "x", "zl")
ROWS = ("y", "core")
COLS = ("zh", "x")
SIZES = (4, 2, 4, 4, 2)
F8 = jnp.float8_e4m3fn
F32 = jnp.float32
I32 = jnp.int32
BITS = 8
OUT = 96


def flat(y, core, zh, x, zl):
    return (((y * 2 + core) * 4 + zh) * 4 + x) * 2 + zl


def permutation(source_of):
    pairs = []
    for y in range(4):
        for core in range(2):
            for zh in range(4):
                for x in range(4):
                    for zl in range(2):
                        s = source_of(y, core, zh, x, zl)
                        if s is not None:
                            pairs.append((flat(*s), flat(y, core, zh, x, zl)))
    return pairs


def slots(zh, zl):
    return ((zh + zl) % 4, (zh + 3 + 3 * zl) % 4)


def z_near(y, core, zh, x, zl):
    return (y, core, (zh + 3) % 4, x, 1) if zl == 0 else (y, core, (zh + 1) % 4, x, 0)


def z_far(y, core, zh, x, zl):
    return None if zl == 0 else (y, core, (zh + 2) % 4, x, 0)


def y_out(y, core, zh, x, zl):
    a, b = slots(zh, zl)
    away = 1 if zl == 0 else 3
    if y == (a + away) % 4:
        return (a, core, zh, x, zl)
    if y == (b - away) % 4:
        return (b, core, zh, x, zl)
    return None


def y_swap(y, core, zh, x, zl):
    a, b = slots(zh, zl)
    away = 1 if zl == 0 else 3
    oa, ob = (a + away) % 4, (b - away) % 4
    return ({a: b, b: a, oa: ob, ob: oa}[y], core, zh, x, zl)


def unpack(words, dtype):
    n = words.shape[1]
    shifts = lax.broadcasted_iota(I32, (32, n), 0)
    rows = [
        jnp.right_shift(jnp.broadcast_to(words[i : i + 1, :], (32, n)), shifts) & 1
        for i in range(words.shape[0])
    ]
    return jnp.concatenate(rows, 0).astype(F32).astype(dtype)


def place():
    y, core = lax.axis_index("y"), lax.axis_index("core")
    zh, x, zl = lax.axis_index("zh"), lax.axis_index("x"), lax.axis_index("zl")
    return y, core, zh, x, zl


def planes(words, bits):
    return jnp.concatenate([jnp.right_shift(words, b) & 1 for b in bits], 0)


def count_kernel(idp, own, hub, r0, rp, rm, r2, yy, yc, out, keep, lhs, rhs, near, turned, res):
    y, core, zh, x, zl = place()
    row, col = 2 * y + core, 4 * zh + x
    groups = (lax.rem(zh + zl, 4), lax.rem(zh + 3 + 3 * zl, 4))
    sources = ((r0, 0), (rp, 1), (rm, 3), (r2, 2))
    ids = idp[...]
    q = (lax.broadcasted_iota(I32, (256, 16), 1) == ids // 768).astype(jnp.bfloat16)
    r = (lax.broadcasted_iota(I32, (256, 768), 1) == ids % 768).astype(jnp.bfloat16)
    outer = (((0,), (0,)), ((), ()))
    keep[...] = jnp.where(lax.dot_general(q, r, outer, preferred_element_type=F32) > 0.5, 0, -1)
    wordhot = (lax.broadcasted_iota(I32, (256, 48), 1) + 48 * row == ids // 32).astype(F32)
    bithot = (lax.broadcasted_iota(I32, (256, 32), 1) == ids % 32).astype(F32)
    light = 1.0 - lax.dot_general(
        wordhot.astype(jnp.bfloat16), bithot.astype(jnp.bfloat16), outer, preferred_element_type=F32
    )
    for n, (ref, rel) in enumerate(sources):
        xs = lax.rem(x + rel, 4)
        other = (xs // 2) != core
        for s in range(2):
            at = pl.multiple_of(48 * s + 24 * lax.rem(xs, 2), 8)
            words = jnp.where(other, yc[pl.ds(at, 24), :], yy[pl.ds(at, 24), :])
            base = (2 * n + s) * 768
            for part in range(3):
                rhs[base + 256 * part : base + 256 * part + 256, :] = unpack(
                    words[8 * part : 8 * part + 8, :], F8
                )
    keep_col = keep[pl.ds(col, 1), :]
    mine = own[...] & keep_col
    hub_col = planes(hub[...] & keep_col, range(32)).astype(F32)
    near[...] = hub_col.astype(F8)
    for side in range(2):
        xs = 2 * core + side
        words = jnp.zeros((8, 768), I32)
        for ref, rel in sources:
            for s in range(2):
                hit = (lax.rem(x + rel, 4) == xs) & (groups[s] == y)
                words = jnp.where(hit, ref[56 * s + 48 : 56 * s + 56, :], words)
        words = words & keep[pl.ds(2 * row + side, 1), :]
        turned[768 * side : 768 * side + 768, :] = jnp.concatenate([words] * 16, 0).T
    lane = lax.broadcasted_iota(I32, (48, 128), 1) // 8
    first = (zl == 0).astype(F32)
    once = (col == 0).astype(F32)
    tiles = 32 // BITS
    for t in range(tiles + 1):
        hubs = t == tiles
        size = 256 if hubs else 48 * BITS
        for n, (ref, rel) in enumerate(sources):
            xs = lax.rem(x + rel, 4)
            for s in range(2):
                lo, hi = (56 * s + 48, 56 * s + 56) if hubs else (56 * s, 56 * s + 48)
                words = ref[lo:hi, :] & keep[pl.ds(4 * groups[s] + xs, 1), :]
                bits = planes(words, range(32) if hubs else range(t * BITS, t * BITS + BITS))
                base = (2 * n + s) * 768
                lhs[t % 2, :size, base : base + 768] = bits.astype(F32).astype(F8)
        paths = jnp.dot(lhs[t % 2, :size, :], rhs[...], preferred_element_type=F32)
        if hubs:
            hub_tri = 0.5 * jnp.sum(paths * hub_col, axis=1, keepdims=True)
            hub_deg = first * jnp.sum(hub_col, axis=1, keepdims=True)
            spread = jnp.concatenate([hub_tri * bithot, hub_deg * bithot], 1)
            hub_part = lax.dot_general(
                wordhot,
                spread,
                outer,
                precision=lax.Precision.HIGHEST,
                preferred_element_type=F32,
            )
        else:
            edges = planes(mine, range(t * BITS, t * BITS + BITS)).astype(F32)
            reach = lax.dot_general(
                edges.astype(F8),
                near[...],
                (((1,), (1,)), ((), ())),
                preferred_element_type=F32,
            )
            for b in range(BITS):
                at = t * BITS + b
                rows = slice(48 * b, 48 * b + 48)
                words = turned[pl.ds(at, 48, stride=32), :]
                low = (jnp.right_shift(words, lane) & 1).astype(F32)
                high = (jnp.right_shift(words, lane + 16) & 1).astype(F32)
                closed = paths[rows, :] * edges[rows, :]
                with_hub = reach[rows, :128] * low + reach[rows, 128:] * high
                res[:, at : at + 1] = 0.5 * jnp.sum(closed, axis=1, keepdims=True) + jnp.sum(
                    with_hub, axis=1, keepdims=True
                )
                res[:, 32 + at : 33 + at] = first * jnp.sum(
                    edges[rows, :], axis=1, keepdims=True
                ) + once * jnp.sum(low + high, axis=1, keepdims=True)
    light = jnp.concatenate([light, light], 1)
    total = res[...] * light + hub_part
    out[...] = jnp.zeros_like(out)
    for c in range(16):
        for z in range(2):
            out[2 * c + z, 0:3, 0:64] = total[3 * c : 3 * c + 3, :]


def call(kernel, outs, scratch, args, flops):
    vmem = pl.BlockSpec(memory_space=pltpu.VMEM)
    return pl.pallas_call(
        kernel,
        out_shape=[jax.ShapeDtypeStruct(s, F32) for s in outs],
        in_specs=[vmem] * len(args),
        out_specs=[vmem] * len(outs),
        scratch_shapes=scratch,
        cost_estimate=pl.CostEstimate(flops=flops, bytes_accessed=1 << 20, transcendentals=0),
        compiler_params=pltpu.CompilerParams(vmem_limit_bytes=28 * 2**20),
    )(*args)


def body(light_bits, hub_bits, hub_ids):
    y, core, zh, x, zl = place()
    send = functools.partial(lax.ppermute, axis_name=AXES)
    even = zl == 0
    twin = lax.ppermute(hub_bits, "zl", [(0, 1), (1, 0)])
    hub = jnp.concatenate([jnp.where(even, hub_bits, twin), jnp.where(even, twin, hub_bits)], 0)
    block = jnp.concatenate([light_bits, hub], 0)
    near = send(block, perm=permutation(z_near))
    far = send(block, perm=permutation(z_far))
    group = jnp.concatenate([jnp.where(even, block, near), jnp.where(even, near, far)], 0)
    ring = [
        lax.ppermute(group, "x", [((d + r) % 4, d) for d in range(4)]) for r in (1, 3, 2)
    ]
    out = send(light_bits, perm=permutation(y_out))
    ga, gb = (zh + zl) % 4, (zh + 3 + 3 * zl) % 4
    root = (y == ga) | (y == gb)
    have = jnp.where(root, light_bits, out)
    got = send(have, perm=permutation(y_swap))
    first = (y == ga) | (y == (ga + 1 + 2 * zl) % 4)
    yy = jnp.concatenate([jnp.where(first, have, got), jnp.where(first, got, have)], 0)
    yc = lax.ppermute(yy, "core", [(0, 1), (1, 0)])
    planed = hub_ids.reshape(8, 32).T.reshape(256, 1)
    (table,) = call(
        count_kernel,
        [(32, 8, 128)],
        [
            pltpu.VMEM((16, 768), I32),
            pltpu.VMEM((2, 48 * BITS, 6144), F8),
            pltpu.VMEM((6144, 768), F8),
            pltpu.VMEM((256, 768), F8),
            pltpu.VMEM((1536, 128), I32),
            pltpu.VMEM((48, 64), F32),
        ],
        (planed, light_bits, hub, group, *ring, yy, yc),
        1 << 33,
    )
    everyone = lax.all_to_all(table, ("zh", "x", "zl"), 0, 0, tiled=True)
    total = jnp.sum(everyone, axis=0)
    return (total[:3, :32] / (1.0 + total[:3, 32:64])).reshape(OUT)


def solution(mesh):
    finer = Mesh(mesh.devices.reshape(SIZES), AXES)
    placed = (P(ROWS, COLS), P("zl", COLS), P())
    return jax.shard_map(
        body, mesh=finer, in_specs=placed, out_specs=P(ROWS + COLS), check_vma=False
    )
```

time: 97.8 us -> 73.5 us (0.75)
  blocking collectives: 33 us -> 16.5 us
  waiting for transfers between devices: 10.4 us -> 17 us
  local copies, waits for them, and re-layouts: 5.85 us -> 0.86 us
  starting transfers between devices: 28.3 us -> 24.1 us
  Pallas kernels: 16.9 us -> 13.2 us
  other arithmetic: 2.65 us -> 1 us
    all_to_all x1, blocking collectives: 33 us -> 16.5 us  [body(): everyone = lax.all_to_all(table, ('zh', 'x', 'zl'), 0, 0, tiled=True)]
    ppermute x3, waiting for transfers between devices: 0.01 us -> 9.44 us  [body(): lax.ppermute(group, 'x', [((d + r) % 4, d) for d in range(4)])]
    ppermute x4 -> x3, starting transfers between devices: 15.5 us -> 10 us  [the longest x1 7.47 us: body(): far = send(block, perm=permutation(z_far))]
    pallas_call x2 -> x1, Pallas kernels: 16.9 us -> 13.2 us  [call(): pl.pallas_call(kernel, out_shape=[jax.ShapeDtypeStruct(s, F32) for s in o...]
    unnamed x26 -> x4, local copies, waits for them, and re-layouts: 3.54 us -> 0.01 us
    ppermute x1, waiting for transfers between devices: 1.72 us -> 0.01 us  [body(): out = send(light_bits, perm=permutation(y_out))]
    ppermute x3, starting transfers between devices: 4.29 us -> 5.51 us  [body(): lax.ppermute(group, 'x', [((d + r) % 4, d) for d in range(4)])]
    ppermute x4 -> x3, waiting for transfers between devices: 8.71 us -> 7.57 us  [the longest x1 7.37 us: body(): near = send(block, perm=permutation(z_near))]
  transfers between devices with their start and end apart: 10 -> 9, of which waited for: 4 -> 3; matrix products, arithmetic and copies ran while one was open for 2% -> 2% of each run, Pallas kernels for 3% -> 0%
where the time goes in v2:
time: 73.5 us; the launch traced here: 72.7 us
  starting transfers between devices  24.1 us (33%)
  waiting for transfers between devices  17 us (23%)
  blocking collectives  16.5 us (22%)
  Pallas kernels  13.2 us (18%)
  other arithmetic  1 us (1%)
  local copies, waits for them, and re-layouts  0.86 us (1%)
    all_to_all x1, blocking collectives, body(): everyone = lax.all_to_all(table, ('zh', 'x', 'zl'), 0, 0, tiled=True)  16.5 us
    pallas_call x1, Pallas kernels, call(): pl.pallas_call(kernel, out_shape=[jax.ShapeDtypeStruct(s, F32) for s in o...  13.2 us
    ppermute x3, waiting for transfers between devices, body(): lax.ppermute(group, 'x', [((d + r) % 4, d) for d in range(4)])  9.44 us
    ppermute x1, starting transfers between devices, body(): far = send(block, perm=permutation(z_far))  7.47 us
    ppermute x1, waiting for transfers between devices, body(): near = send(block, perm=permutation(z_near))  7.37 us
    ppermute x3, starting transfers between devices, body(): lax.ppermute(group, 'x', [((d + r) % 4, d) for d in range(4)])  5.51 us
    ppermute x1, starting transfers between devices, body(): yc = lax.ppermute(yy, 'core', [(0, 1), (1, 0)])  3.34 us
    ppermute x1, starting transfers between devices, body(): out = send(light_bits, perm=permutation(y_out))  3.2 us
  transfers between devices with their start and end apart: 9, of which 3 were waited for; matrix products, arithmetic and copies ran while one was open for 2% of the time, Pallas kernels for 0%

profile of v2, /device:TPU:1, one launch (start us, length us, event | category | flops | bytes accessed | tf_op | source)
XLA Modules:
  0.0 72.7 jit_solution(2134976102728833587)
XLA Ops:
  0.0 0.0 copy-start
  0.0 2.5 %collective-permute-start = (s32[4,768]{1,0:T(4,128)}, s32[4,768]{1,0:T(4,128)S(1)}, u32[]{:S(2)}, u32[]{:S(2)}) collective-permute-start(s32[4,768]{1,0:T(4,128)} %param.4), channel_id=1, source_target_pairs={{0,1},{1,0},{2,3},{3,2},{4,5},{5,4},{6,7},{7,6},{8,9},{9,8},{10,11... | collective-permute-start | bytes 36872 | tf_op jit(solution)/shard_map/ppermute | solution.py:201
  2.5 3.2 %collective-permute-start.6 = (s32[48,768]{1,0:T(8,128)}, s32[48,768]{1,0:T(8,128)S(1)}, u32[]{:S(2)}, u32[]{:S(2)}) collective-permute-start(s32[48,768]{1,0:T(8,128)} %own.1), channel_id=1, source_target_pairs={{65,1},{67,3},{69,5},{71,7},{201,9},{203,11},{205,13},{207,15},{80... | collective-permute-start | bytes 442376 | tf_op jit(solution)/shard_map/ppermute | solution.py:210
  5.7 0.0 collective-permute-done
  5.7 0.7 broadcast_select_fusion.6
  6.4 0.0 copy-done
  6.5 7.5 %collective-permute-start.2 = (s32[56,768]{1,0:T(8,128)S(1)}, s32[56,768]{1,0:T(8,128)S(1)}, u32[]{:S(2)}, u32[]{:S(2)}) collective-permute-start(s32[56,768]{1,0:T(8,128)S(1)} %pad_add_fusion.2), channel_id=1, source_target_pairs={{16,1},{18,3},{20,5},{22,7},{24,9},{26,11},{28,13},{30,15},{0,17},... | collective-permute-start | bytes 516104 | tf_op jit(solution)/shard_map/ppermute | solution.py:205
  13.9 0.1 collective-permute-start.1
  14.0 0.0 collective-permute-done.6
  14.1 2.0 %collective-permute-start.7 = (s32[48,768]{1,0:T(8,128)S(1)}, s32[48,768]{1,0:T(8,128)S(1)}, u32[]{:S(2)}, u32[]{:S(2)}) collective-permute-start(s32[48,768]{1,0:T(8,128)S(1)} %broadcast_select_fusion.2), channel_id=1, source_target_pairs={{192,0},{193,1},{194,2},{195,3},{196,4},{197,5},{198,6},{199,7},{7... | collective-permute-start | bytes 442376 | tf_op jit(solution)/shard_map/ppermute | solution.py:214
  16.1 0.2 collective-permute-done.2
  16.3 7.4 %collective-permute-done.1 = s32[56,768]{1,0:T(8,128)S(1)} collective-permute-done((s32[56,768]{1,0:T(8,128)S(1)}, s32[56,768]{1,0:T(8,128)S(1)}, u32[]{:S(2)}, u32[]{:S(2)}) %collective-permute-start.1) | collective-permute-done | bytes 172064 | tf_op jit(solution)/shard_map/ppermute | solution.py:204
  23.7 2.8 %collective-permute-start.5 = (s32[112,768]{1,0:T(8,128)S(1)}, s32[112,768]{1,0:T(8,128)S(1)}, u32[]{:S(2)}, u32[]{:S(2)}) collective-permute-start(s32[112,768]{1,0:T(8,128)S(1)} %pad_add_fusion.r0), channel_id=1, source_target_pairs={{4,0},{6,2},{0,4},{2,6},{5,1},{7,3},{1,5},{3,7},{12,8},{14,10},{8,... | collective-permute-start | bytes 1032200 | tf_op jit(solution)/shard_map/ppermute | solution.py:208
  26.5 0.3 collective-permute-start.4
  26.9 2.4 %collective-permute-start.3 = (s32[112,768]{1,0:T(8,128)S(1)}, s32[112,768]{1,0:T(8,128)S(1)}, u32[]{:S(2)}, u32[]{:S(2)}) collective-permute-start(s32[112,768]{1,0:T(8,128)S(1)} %pad_add_fusion.r0), channel_id=1, source_target_pairs={{2,0},{4,2},{6,4},{0,6},{3,1},{5,3},{7,5},{1,7},{10,8},{12,10},{14... | collective-permute-start | bytes 1032200 | tf_op jit(solution)/shard_map/ppermute | solution.py:208
  29.2 0.0 collective-permute-done.7
  29.2 0.0 copy-start.1
  29.3 3.3 %collective-permute-start.8 = (s32[96,768]{1,0:T(8,128)S(1)}, s32[96,768]{1,0:T(8,128)S(1)}, u32[]{:S(2)}, u32[]{:S(2)}) collective-permute-start(s32[96,768]{1,0:T(8,128)S(1)} %pad_add_fusion.1.yy), channel_id=1, source_target_pairs={{0,32},{32,0},{1,33},{33,1},{2,34},{34,2},{3,35},{35,3},{4,36},{36... | collective-permute-start | bytes 884744 | tf_op jit(solution)/shard_map/ppermute | solution.py:217
  32.6 0.0 copy-done.1
  32.6 0.1 reshape.9
  32.7 0.1 copy.4
  32.8 0.1 reshape.12.idp
  32.9 0.0 collective-permute-done.5.r2
  32.9 9.4 %collective-permute-done.4.rm = s32[112,768]{1,0:T(8,128)S(1)} collective-permute-done((s32[112,768]{1,0:T(8,128)S(1)}, s32[112,768]{1,0:T(8,128)S(1)}, u32[]{:S(2)}, u32[]{:S(2)}) %collective-permute-start.4) | collective-permute-done | bytes 344096 | tf_op jit(solution)/shard_map/ppermute | solution.py:208
  42.4 0.0 collective-permute-done.3.rp
  42.4 0.0 collective-permute-done.8.yc
  42.4 13.2 %shard_map.37 = f32[32,8,128]{2,1,0:T(8,128)S(1)} custom-call(s32[256,1]{1,0:T(8,128)S(1)} %reshape.12.idp, s32[48,768]{1,0:T(8,128)S(1)} %copy-done, s32[8,768]{1,0:T(8,128)S(1)} %pad_add_fusion.3.hub, s32[112,768]{1,0:T(8,128)S(1)} %pad_add_fusion.r0, s32[112,768]{1,0:T(8,128)S(1)} %collective-permute-done.3.rp, s32[112,768]{1,0:T(8,128)S(1)} %collective-permute-done.4.rm, ...), custom_call_target="tpu_custom_call" | custom-call | flops 8589934592 | bytes 1048576 | tf_op jit(solution)/shard_map/pallas_call | solution.py:186
  55.5 16.5 %all_to_all.5 = f32[32,8,128]{2,1,0:T(8,128)S(1)} all-to-all(f32[32,8,128]{2,1,0:T(8,128)S(1)} %shard_map.37), channel_id=1, replica_groups=mesh['y'=4,'core'=2,'zh'=4,'x'=4,'zl'=2] {'zh','x','zl'}, dimensions={0} | all-to-all | bytes 262144 | tf_op jit(solution)/shard_map/all_to_all | solution.py:233
  72.0 0.1 add_divide_fusion
  72.1 0.6 reshape.11
  (8 shorter events, 0.2 us)
Async XLA Ops:
  0.0 6.4 %copy-start = (s32[48,768]{1,0:T(8,128)S(1)}, s32[48,768]{1,0:T(8,128)}, u32[]{:S(2)}) copy-start(s32[48,768]{1,0:T(8,128)} %own.1) | copy-start | bytes 442372
  0.0 5.7 %collective-permute-start = (s32[4,768]{1,0:T(4,128)}, s32[4,768]{1,0:T(4,128)S(1)}, u32[]{:S(2)}, u32[]{:S(2)}) collective-permute-start(s32[4,768]{1,0:T(4,128)} %param.4), channel_id=1, source_target_pairs={{0,1},{1,0},{2,3},{3,2},{4,5},{5,4},{6,7},{7,6},{8,9},{9,8},{10,11... | collective-permute-start | bytes 36872 | tf_op jit(solution)/shard_map/ppermute | solution.py:201
  2.5 11.6 %collective-permute-start.6 = (s32[48,768]{1,0:T(8,128)}, s32[48,768]{1,0:T(8,128)S(1)}, u32[]{:S(2)}, u32[]{:S(2)}) collective-permute-start(s32[48,768]{1,0:T(8,128)} %own.1), channel_id=1, source_target_pairs={{65,1},{67,3},{69,5},{71,7},{201,9},{203,11},{205,13},{207,15},{80... | collective-permute-start | bytes 442376 | tf_op jit(solution)/shard_map/ppermute | solution.py:210
  6.5 9.8 %collective-permute-start.2 = (s32[56,768]{1,0:T(8,128)S(1)}, s32[56,768]{1,0:T(8,128)S(1)}, u32[]{:S(2)}, u32[]{:S(2)}) collective-permute-start(s32[56,768]{1,0:T(8,128)S(1)} %pad_add_fusion.2), channel_id=1, source_target_pairs={{16,1},{18,3},{20,5},{22,7},{24,9},{26,11},{28,13},{30,15},{0,17},... | collective-permute-start | bytes 516104 | tf_op jit(solution)/shard_map/ppermute | solution.py:205
  13.9 9.7 %collective-permute-start.1 = (s32[56,768]{1,0:T(8,128)S(1)}, s32[56,768]{1,0:T(8,128)S(1)}, u32[]{:S(2)}, u32[]{:S(2)}) collective-permute-start(s32[56,768]{1,0:T(8,128)S(1)} %pad_add_fusion.2), channel_id=1, source_target_pairs={{25,0},{8,1},{27,2},{10,3},{29,4},{12,5},{31,6},{14,7},{1,8},{16,9... | collective-permute-start | bytes 516104 | tf_op jit(solution)/shard_map/ppermute | solution.py:204
  14.1 15.1 %collective-permute-start.7 = (s32[48,768]{1,0:T(8,128)S(1)}, s32[48,768]{1,0:T(8,128)S(1)}, u32[]{:S(2)}, u32[]{:S(2)}) collective-permute-start(s32[48,768]{1,0:T(8,128)S(1)} %broadcast_select_fusion.2), channel_id=1, source_target_pairs={{192,0},{193,1},{194,2},{195,3},{196,4},{197,5},{198,6},{199,7},{7... | collective-permute-start | bytes 442376 | tf_op jit(solution)/shard_map/ppermute | solution.py:214
  23.7 9.2 %collective-permute-start.5 = (s32[112,768]{1,0:T(8,128)S(1)}, s32[112,768]{1,0:T(8,128)S(1)}, u32[]{:S(2)}, u32[]{:S(2)}) collective-permute-start(s32[112,768]{1,0:T(8,128)S(1)} %pad_add_fusion.r0), channel_id=1, source_target_pairs={{4,0},{6,2},{0,4},{2,6},{5,1},{7,3},{1,5},{3,7},{12,8},{14,10},{8,... | collective-permute-start | bytes 1032200 | tf_op jit(solution)/shard_map/ppermute | solution.py:208
  26.5 15.8 %collective-permute-start.4 = (s32[112,768]{1,0:T(8,128)S(1)}, s32[112,768]{1,0:T(8,128)S(1)}, u32[]{:S(2)}, u32[]{:S(2)}) collective-permute-start(s32[112,768]{1,0:T(8,128)S(1)} %pad_add_fusion.r0), channel_id=1, source_target_pairs={{6,0},{0,2},{2,4},{4,6},{7,1},{1,3},{3,5},{5,7},{14,8},{8,10},{10,... | collective-permute-start | bytes 1032200 | tf_op jit(solution)/shard_map/ppermute | solution.py:208
  26.9 15.5 %collective-permute-start.3 = (s32[112,768]{1,0:T(8,128)S(1)}, s32[112,768]{1,0:T(8,128)S(1)}, u32[]{:S(2)}, u32[]{:S(2)}) collective-permute-start(s32[112,768]{1,0:T(8,128)S(1)} %pad_add_fusion.r0), channel_id=1, source_target_pairs={{2,0},{4,2},{6,4},{0,6},{3,1},{5,3},{7,5},{1,7},{10,8},{12,10},{14... | collective-permute-start | bytes 1032200 | tf_op jit(solution)/shard_map/ppermute | solution.py:208
  29.2 3.4 %copy-start.1 = (s32[256]{0:T(256)S(1)}, s32[256]{0:T(256)}, u32[]{:S(2)}) copy-start(s32[256]{0:T(256)} %param.5) | copy-start | bytes 3076
  29.3 13.1 %collective-permute-start.8 = (s32[96,768]{1,0:T(8,128)S(1)}, s32[96,768]{1,0:T(8,128)S(1)}, u32[]{:S(2)}, u32[]{:S(2)}) collective-permute-start(s32[96,768]{1,0:T(8,128)S(1)} %pad_add_fusion.1.yy), channel_id=1, source_target_pairs={{0,32},{32,0},{1,33},{33,1},{2,34},{34,2},{3,35},{35,3},{4,36},{36... | collective-permute-start | bytes 884744 | tf_op jit(solution)/shard_map/ppermute | solution.py:217

commit v3 on v2

v3 whole, which is shorter than its diff:
```python
import functools

import jax
import jax.numpy as jnp
from jax import lax
from jax.experimental import pallas as pl
from jax.experimental.pallas import tpu as pltpu
from jax.sharding import Mesh
from jax.sharding import PartitionSpec as P

AXES = ("y", "core", "zh", "x", "zl")
ROWS = ("y", "core")
COLS = ("zh", "x")
SIZES = (4, 2, 4, 4, 2)
F8 = jnp.float8_e4m3fn
F32 = jnp.float32
I32 = jnp.int32
BITS = 8
OUT = 96


def flat(y, core, zh, x, zl):
    return (((y * 2 + core) * 4 + zh) * 4 + x) * 2 + zl


def permutation(source_of):
    pairs = []
    for y in range(4):
        for core in range(2):
            for zh in range(4):
                for x in range(4):
                    for zl in range(2):
                        s = source_of(y, core, zh, x, zl)
                        if s is not None:
                            pairs.append((flat(*s), flat(y, core, zh, x, zl)))
    return pairs


def group_of(y, zh, zl):
    return y ^ (2 * (zh & 1) + zl)


def fetch(y, core, zh, x, zl):
    group = group_of(y, zh, zl)
    turn = y >> 1 if y in (0, 2) else int(group in (0, 3))
    return (y, core, group, x, turn ^ (zh >> 1))


def partner(y, core, zh, x, zl):
    return (y, core, zh ^ 1, x, zl)


def along_y(y, core, zh, x, zl):
    return (group_of(y, zh, zl), core, zh, x, zl)


def unpack(words, dtype):
    n = words.shape[1]
    shifts = lax.broadcasted_iota(I32, (32, n), 0)
    rows = [
        jnp.right_shift(jnp.broadcast_to(words[i : i + 1, :], (32, n)), shifts) & 1
        for i in range(words.shape[0])
    ]
    return jnp.concatenate(rows, 0).astype(F32).astype(dtype)


def place():
    y, core = lax.axis_index("y"), lax.axis_index("core")
    zh, x, zl = lax.axis_index("zh"), lax.axis_index("x"), lax.axis_index("zl")
    return y, core, zh, x, zl


def planes(words, bits):
    return jnp.concatenate([jnp.right_shift(words, b) & 1 for b in bits], 0)


def count_kernel(idp, pair, hubs, r0, rp, rm, r2, yy, yc, out, keep, lhs, rhs, near, turned, res):
    y, core, zh, x, zl = place()
    row = 2 * y + core
    part_of = 2 * lax.rem(zh, 2) + zl
    group = y ^ part_of
    sources = ((r0, 0), (rp, 1), (rm, 3), (r2, 2))
    ids = idp[...]
    q = (lax.broadcasted_iota(I32, (256, 16), 1) == ids // 768).astype(jnp.bfloat16)
    r = (lax.broadcasted_iota(I32, (256, 768), 1) == ids % 768).astype(jnp.bfloat16)
    outer = (((0,), (0,)), ((), ()))
    keep[...] = jnp.where(lax.dot_general(q, r, outer, preferred_element_type=F32) > 0.5, 0, -1)
    wordhot = (lax.broadcasted_iota(I32, (256, 48), 1) + 48 * row == ids // 32).astype(F32)
    bithot = (lax.broadcasted_iota(I32, (256, 32), 1) == ids % 32).astype(F32)
    light = 1.0 - lax.dot_general(
        wordhot.astype(jnp.bfloat16), bithot.astype(jnp.bfloat16), outer, preferred_element_type=F32
    )
    for n, (ref, rel) in enumerate(sources):
        xs = lax.rem(x + rel, 4)
        other = (xs // 2) != core
        for side in range(2):
            at = pl.multiple_of(48 * side + 24 * lax.rem(xs, 2), 8)
            words = jnp.where(other, yc[pl.ds(at, 24), :], yy[pl.ds(at, 24), :])
            for part in range(3):
                base = 768 * n + 256 * part
                rhs[base : base + 256, 768 * side : 768 * side + 768] = unpack(
                    words[8 * part : 8 * part + 8, :], F8
                )
    left = pl.ds(8 * (zh // 2) + x, 1)
    right = pl.ds(8 * (zh // 2) + 4 + x, 1)
    mine = jnp.concatenate(
        [pair[0:48, :] & keep[left, :], pair[48:96, :] & keep[right, :]], 1
    )
    hub_words = jnp.concatenate(
        [hubs[0:8, :] & keep[left, :], hubs[8:16, :] & keep[right, :]], 1
    )
    hub_col = planes(hub_words, range(32)).astype(F32)
    near[...] = hub_col.astype(F8)
    for side in range(2):
        xs = 2 * core + side
        words = jnp.zeros((8, 768), I32)
        for ref, rel in sources:
            hit = (lax.rem(x + rel, 4) == xs) & (group == y)
            words = jnp.where(hit, ref[48:56, :], words)
        words = words & keep[pl.ds(2 * row + side, 1), :]
        turned[768 * side : 768 * side + 768, :] = jnp.concatenate([words] * 16, 0).T
    lane = lax.broadcasted_iota(I32, (48, 128), 1) // 8
    first = (part_of == 0).astype(F32)
    once = ((x == 0) & (zh < 2)).astype(F32)
    tiles = 32 // BITS
    for t in range(tiles + 1):
        extra = t == tiles
        size = 256 if extra else 48 * BITS
        for n, (ref, rel) in enumerate(sources):
            lo, hi = (48, 56) if extra else (0, 48)
            words = ref[lo:hi, :] & keep[pl.ds(4 * group + lax.rem(x + rel, 4), 1), :]
            bits = planes(words, range(32) if extra else range(t * BITS, t * BITS + BITS))
            lhs[t % 2, :size, 768 * n : 768 * n + 768] = bits.astype(F32).astype(F8)
        paths = jnp.dot(lhs[t % 2, :size, :], rhs[...], preferred_element_type=F32)
        if extra:
            hub_tri = 0.5 * jnp.sum(paths * hub_col, axis=1, keepdims=True)
            hub_deg = first * jnp.sum(hub_col, axis=1, keepdims=True)
            spread = jnp.concatenate([hub_tri * bithot, hub_deg * bithot], 1)
            hub_part = lax.dot_general(
                wordhot,
                spread,
                outer,
                precision=lax.Precision.HIGHEST,
                preferred_element_type=F32,
            )
        else:
            edges = planes(mine, range(t * BITS, t * BITS + BITS)).astype(F32)
            reach = lax.dot_general(
                edges.astype(F8),
                near[...],
                (((1,), (1,)), ((), ())),
                preferred_element_type=F32,
            )
            for b in range(BITS):
                at = t * BITS + b
                rows = slice(48 * b, 48 * b + 48)
                words = turned[pl.ds(at, 48, stride=32), :]
                low = (jnp.right_shift(words, lane) & 1).astype(F32)
                high = (jnp.right_shift(words, lane + 16) & 1).astype(F32)
                closed = paths[rows, :] * edges[rows, :]
                with_hub = reach[rows, :128] * low + reach[rows, 128:] * high
                res[:, at : at + 1] = 0.5 * jnp.sum(closed, axis=1, keepdims=True) + jnp.sum(
                    with_hub, axis=1, keepdims=True
                )
                res[:, 32 + at : 33 + at] = first * jnp.sum(
                    edges[rows, :], axis=1, keepdims=True
                ) + once * jnp.sum(low + high, axis=1, keepdims=True)
    light = jnp.concatenate([light, light], 1)
    total = res[...] * light + hub_part
    for c in range(16):
        line = jnp.concatenate(
            [total[3 * c + k : 3 * c + k + 1, 0:32] for k in range(3)]
            + [jnp.zeros((1, 32), F32)]
            + [total[3 * c + k : 3 * c + k + 1, 32:64] for k in range(3)]
            + [jnp.zeros((1, 32), F32)],
            1,
        )
        out[2 * c : 2 * c + 1, :] = line
        out[2 * c + 1 : 2 * c + 2, :] = line


def call(kernel, outs, scratch, args, flops):
    vmem = pl.BlockSpec(memory_space=pltpu.VMEM)
    return pl.pallas_call(
        kernel,
        out_shape=[jax.ShapeDtypeStruct(s, F32) for s in outs],
        in_specs=[vmem] * len(args),
        out_specs=[vmem] * len(outs),
        scratch_shapes=scratch,
        cost_estimate=pl.CostEstimate(flops=flops, bytes_accessed=1 << 20, transcendentals=0),
        compiler_params=pltpu.CompilerParams(vmem_limit_bytes=28 * 2**20),
    )(*args)


def clustering(light_bits, hub_bits, hub_ids):
    _, _, zh, _, zl = place()
    send = functools.partial(lax.ppermute, axis_name=AXES)
    even = zl == 0
    twin = lax.ppermute(hub_bits, "zl", [(0, 1), (1, 0)])
    block = jnp.concatenate(
        [light_bits, jnp.where(even, hub_bits, twin), jnp.where(even, twin, hub_bits)], 0
    )
    rows = send(block, perm=permutation(fetch))
    beside = send(block, perm=permutation(partner))
    ring = []
    for r in (1, 3, 2):
        ring.append(lax.ppermute(rows, "x", [((d + r) % 4, d) for d in range(4)]))
    lead = zh % 2 == 0
    left = jnp.where(lead, block, beside)
    right = jnp.where(lead, beside, block)
    pair = jnp.concatenate([left[:48], right[:48]], 0)
    hubs = jnp.concatenate([left[48:], right[48:]], 0)
    yy = send(pair, perm=permutation(along_y))
    yc = lax.ppermute(yy, "core", [(0, 1), (1, 0)])
    planed = hub_ids.reshape(8, 32).T.reshape(256, 1)
    (table,) = call(
        count_kernel,
        [(32, 256)],
        [
            pltpu.VMEM((16, 768), I32),
            pltpu.VMEM((2, 48 * BITS, 3072), F8),
            pltpu.VMEM((3072, 1536), F8),
            pltpu.VMEM((256, 1536), F8),
            pltpu.VMEM((1536, 128), I32),
            pltpu.VMEM((48, 64), F32),
        ],
        (planed, pair, hubs, rows, *ring, yy, yc),
        1 << 33,
    )
    everyone = lax.all_to_all(table, ("zh", "x", "zl"), 0, 0, tiled=True)
    total = jnp.sum(everyone, axis=0)
    return total[:OUT] / (1.0 + total[128 : 128 + OUT])


def solution(mesh):
    finer = Mesh(mesh.devices.reshape(SIZES), AXES)
    placed = (P(ROWS, COLS), P("zl", COLS), P())
    return jax.shard_map(
        clustering, mesh=finer, in_specs=placed, out_specs=P(ROWS + COLS), check_vma=False
    )
```

time: 73.5 us -> 75.4 us (1.026)
  blocking collectives: 16.5 us -> 29.7 us
  starting transfers between devices: 24.1 us -> 14.1 us
  waiting for transfers between devices: 17 us -> 14.4 us
  other arithmetic: 1 us -> 2.35 us
    all_to_all x1, blocking collectives: 16.5 us -> 29.7 us  [clustering(): everyone = lax.all_to_all(table, ('zh', 'x', 'zl'), 0, 0, tiled=True)]
    ppermute x9 -> x8, starting transfers between devices: 24.1 us -> 14.1 us  [the longest x3 5.42 us: clustering(): ring.append(lax.ppermute(rows, 'x', [((d + r) % 4, d) for d in range(4)]))]
    ppermute x9 -> x8, waiting for transfers between devices: 17 us -> 14.4 us  [the longest x1 7.28 us: clustering(): beside = send(block, perm=permutation(partner))]
    concatenate x4 -> x3, other arithmetic: 0.07 us -> 1.03 us  [the longest x1 1 us: clustering(): jnp.concatenate([light_bits, jnp.where(even, hub_bits, twin), jnp.where(e...]
  transfers between devices with their start and end apart: 9 -> 8, of which waited for: 3 -> 4; matrix products, arithmetic and copies ran while one was open for 2% -> 0% of each run, Pallas kernels for 0% -> 0%
where the time goes in v3:
time: 75.4 us; the launch traced here: 74.8 us
  blocking collectives  29.7 us (39%)
  waiting for transfers between devices  14.4 us (19%)
  starting transfers between devices  14.1 us (19%)
  Pallas kernels  13.8 us (18%)
  other arithmetic  2.35 us (3%)
    all_to_all x1, blocking collectives, clustering(): everyone = lax.all_to_all(table, ('zh', 'x', 'zl'), 0, 0, tiled=True)  29.7 us
    pallas_call x1, Pallas kernels, call(): pl.pallas_call(kernel, out_shape=[jax.ShapeDtypeStruct(s, F32) for s in o...  13.8 us
    ppermute x1, waiting for transfers between devices, clustering(): beside = send(block, perm=permutation(partner))  7.28 us
    ppermute x3, waiting for transfers between devices, clustering(): ring.append(lax.ppermute(rows, 'x', [((d + r) % 4, d) for d in range(4)]))  5.77 us
    ppermute x3, starting transfers between devices, clustering(): ring.append(lax.ppermute(rows, 'x', [((d + r) % 4, d) for d in range(4)]))  5.42 us
    ppermute x1, starting transfers between devices, clustering(): beside = send(block, perm=permutation(partner))  3.08 us
    ppermute x1, starting transfers between devices, clustering(): twin = lax.ppermute(hub_bits, 'zl', [(0, 1), (1, 0)])  2.46 us
    ppermute x1, starting transfers between devices, clustering(): yc = lax.ppermute(yy, 'core', [(0, 1), (1, 0)])  1.83 us
  transfers between devices with their start and end apart: 8, of which 4 were waited for; matrix products, arithmetic and copies ran while one was open for 0% of the time, Pallas kernels for 0%

profile of v3, /device:TPU:1, one launch (start us, length us, event | category | flops | bytes accessed | tf_op | source)
XLA Modules:
  0.0 74.8 jit_solution(2317909695821871731)
XLA Ops:
  0.0 2.5 %collective-permute-start = (s32[4,768]{1,0:T(4,128)}, s32[4,768]{1,0:T(4,128)S(1)}, u32[]{:S(2)}, u32[]{:S(2)}) collective-permute-start(s32[4,768]{1,0:T(4,128)} %param.4), channel_id=1, source_target_pairs={{0,1},{1,0},{2,3},{3,2},{4,5},{5,4},{6,7},{7,6},{8,9},{9,8},{10,11... | collective-permute-start | bytes 36872 | tf_op jit(solution)/shard_map/ppermute | solution.py:199
  2.5 1.3 %collective-permute-done = s32[4,768]{1,0:T(4,128)S(1)} collective-permute-done((s32[4,768]{1,0:T(4,128)}, s32[4,768]{1,0:T(4,128)S(1)}, u32[]{:S(2)}, u32[]{:S(2)}) %collective-permute-start) | collective-permute-done | bytes 12320 | tf_op jit(solution)/shard_map/ppermute | solution.py:199
  3.7 0.7 broadcast_select_fusion.3
  4.5 0.0 copy-start
  4.5 1.0 %pad_add_fusion.1 = s32[56,768]{1,0:T(8,128)S(1)} fusion(s32[4,768]{1,0:T(4,128)S(1)} %get-tuple-element.8, s32[4,768]{1,0:T(4,128)S(1)} %get-tuple-element.7, s32[48,768]{1,0:T(8,128)} %param.3), kind=kLoop, calls=%fused_computation.1 | loop fusion | flops 86016 | bytes 344064 | tf_op jit(solution)/shard_map/concatenate | solution.py:200
  5.5 3.1 %collective-permute-start.1 = (s32[56,768]{1,0:T(8,128)S(1)}, s32[56,768]{1,0:T(8,128)S(1)}, u32[]{:S(2)}, u32[]{:S(2)}) collective-permute-start(s32[56,768]{1,0:T(8,128)S(1)} %pad_add_fusion.1), channel_id=1, source_target_pairs={{8,0},{9,1},{10,2},{11,3},{12,4},{13,5},{14,6},{15,7},{0,8},{1,9},... | collective-permute-start | bytes 516104 | tf_op jit(solution)/shard_map/ppermute | solution.py:204
  8.5 7.3 %collective-permute-done.1 = s32[56,768]{1,0:T(8,128)S(1)} collective-permute-done((s32[56,768]{1,0:T(8,128)S(1)}, s32[56,768]{1,0:T(8,128)S(1)}, u32[]{:S(2)}, u32[]{:S(2)}) %collective-permute-start.1) | collective-permute-done | bytes 172064 | tf_op jit(solution)/shard_map/ppermute | solution.py:204
  15.8 0.0 copy-done
  15.9 0.0 copy-start.1
  15.9 0.7 collective-permute-start.6
  16.6 0.7 collective-permute-start.2
  17.3 0.0 collective-permute-done.6.yy
  17.3 1.8 %collective-permute-start.7 = (s32[96,768]{1,0:T(8,128)S(1)}, s32[96,768]{1,0:T(8,128)S(1)}, u32[]{:S(2)}, u32[]{:S(2)}) collective-permute-start(s32[96,768]{1,0:T(8,128)S(1)} %collective-permute-done.6.yy), channel_id=1, source_target_pairs={{0,32},{32,0},{1,33},{33,1},{2,34},{34,2},{3,35},{35,3},{4,36},{36... | collective-permute-start | bytes 884744 | tf_op jit(solution)/shard_map/ppermute | solution.py:214
  19.1 0.0 collective-permute-done.2.r0
  19.1 2.7 %collective-permute-start.5 = (s32[56,768]{1,0:T(8,128)S(1)}, s32[56,768]{1,0:T(8,128)S(1)}, u32[]{:S(2)}, u32[]{:S(2)}) collective-permute-start(s32[56,768]{1,0:T(8,128)S(1)} %collective-permute-done.2.r0), channel_id=1, source_target_pairs={{4,0},{6,2},{0,4},{2,6},{5,1},{7,3},{1,5},{3,7},{12,8},{14,10},{8,... | collective-permute-start | bytes 516104 | tf_op jit(solution)/shard_map/ppermute | solution.py:207
  21.9 0.3 collective-permute-start.4
  22.2 2.4 %collective-permute-start.3 = (s32[56,768]{1,0:T(8,128)S(1)}, s32[56,768]{1,0:T(8,128)S(1)}, u32[]{:S(2)}, u32[]{:S(2)}) collective-permute-start(s32[56,768]{1,0:T(8,128)S(1)} %collective-permute-done.2.r0), channel_id=1, source_target_pairs={{2,0},{4,2},{6,4},{0,6},{3,1},{5,3},{7,5},{1,7},{10,8},{12,10},{14... | collective-permute-start | bytes 516104 | tf_op jit(solution)/shard_map/ppermute | solution.py:207
  24.6 0.0 copy-done.1
  24.6 0.1 reshape.8
  24.6 0.1 copy.6
  24.7 0.1 reshape.10.idp
  24.9 1.6 %collective-permute-done.5.r2 = s32[56,768]{1,0:T(8,128)S(1)} collective-permute-done((s32[56,768]{1,0:T(8,128)S(1)}, s32[56,768]{1,0:T(8,128)S(1)}, u32[]{:S(2)}, u32[]{:S(2)}) %collective-permute-start.5) | collective-permute-done | bytes 172064 | tf_op jit(solution)/shard_map/ppermute | solution.py:207
  26.5 4.2 %collective-permute-done.4.rm = s32[56,768]{1,0:T(8,128)S(1)} collective-permute-done((s32[56,768]{1,0:T(8,128)S(1)}, s32[56,768]{1,0:T(8,128)S(1)}, u32[]{:S(2)}, u32[]{:S(2)}) %collective-permute-start.4) | collective-permute-done | bytes 172064 | tf_op jit(solution)/shard_map/ppermute | solution.py:207
  30.6 0.0 collective-permute-done.3.rp
  30.6 0.0 collective-permute-done.7.yc
  30.6 13.8 %shard_map.37 = f32[32,256]{1,0:T(8,128)S(1)} custom-call(s32[256,1]{1,0:T(8,128)S(1)} %reshape.10.idp, s32[96,768]{1,0:T(8,128)S(1)} %pad_add_fusion.pair, s32[16,768]{1,0:T(8,128)S(1)} %pad_add_fusion.2.hubs, s32[56,768]{1,0:T(8,128)S(1)} %collective-permute-done.2.r0, s32[56,768]{1,0:T(8,128)S(1)} %collective-permute-done.3.rp, ...), custom_call_target="tpu_custom_call" | custom-call | flops 8589934592 | bytes 1048576 | tf_op jit(solution)/shard_map/pallas_call | solution.py:184
  44.5 29.7 %all_to_all.9 = f32[32,1,256]{2,1,0:T(1,128)S(1)} all-to-all(f32[32,1,256]{2,1,0:T(1,128)S(1)} %copy.8), channel_id=1, replica_groups=mesh['y'=4,'core'=2,'zh'=4,'x'=4,'zl'=2] {'zh','x','zl'}, dimensions={0} | all-to-all | bytes 65536 | tf_op jit(solution)/shard_map/all_to_all | solution.py:230
  74.2 0.1 reduce_sum.9
  74.2 0.5 add_divide_fusion
  (8 shorter events, 0.1 us)
Async XLA Ops:
  0.0 3.7 %collective-permute-start = (s32[4,768]{1,0:T(4,128)}, s32[4,768]{1,0:T(4,128)S(1)}, u32[]{:S(2)}, u32[]{:S(2)}) collective-permute-start(s32[4,768]{1,0:T(4,128)} %param.4), channel_id=1, source_target_pairs={{0,1},{1,0},{2,3},{3,2},{4,5},{5,4},{6,7},{7,6},{8,9},{9,8},{10,11... | collective-permute-start | bytes 36872 | tf_op jit(solution)/shard_map/ppermute | solution.py:199
  4.5 11.4 %copy-start = (s32[48,768]{1,0:T(8,128)S(1)}, s32[48,768]{1,0:T(8,128)}, u32[]{:S(2)}) copy-start(s32[48,768]{1,0:T(8,128)} %param.3) | copy-start | bytes 442372
  5.5 10.4 %collective-permute-start.1 = (s32[56,768]{1,0:T(8,128)S(1)}, s32[56,768]{1,0:T(8,128)S(1)}, u32[]{:S(2)}, u32[]{:S(2)}) collective-permute-start(s32[56,768]{1,0:T(8,128)S(1)} %pad_add_fusion.1), channel_id=1, source_target_pairs={{8,0},{9,1},{10,2},{11,3},{12,4},{13,5},{14,6},{15,7},{0,8},{1,9},... | collective-permute-start | bytes 516104 | tf_op jit(solution)/shard_map/ppermute | solution.py:204
  15.9 8.7 %copy-start.1 = (s32[256]{0:T(256)S(1)}, s32[256]{0:T(256)}, u32[]{:S(2)}) copy-start(s32[256]{0:T(256)} %param.5) | copy-start | bytes 3076
  15.9 1.4 %collective-permute-start.6 = (s32[96,768]{1,0:T(8,128)S(1)}, s32[96,768]{1,0:T(8,128)S(1)}, u32[]{:S(2)}, u32[]{:S(2)}) collective-permute-start(s32[96,768]{1,0:T(8,128)S(1)} %pad_add_fusion.pair), channel_id=1, source_target_pairs={{0,0},{65,1},{2,2},{67,3},{4,4},{69,5},{6,6},{71,7},{136,8},{201,9... | collective-permute-start | bytes 884744 | tf_op jit(solution)/shard_map/ppermute | solution.py:213
  16.6 2.5 %collective-permute-start.2 = (s32[56,768]{1,0:T(8,128)S(1)}, s32[56,768]{1,0:T(8,128)S(1)}, u32[]{:S(2)}, u32[]{:S(2)}) collective-permute-start(s32[56,768]{1,0:T(8,128)S(1)} %pad_add_fusion.1), channel_id=1, source_target_pairs={{0,0},{8,1},{2,2},{10,3},{4,4},{12,5},{6,6},{14,7},{16,8},{24,9},{... | collective-permute-start | bytes 516104 | tf_op jit(solution)/shard_map/ppermute | solution.py:203
  17.3 13.3 %collective-permute-start.7 = (s32[96,768]{1,0:T(8,128)S(1)}, s32[96,768]{1,0:T(8,128)S(1)}, u32[]{:S(2)}, u32[]{:S(2)}) collective-permute-start(s32[96,768]{1,0:T(8,128)S(1)} %collective-permute-done.6.yy), channel_id=1, source_target_pairs={{0,32},{32,0},{1,33},{33,1},{2,34},{34,2},{3,35},{35,3},{4,36},{36... | collective-permute-start | bytes 884744 | tf_op jit(solution)/shard_map/ppermute | solution.py:214
  19.1 7.3 %collective-permute-start.5 = (s32[56,768]{1,0:T(8,128)S(1)}, s32[56,768]{1,0:T(8,128)S(1)}, u32[]{:S(2)}, u32[]{:S(2)}) collective-permute-start(s32[56,768]{1,0:T(8,128)S(1)} %collective-permute-done.2.r0), channel_id=1, source_target_pairs={{4,0},{6,2},{0,4},{2,6},{5,1},{7,3},{1,5},{3,7},{12,8},{14,10},{8,... | collective-permute-start | bytes 516104 | tf_op jit(solution)/shard_map/ppermute | solution.py:207
  21.9 8.7 %collective-permute-start.4 = (s32[56,768]{1,0:T(8,128)S(1)}, s32[56,768]{1,0:T(8,128)S(1)}, u32[]{:S(2)}, u32[]{:S(2)}) collective-permute-start(s32[56,768]{1,0:T(8,128)S(1)} %collective-permute-done.2.r0), channel_id=1, source_target_pairs={{6,0},{0,2},{2,4},{4,6},{7,1},{1,3},{3,5},{5,7},{14,8},{8,10},{10,... | collective-permute-start | bytes 516104 | tf_op jit(solution)/shard_map/ppermute | solution.py:207
  22.2 8.4 %collective-permute-start.3 = (s32[56,768]{1,0:T(8,128)S(1)}, s32[56,768]{1,0:T(8,128)S(1)}, u32[]{:S(2)}, u32[]{:S(2)}) collective-permute-start(s32[56,768]{1,0:T(8,128)S(1)} %collective-permute-done.2.r0), channel_id=1, source_target_pairs={{2,0},{4,2},{6,4},{0,6},{3,1},{5,3},{7,5},{1,7},{10,8},{12,10},{14... | collective-permute-start | bytes 516104 | tf_op jit(solution)/shard_map/ppermute | solution.py:207

commit v4 on v3

v4 whole, which is shorter than its diff:
```python
import jax
import jax.numpy as jnp
from jax import lax
from jax.experimental import pallas as pl
from jax.experimental.pallas import tpu as pltpu
from jax.sharding import Mesh
from jax.sharding import PartitionSpec as P

AXES = ("y", "core", "zh", "x", "zl")
ROWS = ("y", "core")
COLS = ("zh", "x")
SIZES = (4, 2, 4, 4, 2)
F8 = jnp.float8_e4m3fn
F32 = jnp.float32
I32 = jnp.int32
OUT = 96


def flat(y, core, zh, x, zl):
    return (((y * 2 + core) * 4 + zh) * 4 + x) * 2 + zl


def permutation(source_of):
    pairs = []
    for y in range(4):
        for core in range(2):
            for zh in range(4):
                for x in range(4):
                    for zl in range(2):
                        s = source_of(y, core, zh, x, zl)
                        if s is not None:
                            pairs.append((flat(*s), flat(y, core, zh, x, zl)))
    return pairs


FETCH = ((0, 1, 0, 1), (1, 0, 0, 1), (1, 0, 1, 0), (1, 0, 0, 1))


def group_of(y, z):
    return (-(y + z)) & 3


def fetch(y, core, zh, x, zl):
    z = 2 * zh + zl
    group = group_of(y, z)
    return (y, core, group, x, FETCH[(-y) & 3][group] ^ (z >> 2))


def partner(y, core, zh, x, zl):
    return (y, core, (zh + 1) % 4, x, 0) if zl == 1 else (y, core, (zh + 3) % 4, x, 1)


def along_y(y, core, zh, x, zl):
    return (group_of(y, 2 * zh + zl), core, zh, x, zl)


def unpack(words, dtype):
    n = words.shape[1]
    shifts = lax.broadcasted_iota(I32, (32, n), 0)
    rows = [
        jnp.right_shift(jnp.broadcast_to(words[i : i + 1, :], (32, n)), shifts) & 1
        for i in range(words.shape[0])
    ]
    return jnp.concatenate(rows, 0).astype(F32).astype(dtype)


def place():
    y, core = lax.axis_index("y"), lax.axis_index("core")
    zh, x, zl = lax.axis_index("zh"), lax.axis_index("x"), lax.axis_index("zl")
    return y, core, zh, x, zl


def planes(words, bits):
    return jnp.concatenate([jnp.right_shift(words, b) & 1 for b in bits], 0)


def scaled(words, bits):
    return jnp.concatenate(
        [jnp.right_shift(words, b - b % 8) & (1 << (b % 8)) for b in bits], 0
    )


OUTER = (((0,), (0,)), ((), ()))


def left_kernel(idp, r0, rp, rm, r2, lhs, keep):
    y, _, zh, x, zl = place()
    group = (16 - y - 2 * zh - zl) & 3
    ids = idp[...]
    q = (lax.broadcasted_iota(I32, (256, 16), 1) == ids // 768).astype(jnp.bfloat16)
    r = (lax.broadcasted_iota(I32, (256, 768), 1) == ids % 768).astype(jnp.bfloat16)
    keep[...] = jnp.where(lax.dot_general(q, r, OUTER, preferred_element_type=F32) > 0.5, 0, -1)
    for n, (ref, rel) in enumerate(((r0, 0), (rp, 1), (rm, 3), (r2, 2))):
        words = ref[...] & keep[pl.ds(4 * group + lax.rem(x + rel, 4), 1), :]
        at = slice(768 * n, 768 * n + 768)
        for t in range(4):
            bits = scaled(words[:48], range(8 * t, 8 * t + 8))
            lhs[384 * t : 384 * t + 384, at] = bits.astype(F32).astype(F8)
        lhs[1536:1792, at] = scaled(words[48:], range(32)).astype(F32).astype(F8)


def count_kernel(idp, keep, pair, hubs, r0, rp, rm, r2, yy, yc, lhs, out, rhs, near, turned, res):
    y, core, zh, x, zl = place()
    row = 2 * y + core
    z = 2 * zh + zl
    group = (16 - y - z) & 3
    sources = ((r0, 0), (rp, 1), (rm, 3), (r2, 2))
    ids = idp[...]
    wordhot = (lax.broadcasted_iota(I32, (256, 48), 1) + 48 * row == ids // 32).astype(F32)
    bithot = (lax.broadcasted_iota(I32, (256, 32), 1) == ids % 32).astype(F32)
    light = 1.0 - lax.dot_general(
        wordhot.astype(jnp.bfloat16), bithot.astype(jnp.bfloat16), OUTER, preferred_element_type=F32
    )
    for n, (ref, rel) in enumerate(sources):
        xs = lax.rem(x + rel, 4)
        other = (xs // 2) != core
        for side in range(2):
            at = pl.multiple_of(48 * side + 24 * lax.rem(xs, 2), 8)
            words = jnp.where(other, yc[pl.ds(at, 24), :], yy[pl.ds(at, 24), :])
            for part in range(3):
                base = 768 * n + 256 * part
                rhs[base : base + 256, 768 * side : 768 * side + 768] = unpack(
                    words[8 * part : 8 * part + 8, :], F8
                )
    zhl = (zh + 3 + zl) & 3
    left = pl.ds(4 * zhl + x, 1)
    right = pl.ds(4 * ((zhl + 1) & 3) + x, 1)
    mine = jnp.concatenate(
        [pair[0:48, :] & keep[left, :], pair[48:96, :] & keep[right, :]], 1
    )
    hub_words = jnp.concatenate(
        [hubs[0:8, :] & keep[left, :], hubs[8:16, :] & keep[right, :]], 1
    )
    hub_col = planes(hub_words, range(32)).astype(F32)
    near[...] = hub_col.astype(F8)
    for side in range(2):
        xs = 2 * core + side
        words = jnp.zeros((8, 768), I32)
        for ref, rel in sources:
            hit = (lax.rem(x + rel, 4) == xs) & (group == y)
            words = jnp.where(hit, ref[48:56, :], words)
        words = words & keep[pl.ds(2 * row + side, 1), :]
        turned[768 * side : 768 * side + 768, :] = jnp.concatenate([words] * 16, 0).T
    lane = lax.broadcasted_iota(I32, (48, 128), 1) // 8
    first = (zl == 0).astype(F32)
    once = ((x == 0) & (z == ((16 - 2 * y) & 3))).astype(F32)
    for t in range(4):
        paths = jnp.dot(
            lhs[384 * t : 384 * t + 384, :], rhs[...], preferred_element_type=F32
        )
        edges = planes(mine, range(8 * t, 8 * t + 8)).astype(F32)
        reach = lax.dot_general(
            edges.astype(F8), near[...], (((1,), (1,)), ((), ())), preferred_element_type=F32
        )
        for b in range(8):
            at = 8 * t + b
            rows = slice(48 * b, 48 * b + 48)
            words = turned[pl.ds(at, 48, stride=32), :]
            low = (jnp.right_shift(words, lane) & 1).astype(F32)
            high = (jnp.right_shift(words, lane + 16) & 1).astype(F32)
            closed = paths[rows, :] * edges[rows, :]
            with_hub = reach[rows, :128] * low + reach[rows, 128:] * high
            res[:, at : at + 1] = (0.5 / (1 << b)) * jnp.sum(
                closed, axis=1, keepdims=True
            ) + jnp.sum(with_hub, axis=1, keepdims=True)
            res[:, 32 + at : 33 + at] = first * jnp.sum(
                edges[rows, 768:], axis=1, keepdims=True
            ) + once * jnp.sum(low + high, axis=1, keepdims=True)
    paths = jnp.dot(lhs[1536:1792, :], rhs[...], preferred_element_type=F32)
    bit = (lax.broadcasted_iota(I32, (256, 1), 0) // 8) & 7
    unscale = jnp.right_shift(128, bit).astype(F32) * (0.5 / 128)
    hub_tri = unscale * jnp.sum(paths * hub_col, axis=1, keepdims=True)
    hub_deg = first * jnp.sum(hub_col[:, 768:], axis=1, keepdims=True)
    hub_part = lax.dot_general(
        wordhot,
        jnp.concatenate([hub_tri * bithot, hub_deg * bithot], 1),
        OUTER,
        precision=lax.Precision.HIGHEST,
        preferred_element_type=F32,
    )
    total = res[...] * jnp.concatenate([light, light], 1) + hub_part
    for c in range(16):
        line = jnp.concatenate(
            [total[3 * c + k : 3 * c + k + 1, 0:32] for k in range(3)]
            + [jnp.zeros((1, 32), F32)]
            + [total[3 * c + k : 3 * c + k + 1, 32:64] for k in range(3)]
            + [jnp.zeros((1, 32), F32)],
            1,
        )
        out[2 * c : 2 * c + 1, :] = line
        out[2 * c + 1 : 2 * c + 2, :] = line


def call(kernel, outs, scratch, args, flops, limit):
    vmem = pl.BlockSpec(memory_space=pltpu.VMEM)
    return pl.pallas_call(
        kernel,
        out_shape=[jax.ShapeDtypeStruct(*o) for o in outs],
        in_specs=[vmem] * len(args),
        out_specs=[vmem] * len(outs),
        scratch_shapes=scratch,
        cost_estimate=pl.CostEstimate(flops=flops, bytes_accessed=1 << 20, transcendentals=0),
        compiler_params=pltpu.CompilerParams(vmem_limit_bytes=limit * 2**20),
    )(*args)


def clustering(light_bits, hub_bits, hub_ids):
    _, _, _, _, zl = place()

    def send(value, source):
        return lax.ppermute(value, AXES, perm=permutation(source))

    rows = send(light_bits, fetch)
    beside = send(light_bits, partner)
    twin = send(hub_bits, lambda y, core, zh, x, zl: (y, core, zh, x, zl ^ 1))
    even = zl == 0
    hub = jnp.concatenate([jnp.where(even, hub_bits, twin), jnp.where(even, twin, hub_bits)], 0)
    hub_rows = send(hub, fetch)
    hub_beside = send(hub, partner)
    rows = jnp.concatenate([rows, hub_rows], 0)
    ring = [
        send(rows, lambda y, core, zh, x, zl, r=r: (y, core, zh, (x + r) % 4, zl))
        for r in (1, 3, 2)
    ]
    pair = jnp.concatenate(
        [jnp.where(even, beside, light_bits), jnp.where(even, light_bits, beside)], 0
    )
    hubs = jnp.concatenate([jnp.where(even, hub_beside, hub), jnp.where(even, hub, hub_beside)], 0)
    yy = send(pair, along_y)
    yc = send(yy, lambda y, core, zh, x, zl: (y, core ^ 1, zh, x, zl))
    planed = hub_ids.reshape(8, 32).T.reshape(256, 1)
    lhs, keep = call(
        left_kernel,
        [((1792, 3072), F8), ((16, 768), I32)],
        [],
        (planed, rows, *ring),
        1 << 30,
        12,
    )
    (table,) = call(
        count_kernel,
        [((32, 256), F32)],
        [
            pltpu.VMEM((3072, 1536), F8),
            pltpu.VMEM((256, 1536), F8),
            pltpu.VMEM((1536, 128), I32),
            pltpu.VMEM((48, 64), F32),
        ],
        (planed, keep, pair, hubs, rows, *ring, yy, yc, lhs),
        1 << 33,
        26,
    )
    everyone = lax.all_to_all(table, ("zh", "x", "zl"), 0, 0, tiled=True)
    total = jnp.sum(everyone, axis=0)
    return total[:OUT] / (1.0 + total[128 : 128 + OUT])


def solution(mesh):
    finer = Mesh(mesh.devices.reshape(SIZES), AXES)
    placed = (P(ROWS, COLS), P("zl", COLS), P())
    return jax.shard_map(
        clustering, mesh=finer, in_specs=placed, out_specs=P(ROWS + COLS), check_vma=False
    )
```

time: 75.4 us -> 73.3 us (0.972)
  the two profiles are of different devices: /device:TPU:1 before, /device:TPU:2 now
where the time goes in v4:
time: 73.3 us; the launch traced here: 73 us
  blocking collectives  23.2 us (32%)
  starting transfers between devices  20.3 us (28%)
  Pallas kernels  15.4 us (21%)
  waiting for transfers between devices  10.7 us (15%)
  other arithmetic  2.28 us (3%)
  local copies, waits for them, and re-layouts  0.98 us (1%)
    all_to_all x1, blocking collectives, clustering(): everyone = lax.all_to_all(table, ('zh', 'x', 'zl'), 0, 0, tiled=True)  23.2 us
    ppermute x10, starting transfers between devices, send(): return lax.ppermute(value, AXES, perm=permutation(source))  20.3 us
    pallas_call x2, Pallas kernels, call(): pl.pallas_call(kernel, out_shape=[jax.ShapeDtypeStruct(*o) for o in outs]...  15.4 us
    ppermute x10, waiting for transfers between devices, send(): return lax.ppermute(value, AXES, perm=permutation(source))  10.7 us
  transfers between devices with their start and end apart: 10, of which 3 were waited for; matrix products, arithmetic and copies ran while one was open for 4% of the time, Pallas kernels for 4%

profile of v4, /device:TPU:2, one launch (start us, length us, event | category | flops | bytes accessed | tf_op | source)
XLA Modules:
  0.0 73.0 jit_solution(16416937274927635043)
XLA Ops:
  0.0 1.9 %collective-permute-start.1 = (s32[4,768]{1,0:T(4,128)}, s32[4,768]{1,0:T(4,128)S(1)}, u32[]{:S(2)}, u32[]{:S(2)}) collective-permute-start(s32[4,768]{1,0:T(4,128)} %param.4), channel_id=1, source_target_pairs={{1,0},{0,1},{3,2},{2,3},{5,4},{4,5},{7,6},{6,7},{9,8},{8,9},{11,10... | collective-permute-start | bytes 36872 | tf_op jit(solution)/shard_map/ppermute | solution.py:211
  1.9 1.6 %collective-permute-start = (s32[48,768]{1,0:T(8,128)}, s32[48,768]{1,0:T(8,128)S(1)}, u32[]{:S(2)}, u32[]{:S(2)}) collective-permute-start(s32[48,768]{1,0:T(8,128)} %param.3), channel_id=1, source_target_pairs={{0,0},{25,1},{2,2},{27,3},{4,4},{29,5},{6,6},{31,7},{16,8},{9,9},{... | collective-permute-start | bytes 442376 | tf_op jit(solution)/shard_map/ppermute | solution.py:211
  3.5 5.4 %collective-permute-start.6 = (s32[48,768]{1,0:T(8,128)}, s32[48,768]{1,0:T(8,128)S(1)}, u32[]{:S(2)}, u32[]{:S(2)}) collective-permute-start(s32[48,768]{1,0:T(8,128)} %param.3), channel_id=1, source_target_pairs={{25,0},{8,1},{27,2},{10,3},{29,4},{12,5},{31,6},{14,7},{1,8},{16,9... | collective-permute-start | bytes 442376 | tf_op jit(solution)/shard_map/ppermute | solution.py:211
  8.9 0.8 %reshape.8 = s32[8,32]{1,0:T(8,128)S(1)} reshape(s32[256]{0:T(256)} %param.5) | data formatting | bytes 2048 | tf_op jit(solution)/shard_map/reshape | solution.py:231
  9.6 0.1 copy.7
  9.7 0.1 reshape.10.idp
  9.8 0.0 collective-permute-done.1
  9.8 0.7 broadcast_select_fusion.5
  10.5 5.2 %collective-permute-done.6 = s32[48,768]{1,0:T(8,128)S(1)} collective-permute-done((s32[48,768]{1,0:T(8,128)}, s32[48,768]{1,0:T(8,128)S(1)}, u32[]{:S(2)}, u32[]{:S(2)}) %collective-permute-start.6) | collective-permute-done | bytes 147488 | tf_op jit(solution)/shard_map/ppermute | solution.py:211
  15.7 0.9 %broadcast_select_fusion.1 = (s32[48,768]{1,0:T(8,128)S(1)}, s32[48,768]{1,0:T(8,128)S(1)}) fusion(s32[48,768]{1,0:T(8,128)S(1)} %collective-permute-done.6, s32[48,768]{1,0:T(8,128)} %param.3, pred[]{:T(512)S(6)} %eq.3), kind=kLoop, calls=%fused_computation.2 | loop fusion | flops 73728 | bytes 589825 | tf_op jit(solution)/shard_map/jit(_where)/select_n | solution.py:226
  16.7 0.7 collective-permute-start.8
  17.4 5.8 %collective-permute-start.7 = (s32[8,768]{1,0:T(8,128)S(1)}, s32[8,768]{1,0:T(8,128)S(1)}, u32[]{:S(2)}, u32[]{:S(2)}) collective-permute-start(s32[8,768]{1,0:T(8,128)S(1)} %pad_add_fusion.2), channel_id=1, source_target_pairs={{25,0},{8,1},{27,2},{10,3},{29,4},{12,5},{31,6},{14,7},{1,8},{16,9... | collective-permute-start | bytes 73736 | tf_op jit(solution)/shard_map/ppermute | solution.py:211
  23.2 0.7 collective-permute-start.2
  23.9 0.0 collective-permute-done
  23.9 0.0 collective-permute-done.2
  23.9 2.2 %collective-permute-start.5 = (s32[56,768]{1,0:T(8,128)S(1)}, s32[56,768]{1,0:T(8,128)S(1)}, u32[]{:S(2)}, u32[]{:S(2)}) collective-permute-start(s32[56,768]{1,0:T(8,128)S(1)} %constant_dynamic-update-slice_fusion.r0), channel_id=1, source_target_pairs={{4,0},{5,1},{6,2},{7,3},{0,4},{1,5},{2,6},{3,7},{12,8},{13,9},{14,... | collective-permute-start | bytes 516104 | tf_op jit(solution)/shard_map/ppermute | solution.py:211
  26.1 0.0 collective-permute-start.4
  26.1 2.0 %collective-permute-start.3 = (s32[56,768]{1,0:T(8,128)S(1)}, s32[56,768]{1,0:T(8,128)S(1)}, u32[]{:S(2)}, u32[]{:S(2)}) collective-permute-start(s32[56,768]{1,0:T(8,128)S(1)} %constant_dynamic-update-slice_fusion.r0), channel_id=1, source_target_pairs={{2,0},{3,1},{4,2},{5,3},{6,4},{7,5},{0,6},{1,7},{10,8},{11,9},{12,... | collective-permute-start | bytes 516104 | tf_op jit(solution)/shard_map/ppermute | solution.py:211
  28.2 0.0 collective-permute-done.8.yy
  28.2 0.0 collective-permute-start.9
  28.2 0.0 collective-permute-done.7
  28.2 3.7 %collective-permute-done.5.r2 = s32[56,768]{1,0:T(8,128)S(1)} collective-permute-done((s32[56,768]{1,0:T(8,128)S(1)}, s32[56,768]{1,0:T(8,128)S(1)}, u32[]{:S(2)}, u32[]{:S(2)}) %collective-permute-start.5) | collective-permute-done | bytes 172064 | tf_op jit(solution)/shard_map/ppermute | solution.py:211
  31.9 1.8 %collective-permute-done.4.rm = s32[56,768]{1,0:T(8,128)S(1)} collective-permute-done((s32[56,768]{1,0:T(8,128)S(1)}, s32[56,768]{1,0:T(8,128)S(1)}, u32[]{:S(2)}, u32[]{:S(2)}) %collective-permute-start.4) | collective-permute-done | bytes 172064 | tf_op jit(solution)/shard_map/ppermute | solution.py:211
  33.7 0.0 collective-permute-done.3.rp
  33.7 2.9 %shard_map.37 = (f8e4m3fn[1792,3072]{1,0:T(32,128)(4,1)S(1)}, s32[16,768]{1,0:T(8,128)S(1)}) custom-call(s32[256,1]{1,0:T(8,128)S(1)} %reshape.10.idp, s32[56,768]{1,0:T(8,128)S(1)} %constant_dynamic-update-slice_fusion.r0, s32[56,768]{1,0:T(8,128)S(1)} %collective-permute-done.3.rp, s32[56,768]{1,0:T(8,128)S(1)} %collective-permute-done.4.rm, ...), custom_call_target="tpu_custom_call" | custom-call | flops 1073741824 | bytes 1048576 | tf_op jit(solution)/shard_map/pallas_call | solution.py:196
  36.6 0.0 collective-permute-done.9.yc
  36.6 12.5 %shard_map.38 = f32[32,256]{1,0:T(8,128)S(1)} custom-call(s32[256,1]{1,0:T(8,128)S(1)} %reshape.10.idp, s32[16,768]{1,0:T(8,128)S(1)} %get-tuple-element.7.keep, s32[96,768]{1,0:T(8,128)S(1)} %pad_add_fusion.pair, s32[16,768]{1,0:T(8,128)S(1)} %pad_add_fusion.1.hubs, s32[56,768]{1,0:T(8,128)S(1)} %constant_dynamic-update-slice_fusion.r0, ...), custom_call_target="tpu_custom_call" | custom-call | flops 8589934592 | bytes 1048576 | tf_op jit(solution)/shard_map/pallas_call | solution.py:196
  49.2 23.2 %all_to_all.9 = f32[32,1,256]{2,1,0:T(1,128)S(1)} all-to-all(f32[32,1,256]{2,1,0:T(1,128)S(1)} %copy.10), channel_id=1, replica_groups=mesh['y'=4,'core'=2,'zh'=4,'x'=4,'zl'=2] {'zh','x','zl'}, dimensions={0} | all-to-all | bytes 65536 | tf_op jit(solution)/shard_map/all_to_all | solution.py:253
  72.4 0.1 reduce_sum.9
  72.4 0.5 add_divide_fusion
  (7 shorter events, 0.1 us)
Async XLA Ops:
  0.0 9.8 %collective-permute-start.1 = (s32[4,768]{1,0:T(4,128)}, s32[4,768]{1,0:T(4,128)S(1)}, u32[]{:S(2)}, u32[]{:S(2)}) collective-permute-start(s32[4,768]{1,0:T(4,128)} %param.4), channel_id=1, source_target_pairs={{1,0},{0,1},{3,2},{2,3},{5,4},{4,5},{7,6},{6,7},{9,8},{8,9},{11,10... | collective-permute-start | bytes 36872 | tf_op jit(solution)/shard_map/ppermute | solution.py:211
  1.9 21.9 %collective-permute-start = (s32[48,768]{1,0:T(8,128)}, s32[48,768]{1,0:T(8,128)S(1)}, u32[]{:S(2)}, u32[]{:S(2)}) collective-permute-start(s32[48,768]{1,0:T(8,128)} %param.3), channel_id=1, source_target_pairs={{0,0},{25,1},{2,2},{27,3},{4,4},{29,5},{6,6},{31,7},{16,8},{9,9},{... | collective-permute-start | bytes 442376 | tf_op jit(solution)/shard_map/ppermute | solution.py:211
  3.5 12.2 %collective-permute-start.6 = (s32[48,768]{1,0:T(8,128)}, s32[48,768]{1,0:T(8,128)S(1)}, u32[]{:S(2)}, u32[]{:S(2)}) collective-permute-start(s32[48,768]{1,0:T(8,128)} %param.3), channel_id=1, source_target_pairs={{25,0},{8,1},{27,2},{10,3},{29,4},{12,5},{31,6},{14,7},{1,8},{16,9... | collective-permute-start | bytes 442376 | tf_op jit(solution)/shard_map/ppermute | solution.py:211
  16.7 11.5 %collective-permute-start.8 = (s32[96,768]{1,0:T(8,128)S(1)}, s32[96,768]{1,0:T(8,128)S(1)}, u32[]{:S(2)}, u32[]{:S(2)}) collective-permute-start(s32[96,768]{1,0:T(8,128)S(1)} %pad_add_fusion.pair), channel_id=1, source_target_pairs={{0,0},{193,1},{2,2},{195,3},{4,4},{197,5},{6,6},{199,7},{136,8},{7... | collective-permute-start | bytes 884744 | tf_op jit(solution)/shard_map/ppermute | solution.py:211
  17.4 10.8 %collective-permute-start.7 = (s32[8,768]{1,0:T(8,128)S(1)}, s32[8,768]{1,0:T(8,128)S(1)}, u32[]{:S(2)}, u32[]{:S(2)}) collective-permute-start(s32[8,768]{1,0:T(8,128)S(1)} %pad_add_fusion.2), channel_id=1, source_target_pairs={{25,0},{8,1},{27,2},{10,3},{29,4},{12,5},{31,6},{14,7},{1,8},{16,9... | collective-permute-start | bytes 73736 | tf_op jit(solution)/shard_map/ppermute | solution.py:211
  23.2 0.7 collective-permute-start.2
  23.9 8.0 %collective-permute-start.5 = (s32[56,768]{1,0:T(8,128)S(1)}, s32[56,768]{1,0:T(8,128)S(1)}, u32[]{:S(2)}, u32[]{:S(2)}) collective-permute-start(s32[56,768]{1,0:T(8,128)S(1)} %constant_dynamic-update-slice_fusion.r0), channel_id=1, source_target_pairs={{4,0},{5,1},{6,2},{7,3},{0,4},{1,5},{2,6},{3,7},{12,8},{13,9},{14,... | collective-permute-start | bytes 516104 | tf_op jit(solution)/shard_map/ppermute | solution.py:211
  26.1 7.6 %collective-permute-start.4 = (s32[56,768]{1,0:T(8,128)S(1)}, s32[56,768]{1,0:T(8,128)S(1)}, u32[]{:S(2)}, u32[]{:S(2)}) collective-permute-start(s32[56,768]{1,0:T(8,128)S(1)} %constant_dynamic-update-slice_fusion.r0), channel_id=1, source_target_pairs={{6,0},{7,1},{0,2},{1,3},{2,4},{3,5},{4,6},{5,7},{14,8},{15,9},{8,1... | collective-permute-start | bytes 516104 | tf_op jit(solution)/shard_map/ppermute | solution.py:211
  26.1 7.6 %collective-permute-start.3 = (s32[56,768]{1,0:T(8,128)S(1)}, s32[56,768]{1,0:T(8,128)S(1)}, u32[]{:S(2)}, u32[]{:S(2)}) collective-permute-start(s32[56,768]{1,0:T(8,128)S(1)} %constant_dynamic-update-slice_fusion.r0), channel_id=1, source_target_pairs={{2,0},{3,1},{4,2},{5,3},{6,4},{7,5},{0,6},{1,7},{10,8},{11,9},{12,... | collective-permute-start | bytes 516104 | tf_op jit(solution)/shard_map/ppermute | solution.py:211
  28.2 8.5 %collective-permute-start.9 = (s32[96,768]{1,0:T(8,128)S(1)}, s32[96,768]{1,0:T(8,128)S(1)}, u32[]{:S(2)}, u32[]{:S(2)}) collective-permute-start(s32[96,768]{1,0:T(8,128)S(1)} %collective-permute-done.8.yy), channel_id=1, source_target_pairs={{32,0},{33,1},{34,2},{35,3},{36,4},{37,5},{38,6},{39,7},{40,8},{41... | collective-permute-start | bytes 884744 | tf_op jit(solution)/shard_map/ppermute | solution.py:211

commit v5 on v4

--- a/solution.py
+++ b/solution.py
@@ -99,7 +99,22 @@
         lhs[1536:1792, at] = scaled(words[48:], range(32)).astype(F32).astype(F8)
 
 
-def count_kernel(idp, keep, pair, hubs, r0, rp, rm, r2, yy, yc, lhs, out, rhs, near, turned, res):
+def right_kernel(yy, yc, rhs):
+    _, core, _, x, _ = place()
+    for n, rel in enumerate((0, 1, 3, 2)):
+        xs = lax.rem(x + rel, 4)
+        other = (xs // 2) != core
+        for side in range(2):
+            at = pl.multiple_of(48 * side + 24 * lax.rem(xs, 2), 8)
+            words = jnp.where(other, yc[pl.ds(at, 24), :], yy[pl.ds(at, 24), :])
+            for part in range(3):
+                base = 768 * n + 256 * part
+                rhs[base : base + 256, 768 * side : 768 * side + 768] = unpack(
+                    words[8 * part : 8 * part + 8, :], F8
+                )
+
+
+def count_kernel(idp, keep, pair, hubs, r0, rp, rm, r2, lhs, rhs, out, near, turned, res):
     y, core, zh, x, zl = place()
     row = 2 * y + core
     z = 2 * zh + zl
@@ -111,25 +126,11 @@
     light = 1.0 - lax.dot_general(
         wordhot.astype(jnp.bfloat16), bithot.astype(jnp.bfloat16), OUTER, preferred_element_type=F32
     )
-    for n, (ref, rel) in enumerate(sources):
-        xs = lax.rem(x + rel, 4)
-        other = (xs // 2) != core
-        for side in range(2):
-            at = pl.multiple_of(48 * side + 24 * lax.rem(xs, 2), 8)
-            words = jnp.where(other, yc[pl.ds(at, 24), :], yy[pl.ds(at, 24), :])
-            for part in range(3):
-                base = 768 * n + 256 * part
-                rhs[base : base + 256, 768 * side : 768 * side + 768] = unpack(
-                    words[8 * part : 8 * part + 8, :], F8
-                )
-    zhl = (zh + 3 + zl) & 3
-    left = pl.ds(4 * zhl + x, 1)
-    right = pl.ds(4 * ((zhl + 1) & 3) + x, 1)
-    mine = jnp.concatenate(
-        [pair[0:48, :] & keep[left, :], pair[48:96, :] & keep[right, :]], 1
-    )
+    own = pl.ds(4 * zh + x, 1)
+    side = pl.ds(4 * ((zh + 3 + 2 * zl) & 3) + x, 1)
+    mine = jnp.concatenate([pair[0:48, :] & keep[own, :], pair[48:96, :] & keep[side, :]], 1)
     hub_words = jnp.concatenate(
-        [hubs[0:8, :] & keep[left, :], hubs[8:16, :] & keep[right, :]], 1
+        [hubs[0:8, :] & keep[own, :], hubs[8:16, :] & keep[side, :]], 1
     )
     hub_col = planes(hub_words, range(32)).astype(F32)
     near[...] = hub_col.astype(F8)
@@ -164,13 +165,13 @@
                 closed, axis=1, keepdims=True
             ) + jnp.sum(with_hub, axis=1, keepdims=True)
             res[:, 32 + at : 33 + at] = first * jnp.sum(
-                edges[rows, 768:], axis=1, keepdims=True
+                edges[rows, :768], axis=1, keepdims=True
             ) + once * jnp.sum(low + high, axis=1, keepdims=True)
     paths = jnp.dot(lhs[1536:1792, :], rhs[...], preferred_element_type=F32)
     bit = (lax.broadcasted_iota(I32, (256, 1), 0) // 8) & 7
     unscale = jnp.right_shift(128, bit).astype(F32) * (0.5 / 128)
     hub_tri = unscale * jnp.sum(paths * hub_col, axis=1, keepdims=True)
-    hub_deg = first * jnp.sum(hub_col[:, 768:], axis=1, keepdims=True)
+    hub_deg = first * jnp.sum(hub_col[:, :768], axis=1, keepdims=True)
     hub_part = lax.dot_general(
         wordhot,
         jnp.concatenate([hub_tri * bithot, hub_deg * bithot], 1),
@@ -222,13 +223,12 @@
         send(rows, lambda y, core, zh, x, zl, r=r: (y, core, zh, (x + r) % 4, zl))
         for r in (1, 3, 2)
     ]
-    pair = jnp.concatenate(
-        [jnp.where(even, beside, light_bits), jnp.where(even, light_bits, beside)], 0
-    )
-    hubs = jnp.concatenate([jnp.where(even, hub_beside, hub), jnp.where(even, hub, hub_beside)], 0)
+    pair = jnp.concatenate([light_bits, beside], 0)
+    hubs = jnp.concatenate([hub, hub_beside], 0)
     yy = send(pair, along_y)
     yc = send(yy, lambda y, core, zh, x, zl: (y, core ^ 1, zh, x, zl))
     planed = hub_ids.reshape(8, 32).T.reshape(256, 1)
+    (rhs,) = call(right_kernel, [((3072, 1536), F8)], [], (yy, yc), 1 << 30, 8)
     lhs, keep = call(
         left_kernel,
         [((1792, 3072), F8), ((16, 768), I32)],
@@ -241,14 +241,13 @@
         count_kernel,
         [((32, 256), F32)],
         [
-            pltpu.VMEM((3072, 1536), F8),
             pltpu.VMEM((256, 1536), F8),
             pltpu.VMEM((1536, 128), I32),
             pltpu.VMEM((48, 64), F32),
         ],
-        (planed, keep, pair, hubs, rows, *ring, yy, yc, lhs),
+        (planed, keep, pair, hubs, rows, *ring, lhs, rhs),
         1 << 33,
-        26,
+        24,
     )
     everyone = lax.all_to_all(table, ("zh", "x", "zl"), 0, 0, tiled=True)
     total = jnp.sum(everyone, axis=0)

time: 73.3 us -> 68.6 us (0.936)
  the two profiles are of different devices: /device:TPU:2 before, /device:TPU:8 now
where the time goes in v5:
time: 68.6 us; the launch traced here: 68.3 us
  starting transfers between devices  24.1 us (35%)
  blocking collectives  16.9 us (25%)
  Pallas kernels  16.2 us (24%)
  waiting for transfers between devices  7.85 us (11%)
  local copies, waits for them, and re-layouts  1.91 us (3%)
  other arithmetic  1.32 us (2%)
    ppermute x10, starting transfers between devices, send(): return lax.ppermute(value, AXES, perm=permutation(source))  24.1 us
    all_to_all x1, blocking collectives, clustering(): everyone = lax.all_to_all(table, ('zh', 'x', 'zl'), 0, 0, tiled=True)  16.9 us
    pallas_call x3, Pallas kernels, call(): pl.pallas_call(kernel, out_shape=[jax.ShapeDtypeStruct(*o) for o in outs]...  16.2 us
    ppermute x10, waiting for transfers between devices, send(): return lax.ppermute(value, AXES, perm=permutation(source))  7.85 us
  transfers between devices with their start and end apart: 10, of which 5 were waited for; matrix products, arithmetic and copies ran while one was open for 4% of the time, Pallas kernels for 4%

profile of v5, /device:TPU:8, one launch (start us, length us, event | category | flops | bytes accessed | tf_op | source)
XLA Modules:
  0.0 68.3 jit_solution(8481228630438594698)
XLA Ops:
  0.0 5.9 %collective-permute-start.6 = (s32[48,768]{1,0:T(8,128)}, s32[48,768]{1,0:T(8,128)S(1)}, u32[]{:S(2)}, u32[]{:S(2)}) collective-permute-start(s32[48,768]{1,0:T(8,128)} %param.3), channel_id=1, source_target_pairs={{25,0},{8,1},{27,2},{10,3},{29,4},{12,5},{31,6},{14,7},{1,8},{16,9... | collective-permute-start | bytes 442376 | tf_op jit(solution)/shard_map/ppermute | solution.py:212
  5.9 1.9 %collective-permute-start = (s32[48,768]{1,0:T(8,128)}, s32[48,768]{1,0:T(8,128)S(1)}, u32[]{:S(2)}, u32[]{:S(2)}) collective-permute-start(s32[48,768]{1,0:T(8,128)} %param.3), channel_id=1, source_target_pairs={{0,0},{25,1},{2,2},{27,3},{4,4},{29,5},{6,6},{31,7},{16,8},{9,9},{... | collective-permute-start | bytes 442376 | tf_op jit(solution)/shard_map/ppermute | solution.py:212
  7.8 2.5 %collective-permute-start.1 = (s32[4,768]{1,0:T(4,128)}, s32[4,768]{1,0:T(4,128)S(1)}, u32[]{:S(2)}, u32[]{:S(2)}) collective-permute-start(s32[4,768]{1,0:T(4,128)} %param.4), channel_id=1, source_target_pairs={{1,0},{0,1},{3,2},{2,3},{5,4},{4,5},{7,6},{6,7},{9,8},{8,9},{11,10... | collective-permute-start | bytes 36872 | tf_op jit(solution)/shard_map/ppermute | solution.py:212
  10.3 0.9 %constant_dynamic-update-slice_fusion.3 = s32[96,768]{1,0:T(8,128)S(1)} fusion(s32[48,768]{1,0:T(8,128)} %param.3), kind=kLoop, calls=%fused_computation.5 | loop fusion | bytes 294912
  11.2 0.0 collective-permute-done.6
  11.3 3.7 %collective-permute-start.8 = (s32[96,768]{1,0:T(8,128)S(1)}, s32[96,768]{1,0:T(8,128)S(1)}, u32[]{:S(2)}, u32[]{:S(2)}) collective-permute-start(s32[96,768]{1,0:T(8,128)S(1)} %constant_dynamic-update-slice_fusion.2.pair), channel_id=1, source_target_pairs={{0,0},{193,1},{2,2},{195,3},{4,4},{197,5},{6,6},{199,7},{136,8},{7... | collective-permute-start | bytes 884744 | tf_op jit(solution)/shard_map/ppermute | solution.py:212
  15.0 0.0 collective-permute-done.1
  15.0 0.7 %broadcast_select_fusion.1 = (s32[4,768]{1,0:T(4,128)S(1)}, s32[4,768]{1,0:T(4,128)S(1)}) fusion(s32[4,768]{1,0:T(4,128)} %param.4, s32[4,768]{1,0:T(4,128)S(1)} %collective-permute-done.1, pred[]{:T(512)S(6)} %eq.3), kind=kLoop, calls=%fused_computation.7 | loop fusion | flops 6144 | bytes 49153 | tf_op jit(solution)/shard_map/jit(_where)/select_n | solution.py:218
  15.7 2.9 %collective-permute-start.2 = (s32[8,768]{1,0:T(8,128)S(1)}, s32[8,768]{1,0:T(8,128)S(1)}, u32[]{:S(2)}, u32[]{:S(2)}) collective-permute-start(s32[8,768]{1,0:T(8,128)S(1)} %pad_add_fusion.1), channel_id=1, source_target_pairs={{0,0},{25,1},{2,2},{27,3},{4,4},{29,5},{6,6},{31,7},{16,8},{9,9},{... | collective-permute-start | bytes 73736 | tf_op jit(solution)/shard_map/ppermute | solution.py:212
  18.6 0.0 collective-permute-done
  18.6 3.9 %collective-permute-done.8.yy = s32[96,768]{1,0:T(8,128)S(1)} collective-permute-done((s32[96,768]{1,0:T(8,128)S(1)}, s32[96,768]{1,0:T(8,128)S(1)}, u32[]{:S(2)}, u32[]{:S(2)}) %collective-permute-start.8) | collective-permute-done | bytes 294944 | tf_op jit(solution)/shard_map/ppermute | solution.py:212
  22.6 0.0 collective-permute-start.9
  22.6 0.1 collective-permute-done.2
  22.7 3.0 %collective-permute-start.5 = (s32[56,768]{1,0:T(8,128)S(1)}, s32[56,768]{1,0:T(8,128)S(1)}, u32[]{:S(2)}, u32[]{:S(2)}) collective-permute-start(s32[56,768]{1,0:T(8,128)S(1)} %constant_dynamic-update-slice_fusion.r0), channel_id=1, source_target_pairs={{4,0},{5,1},{6,2},{7,3},{0,4},{1,5},{2,6},{3,7},{12,8},{13,9},{14,... | collective-permute-start | bytes 516104 | tf_op jit(solution)/shard_map/ppermute | solution.py:212
  25.7 0.6 collective-permute-start.4
  26.3 2.6 %collective-permute-start.3 = (s32[56,768]{1,0:T(8,128)S(1)}, s32[56,768]{1,0:T(8,128)S(1)}, u32[]{:S(2)}, u32[]{:S(2)}) collective-permute-start(s32[56,768]{1,0:T(8,128)S(1)} %constant_dynamic-update-slice_fusion.r0), channel_id=1, source_target_pairs={{2,0},{3,1},{4,2},{5,3},{6,4},{7,5},{0,6},{1,7},{10,8},{11,9},{12,... | collective-permute-start | bytes 516104 | tf_op jit(solution)/shard_map/ppermute | solution.py:212
  28.9 0.9 %collective-permute-start.7 = (s32[8,768]{1,0:T(8,128)S(1)}, s32[8,768]{1,0:T(8,128)S(1)}, u32[]{:S(2)}, u32[]{:S(2)}) collective-permute-start(s32[8,768]{1,0:T(8,128)S(1)} %pad_add_fusion.1), channel_id=1, source_target_pairs={{25,0},{8,1},{27,2},{10,3},{29,4},{12,5},{31,6},{14,7},{1,8},{16,9... | collective-permute-start | bytes 73736 | tf_op jit(solution)/shard_map/ppermute | solution.py:212
  29.9 0.8 %reshape.8 = s32[8,32]{1,0:T(8,128)S(1)} reshape(s32[256]{0:T(256)} %param.5) | data formatting | bytes 2048 | tf_op jit(solution)/shard_map/reshape | solution.py:230
  30.6 0.1 copy.7
  30.7 0.1 reshape.10.idp
  30.8 3.2 %collective-permute-done.7 = s32[8,768]{1,0:T(8,128)S(1)} collective-permute-done((s32[8,768]{1,0:T(8,128)S(1)}, s32[8,768]{1,0:T(8,128)S(1)}, u32[]{:S(2)}, u32[]{:S(2)}) %collective-permute-start.7) | collective-permute-done | bytes 24608 | tf_op jit(solution)/shard_map/ppermute | solution.py:212
  34.0 0.0 collective-permute-done.5.r2
  34.0 0.6 collective-permute-done.4.rm
  34.6 0.1 collective-permute-done.3.rp
  34.6 2.9 %shard_map.37 = (f8e4m3fn[1792,3072]{1,0:T(32,128)(4,1)S(1)}, s32[16,768]{1,0:T(8,128)S(1)}) custom-call(s32[256,1]{1,0:T(8,128)S(1)} %reshape.10.idp, s32[56,768]{1,0:T(8,128)S(1)} %constant_dynamic-update-slice_fusion.r0, s32[56,768]{1,0:T(8,128)S(1)} %collective-permute-done.3.rp, s32[56,768]{1,0:T(8,128)S(1)} %collective-permute-done.4.rm, ...), custom_call_target="tpu_custom_call" | custom-call | flops 1073741824 | bytes 1048576 | tf_op jit(solution)/shard_map/pallas_call | solution.py:197
  37.6 0.0 collective-permute-done.9.yc
  37.6 2.5 %shard_map.38.rhs = f8e4m3fn[3072,1536]{1,0:T(32,128)(4,1)S(1)} custom-call(s32[96,768]{1,0:T(8,128)S(1)} %collective-permute-done.8.yy, s32[96,768]{1,0:T(8,128)S(1)} %collective-permute-done.9.yc), custom_call_target="tpu_custom_call" | custom-call | flops 1073741824 | bytes 1048576 | tf_op jit(solution)/shard_map/pallas_call | solution.py:197
  40.1 10.8 %shard_map.39 = f32[32,256]{1,0:T(8,128)S(1)} custom-call(s32[256,1]{1,0:T(8,128)S(1)} %reshape.10.idp, s32[16,768]{1,0:T(8,128)S(1)} %get-tuple-element.7.keep, s32[96,768]{1,0:T(8,128)S(1)} %constant_dynamic-update-slice_fusion.2.pair, s32[16,768]{1,0:T(8,128)S(1)} %pad_add_fusion.hubs, s32[56,768]{1,0:T(8,128)S(1)} %constant_dynamic-update-slice_fusion.r0, ...), custom_call_target="tpu_custom_call" | custom-call | flops 8589934592 | bytes 1048576 | tf_op jit(solution)/shard_map/pallas_call | solution.py:197
  50.9 16.9 %all_to_all.9 = f32[32,1,256]{2,1,0:T(1,128)S(1)} all-to-all(f32[32,1,256]{2,1,0:T(1,128)S(1)} %copy.10), channel_id=1, replica_groups=mesh['y'=4,'core'=2,'zh'=4,'x'=4,'zl'=2] {'zh','x','zl'}, dimensions={0} | all-to-all | bytes 65536 | tf_op jit(solution)/shard_map/all_to_all | solution.py:252
  67.8 0.1 reduce_sum.9
  67.8 0.5 add_divide_fusion
  (6 shorter events, 0.1 us)
Async XLA Ops:
  0.0 11.2 %collective-permute-start.6 = (s32[48,768]{1,0:T(8,128)}, s32[48,768]{1,0:T(8,128)S(1)}, u32[]{:S(2)}, u32[]{:S(2)}) collective-permute-start(s32[48,768]{1,0:T(8,128)} %param.3), channel_id=1, source_target_pairs={{25,0},{8,1},{27,2},{10,3},{29,4},{12,5},{31,6},{14,7},{1,8},{16,9... | collective-permute-start | bytes 442376 | tf_op jit(solution)/shard_map/ppermute | solution.py:212
  5.9 12.7 %collective-permute-start = (s32[48,768]{1,0:T(8,128)}, s32[48,768]{1,0:T(8,128)S(1)}, u32[]{:S(2)}, u32[]{:S(2)}) collective-permute-start(s32[48,768]{1,0:T(8,128)} %param.3), channel_id=1, source_target_pairs={{0,0},{25,1},{2,2},{27,3},{4,4},{29,5},{6,6},{31,7},{16,8},{9,9},{... | collective-permute-start | bytes 442376 | tf_op jit(solution)/shard_map/ppermute | solution.py:212
  7.8 7.2 %collective-permute-start.1 = (s32[4,768]{1,0:T(4,128)}, s32[4,768]{1,0:T(4,128)S(1)}, u32[]{:S(2)}, u32[]{:S(2)}) collective-permute-start(s32[4,768]{1,0:T(4,128)} %param.4), channel_id=1, source_target_pairs={{1,0},{0,1},{3,2},{2,3},{5,4},{4,5},{7,6},{6,7},{9,8},{8,9},{11,10... | collective-permute-start | bytes 36872 | tf_op jit(solution)/shard_map/ppermute | solution.py:212
  11.3 11.3 %collective-permute-start.8 = (s32[96,768]{1,0:T(8,128)S(1)}, s32[96,768]{1,0:T(8,128)S(1)}, u32[]{:S(2)}, u32[]{:S(2)}) collective-permute-start(s32[96,768]{1,0:T(8,128)S(1)} %constant_dynamic-update-slice_fusion.2.pair), channel_id=1, source_target_pairs={{0,0},{193,1},{2,2},{195,3},{4,4},{197,5},{6,6},{199,7},{136,8},{7... | collective-permute-start | bytes 884744 | tf_op jit(solution)/shard_map/ppermute | solution.py:212
  15.7 6.9 %collective-permute-start.2 = (s32[8,768]{1,0:T(8,128)S(1)}, s32[8,768]{1,0:T(8,128)S(1)}, u32[]{:S(2)}, u32[]{:S(2)}) collective-permute-start(s32[8,768]{1,0:T(8,128)S(1)} %pad_add_fusion.1), channel_id=1, source_target_pairs={{0,0},{25,1},{2,2},{27,3},{4,4},{29,5},{6,6},{31,7},{16,8},{9,9},{... | collective-permute-start | bytes 73736 | tf_op jit(solution)/shard_map/ppermute | solution.py:212
  22.6 15.0 %collective-permute-start.9 = (s32[96,768]{1,0:T(8,128)S(1)}, s32[96,768]{1,0:T(8,128)S(1)}, u32[]{:S(2)}, u32[]{:S(2)}) collective-permute-start(s32[96,768]{1,0:T(8,128)S(1)} %collective-permute-done.8.yy), channel_id=1, source_target_pairs={{32,0},{33,1},{34,2},{35,3},{36,4},{37,5},{38,6},{39,7},{40,8},{41... | collective-permute-start | bytes 884744 | tf_op jit(solution)/shard_map/ppermute | solution.py:212
  22.7 11.3 %collective-permute-start.5 = (s32[56,768]{1,0:T(8,128)S(1)}, s32[56,768]{1,0:T(8,128)S(1)}, u32[]{:S(2)}, u32[]{:S(2)}) collective-permute-start(s32[56,768]{1,0:T(8,128)S(1)} %constant_dynamic-update-slice_fusion.r0), channel_id=1, source_target_pairs={{4,0},{5,1},{6,2},{7,3},{0,4},{1,5},{2,6},{3,7},{12,8},{13,9},{14,... | collective-permute-start | bytes 516104 | tf_op jit(solution)/shard_map/ppermute | solution.py:212
  25.7 8.9 %collective-permute-start.4 = (s32[56,768]{1,0:T(8,128)S(1)}, s32[56,768]{1,0:T(8,128)S(1)}, u32[]{:S(2)}, u32[]{:S(2)}) collective-permute-start(s32[56,768]{1,0:T(8,128)S(1)} %constant_dynamic-update-slice_fusion.r0), channel_id=1, source_target_pairs={{6,0},{7,1},{0,2},{1,3},{2,4},{3,5},{4,6},{5,7},{14,8},{15,9},{8,1... | collective-permute-start | bytes 516104 | tf_op jit(solution)/shard_map/ppermute | solution.py:212
  26.3 8.4 %collective-permute-start.3 = (s32[56,768]{1,0:T(8,128)S(1)}, s32[56,768]{1,0:T(8,128)S(1)}, u32[]{:S(2)}, u32[]{:S(2)}) collective-permute-start(s32[56,768]{1,0:T(8,128)S(1)} %constant_dynamic-update-slice_fusion.r0), channel_id=1, source_target_pairs={{2,0},{3,1},{4,2},{5,3},{6,4},{7,5},{0,6},{1,7},{10,8},{11,9},{12,... | collective-permute-start | bytes 516104 | tf_op jit(solution)/shard_map/ppermute | solution.py:212
  28.9 5.0 %collective-permute-start.7 = (s32[8,768]{1,0:T(8,128)S(1)}, s32[8,768]{1,0:T(8,128)S(1)}, u32[]{:S(2)}, u32[]{:S(2)}) collective-permute-start(s32[8,768]{1,0:T(8,128)S(1)} %pad_add_fusion.1), channel_id=1, source_target_pairs={{25,0},{8,1},{27,2},{10,3},{29,4},{12,5},{31,6},{14,7},{1,8},{16,9... | collective-permute-start | bytes 73736 | tf_op jit(solution)/shard_map/ppermute | solution.py:212

commit v6 on v5

--- a/solution.py
+++ b/solution.py
@@ -13,6 +13,8 @@
 F8 = jnp.float8_e4m3fn
 F32 = jnp.float32
 I32 = jnp.int32
+I8 = jnp.int8
+BF16 = jnp.bfloat16
 OUT = 96
 
 
@@ -54,14 +56,15 @@
     return (group_of(y, 2 * zh + zl), core, zh, x, zl)
 
 
-def unpack(words, dtype):
+def unpack(words):
     n = words.shape[1]
     shifts = lax.broadcasted_iota(I32, (32, n), 0)
     rows = [
-        jnp.right_shift(jnp.broadcast_to(words[i : i + 1, :], (32, n)), shifts) & 1
+        jnp.right_shift(jnp.broadcast_to(words[i : i + 1, :], (32, n)), shifts)
         for i in range(words.shape[0])
     ]
-    return jnp.concatenate(rows, 0).astype(F32).astype(dtype)
+    bits = jnp.concatenate(rows, 0).astype(I8) & I8(1)
+    return bits.astype(BF16).astype(F8)
 
 
 def place():
@@ -74,29 +77,16 @@
     return jnp.concatenate([jnp.right_shift(words, b) & 1 for b in bits], 0)
 
 
-def scaled(words, bits):
-    return jnp.concatenate(
-        [jnp.right_shift(words, b - b % 8) & (1 << (b % 8)) for b in bits], 0
-    )
-
-
+def octets(words, at):
+    return jnp.concatenate([jnp.right_shift(words, a) for a in at], 0).astype(I8)
+
+
+def plane(bytes8, b):
+    return (bytes8 & I8(SCALE[b])).astype(BF16).astype(F8)
+
+
+SCALE = (1, 2, 4, 8, 16, 32, 64, -128)
 OUTER = (((0,), (0,)), ((), ()))
-
-
-def left_kernel(idp, r0, rp, rm, r2, lhs, keep):
-    y, _, zh, x, zl = place()
-    group = (16 - y - 2 * zh - zl) & 3
-    ids = idp[...]
-    q = (lax.broadcasted_iota(I32, (256, 16), 1) == ids // 768).astype(jnp.bfloat16)
-    r = (lax.broadcasted_iota(I32, (256, 768), 1) == ids % 768).astype(jnp.bfloat16)
-    keep[...] = jnp.where(lax.dot_general(q, r, OUTER, preferred_element_type=F32) > 0.5, 0, -1)
-    for n, (ref, rel) in enumerate(((r0, 0), (rp, 1), (rm, 3), (r2, 2))):
-        words = ref[...] & keep[pl.ds(4 * group + lax.rem(x + rel, 4), 1), :]
-        at = slice(768 * n, 768 * n + 768)
-        for t in range(4):
-            bits = scaled(words[:48], range(8 * t, 8 * t + 8))
-            lhs[384 * t : 384 * t + 384, at] = bits.astype(F32).astype(F8)
-        lhs[1536:1792, at] = scaled(words[48:], range(32)).astype(F32).astype(F8)
 
 
 def right_kernel(yy, yc, rhs):
@@ -110,21 +100,24 @@
             for part in range(3):
                 base = 768 * n + 256 * part
                 rhs[base : base + 256, 768 * side : 768 * side + 768] = unpack(
-                    words[8 * part : 8 * part + 8, :], F8
+                    words[8 * part : 8 * part + 8, :]
                 )
 
 
-def count_kernel(idp, keep, pair, hubs, r0, rp, rm, r2, lhs, rhs, out, near, turned, res):
+def count_kernel(idp, pair, hubs, r0, rp, rm, r2, rhs, out, keep, lhs, near, turned, res):
     y, core, zh, x, zl = place()
     row = 2 * y + core
     z = 2 * zh + zl
     group = (16 - y - z) & 3
     sources = ((r0, 0), (rp, 1), (rm, 3), (r2, 2))
     ids = idp[...]
+    q = (lax.broadcasted_iota(I32, (256, 16), 1) == ids // 768).astype(BF16)
+    r = (lax.broadcasted_iota(I32, (256, 768), 1) == ids % 768).astype(BF16)
+    keep[...] = jnp.where(lax.dot_general(q, r, OUTER, preferred_element_type=F32) > 0.5, 0, -1)
     wordhot = (lax.broadcasted_iota(I32, (256, 48), 1) + 48 * row == ids // 32).astype(F32)
     bithot = (lax.broadcasted_iota(I32, (256, 32), 1) == ids % 32).astype(F32)
     light = 1.0 - lax.dot_general(
-        wordhot.astype(jnp.bfloat16), bithot.astype(jnp.bfloat16), OUTER, preferred_element_type=F32
+        wordhot.astype(BF16), bithot.astype(BF16), OUTER, preferred_element_type=F32
     )
     own = pl.ds(4 * zh + x, 1)
     side = pl.ds(4 * ((zh + 3 + 2 * zl) & 3) + x, 1)
@@ -145,32 +138,70 @@
     lane = lax.broadcasted_iota(I32, (48, 128), 1) // 8
     first = (zl == 0).astype(F32)
     once = ((x == 0) & (z == ((16 - 2 * y) & 3))).astype(F32)
-    for t in range(4):
-        paths = jnp.dot(
-            lhs[384 * t : 384 * t + 384, :], rhs[...], preferred_element_type=F32
+
+    def masked(ref, rel, rows):
+        return ref[rows, :] & keep[pl.ds(4 * group + lax.rem(x + rel, 4), 1), :]
+
+    def fill(tile):
+        half, quarter = tile // 2, tile % 2
+        for n, (ref, rel) in enumerate(sources):
+            words = masked(ref, rel, slice(0, 48))
+            both = octets(words, (16 * half, 16 * half + 8))
+            for b in range(4):
+                lhs[tile % 2, 96 * b : 96 * b + 96, 768 * n : 768 * n + 768] = plane(
+                    both, 4 * quarter + b
+                )
+
+    fill(0)
+    for tile in range(4):
+        half, quarter = tile // 2, tile % 2
+        paths = jnp.dot(lhs[tile % 2], rhs[...], preferred_element_type=F32)
+        if tile < 3:
+            fill(tile + 1)
+        else:
+            for n, (ref, rel) in enumerate(sources):
+                words = octets(masked(ref, rel, slice(48, 56)), (0, 8, 16, 24))
+                for b in range(8):
+                    lhs[0, 32 * b : 32 * b + 32, 768 * n : 768 * n + 768] = plane(words, b)
+        both = octets(mine, (16 * half, 16 * half + 8))
+        edges = jnp.concatenate([plane(both, 4 * quarter + b) for b in range(4)], 0)
+        reach = lax.dot_general(
+            edges, near[...], (((1,), (1,)), ((), ())), preferred_element_type=F32
         )
-        edges = planes(mine, range(8 * t, 8 * t + 8)).astype(F32)
-        reach = lax.dot_general(
-            edges.astype(F8), near[...], (((1,), (1,)), ((), ())), preferred_element_type=F32
-        )
-        for b in range(8):
-            at = 8 * t + b
-            rows = slice(48 * b, 48 * b + 48)
-            words = turned[pl.ds(at, 48, stride=32), :]
-            low = (jnp.right_shift(words, lane) & 1).astype(F32)
-            high = (jnp.right_shift(words, lane + 16) & 1).astype(F32)
-            closed = paths[rows, :] * edges[rows, :]
-            with_hub = reach[rows, :128] * low + reach[rows, 128:] * high
-            res[:, at : at + 1] = (0.5 / (1 << b)) * jnp.sum(
-                closed, axis=1, keepdims=True
-            ) + jnp.sum(with_hub, axis=1, keepdims=True)
-            res[:, 32 + at : 33 + at] = first * jnp.sum(
-                edges[rows, :768], axis=1, keepdims=True
-            ) + once * jnp.sum(low + high, axis=1, keepdims=True)
-    paths = jnp.dot(lhs[1536:1792, :], rhs[...], preferred_element_type=F32)
+        for b in range(4):
+            scale = 1.0 / SCALE[4 * quarter + b]
+            for k in range(2):
+                at = 16 * half + 8 * k + 4 * quarter + b
+                rows = slice(96 * b + 48 * k, 96 * b + 48 * k + 48)
+                words = turned[pl.ds(at, 48, stride=32), :]
+                low = (jnp.right_shift(words, lane) & 1).astype(F32)
+                high = (jnp.right_shift(words, lane + 16) & 1).astype(F32)
+                edge = (jnp.right_shift(mine, at) & 1).astype(F32)
+                closed = jnp.sum(paths[rows, :] * edge, axis=1, keepdims=True)
+                with_hub = jnp.sum(
+                    reach[rows, :128] * low + reach[rows, 128:] * high, axis=1, keepdims=True
+                )
+                res[:, at : at + 1] = (0.5 * scale) * closed + scale * with_hub
+                res[:, 32 + at : 33 + at] = first * jnp.sum(
+                    edge[:, :768], axis=1, keepdims=True
+                ) + once * jnp.sum(low + high, axis=1, keepdims=True)
+    paths = jnp.dot(lhs[0, :256, :], rhs[...], preferred_element_type=F32)
+    tri = jnp.concatenate(
+        [
+            jnp.sum(
+                paths[32 * b + 8 * s : 32 * b + 8 * s + 8, :]
+                * hub_col[64 * s + 8 * b : 64 * s + 8 * b + 8, :],
+                axis=1,
+                keepdims=True,
+            )
+            for s in range(4)
+            for b in range(8)
+        ],
+        0,
+    )
     bit = (lax.broadcasted_iota(I32, (256, 1), 0) // 8) & 7
-    unscale = jnp.right_shift(128, bit).astype(F32) * (0.5 / 128)
-    hub_tri = unscale * jnp.sum(paths * hub_col, axis=1, keepdims=True)
+    unscale = jnp.right_shift(128, bit).astype(F32) * jnp.where(bit == 7, -0.5 / 128, 0.5 / 128)
+    hub_tri = unscale * tri
     hub_deg = first * jnp.sum(hub_col[:, :768], axis=1, keepdims=True)
     hub_part = lax.dot_general(
         wordhot,
@@ -229,23 +260,17 @@
     yc = send(yy, lambda y, core, zh, x, zl: (y, core ^ 1, zh, x, zl))
     planed = hub_ids.reshape(8, 32).T.reshape(256, 1)
     (rhs,) = call(right_kernel, [((3072, 1536), F8)], [], (yy, yc), 1 << 30, 8)
-    lhs, keep = call(
-        left_kernel,
-        [((1792, 3072), F8), ((16, 768), I32)],
-        [],
-        (planed, rows, *ring),
-        1 << 30,
-        12,
-    )
     (table,) = call(
         count_kernel,
         [((32, 256), F32)],
         [
+            pltpu.VMEM((16, 768), I32),
+            pltpu.VMEM((2, 384, 3072), F8),
             pltpu.VMEM((256, 1536), F8),
             pltpu.VMEM((1536, 128), I32),
             pltpu.VMEM((48, 64), F32),
         ],
-        (planed, keep, pair, hubs, rows, *ring, lhs, rhs),
+        (planed, pair, hubs, rows, *ring, rhs),
         1 << 33,
         24,
     )

time: 68.6 us -> 64.2 us (0.936)
  Pallas kernels: 16.2 us -> 12.7 us
  blocking collectives: 16.9 us -> 14.3 us
  waiting for transfers between devices: 7.85 us -> 9.28 us
    pallas_call x3 -> x2, Pallas kernels: 16.2 us -> 12.7 us  [call(): pl.pallas_call(kernel, out_shape=[jax.ShapeDtypeStruct(*o) for o in outs]...]
    all_to_all x1, blocking collectives: 16.9 us -> 14.3 us  [clustering(): everyone = lax.all_to_all(table, ('zh', 'x', 'zl'), 0, 0, tiled=True)]
    ppermute x10, waiting for transfers between devices: 7.85 us -> 9.28 us  [send(): return lax.ppermute(value, AXES, perm=permutation(source))]
  transfers between devices with their start and end apart: 10 -> 10, of which waited for: 5 -> 4; matrix products, arithmetic and copies ran while one was open for 4% -> 4% of each run, Pallas kernels for 4% -> 2%
where the time goes in v6:
time: 64.2 us; the launch traced here: 63.9 us
  starting transfers between devices  24.2 us (38%)
  blocking collectives  14.3 us (22%)
  Pallas kernels  12.7 us (20%)
  waiting for transfers between devices  9.28 us (14%)
  local copies, waits for them, and re-layouts  1.91 us (3%)
  other arithmetic  1.32 us (2%)
    ppermute x10, starting transfers between devices, send(): return lax.ppermute(value, AXES, perm=permutation(source))  24.2 us
    all_to_all x1, blocking collectives, clustering(): everyone = lax.all_to_all(table, ('zh', 'x', 'zl'), 0, 0, tiled=True)  14.3 us
    pallas_call x2, Pallas kernels, call(): pl.pallas_call(kernel, out_shape=[jax.ShapeDtypeStruct(*o) for o in outs]...  12.7 us
    ppermute x10, waiting for transfers between devices, send(): return lax.ppermute(value, AXES, perm=permutation(source))  9.28 us
  transfers between devices with their start and end apart: 10, of which 4 were waited for; matrix products, arithmetic and copies ran while one was open for 4% of the time, Pallas kernels for 2%

profile of v6, /device:TPU:8, one launch (start us, length us, event | category | flops | bytes accessed | tf_op | source)
XLA Modules:
  0.0 63.9 jit_solution(335951606963043074)
XLA Ops:
  0.0 5.9 %collective-permute-start = (s32[48,768]{1,0:T(8,128)}, s32[48,768]{1,0:T(8,128)S(1)}, u32[]{:S(2)}, u32[]{:S(2)}) collective-permute-start(s32[48,768]{1,0:T(8,128)} %param.3), channel_id=1, source_target_pairs={{25,0},{8,1},{27,2},{10,3},{29,4},{12,5},{31,6},{14,7},{1,8},{16,9... | collective-permute-start | bytes 442376 | tf_op jit(solution)/shard_map/ppermute | solution.py:243
  5.9 1.9 %collective-permute-start.3 = (s32[48,768]{1,0:T(8,128)}, s32[48,768]{1,0:T(8,128)S(1)}, u32[]{:S(2)}, u32[]{:S(2)}) collective-permute-start(s32[48,768]{1,0:T(8,128)} %param.3), channel_id=1, source_target_pairs={{0,0},{25,1},{2,2},{27,3},{4,4},{29,5},{6,6},{31,7},{16,8},{9,9},{... | collective-permute-start | bytes 442376 | tf_op jit(solution)/shard_map/ppermute | solution.py:243
  7.8 2.5 %collective-permute-start.1 = (s32[4,768]{1,0:T(4,128)}, s32[4,768]{1,0:T(4,128)S(1)}, u32[]{:S(2)}, u32[]{:S(2)}) collective-permute-start(s32[4,768]{1,0:T(4,128)} %param.4), channel_id=1, source_target_pairs={{1,0},{0,1},{3,2},{2,3},{5,4},{4,5},{7,6},{6,7},{9,8},{8,9},{11,10... | collective-permute-start | bytes 36872 | tf_op jit(solution)/shard_map/ppermute | solution.py:243
  10.3 0.8 %reshape.8 = s32[8,32]{1,0:T(8,128)S(1)} reshape(s32[256]{0:T(256)} %param.5) | data formatting | bytes 2048 | tf_op jit(solution)/shard_map/reshape | solution.py:261
  11.1 0.1 copy.6
  11.1 0.1 reshape.10.idp
  11.3 0.9 %constant_dynamic-update-slice_fusion.1 = s32[96,768]{1,0:T(8,128)S(1)} fusion(s32[48,768]{1,0:T(8,128)} %param.3), kind=kLoop, calls=%fused_computation.3 | loop fusion | bytes 294912
  12.2 0.0 collective-permute-done
  12.2 3.7 %collective-permute-start.8 = (s32[96,768]{1,0:T(8,128)S(1)}, s32[96,768]{1,0:T(8,128)S(1)}, u32[]{:S(2)}, u32[]{:S(2)}) collective-permute-start(s32[96,768]{1,0:T(8,128)S(1)} %constant_dynamic-update-slice_fusion.pair), channel_id=1, source_target_pairs={{0,0},{193,1},{2,2},{195,3},{4,4},{197,5},{6,6},{199,7},{136,8},{7... | collective-permute-start | bytes 884744 | tf_op jit(solution)/shard_map/ppermute | solution.py:243
  15.9 0.0 collective-permute-done.1
  15.9 0.7 %broadcast_select_fusion.1 = (s32[4,768]{1,0:T(4,128)S(1)}, s32[4,768]{1,0:T(4,128)S(1)}) fusion(s32[4,768]{1,0:T(4,128)} %param.4, s32[4,768]{1,0:T(4,128)S(1)} %collective-permute-done.1, pred[]{:T(512)S(6)} %eq.3), kind=kLoop, calls=%fused_computation.7 | loop fusion | flops 6144 | bytes 49153 | tf_op jit(solution)/shard_map/jit(_where)/select_n | solution.py:249
  16.6 0.1 collective-permute-start.2
  16.8 5.1 %collective-permute-start.4 = (s32[8,768]{1,0:T(8,128)S(1)}, s32[8,768]{1,0:T(8,128)S(1)}, u32[]{:S(2)}, u32[]{:S(2)}) collective-permute-start(s32[8,768]{1,0:T(8,128)S(1)} %pad_add_fusion.1), channel_id=1, source_target_pairs={{0,0},{25,1},{2,2},{27,3},{4,4},{29,5},{6,6},{31,7},{16,8},{9,9},{... | collective-permute-start | bytes 73736 | tf_op jit(solution)/shard_map/ppermute | solution.py:243
  21.9 1.7 %collective-permute-done.8.yy = s32[96,768]{1,0:T(8,128)S(1)} collective-permute-done((s32[96,768]{1,0:T(8,128)S(1)}, s32[96,768]{1,0:T(8,128)S(1)}, u32[]{:S(2)}, u32[]{:S(2)}) %collective-permute-start.8) | collective-permute-done | bytes 294944 | tf_op jit(solution)/shard_map/ppermute | solution.py:243
  23.5 0.0 collective-permute-start.9
  23.5 0.0 collective-permute-done.3
  23.5 0.1 collective-permute-done.4
  23.7 2.8 %collective-permute-start.5 = (s32[56,768]{1,0:T(8,128)S(1)}, s32[56,768]{1,0:T(8,128)S(1)}, u32[]{:S(2)}, u32[]{:S(2)}) collective-permute-start(s32[56,768]{1,0:T(8,128)S(1)} %constant_dynamic-update-slice_fusion.2.r0), channel_id=1, source_target_pairs={{2,0},{3,1},{4,2},{5,3},{6,4},{7,5},{0,6},{1,7},{10,8},{11,9},{12,... | collective-permute-start | bytes 516104 | tf_op jit(solution)/shard_map/ppermute | solution.py:243
  26.4 0.0 collective-permute-start.6
  26.5 2.3 %collective-permute-start.7 = (s32[56,768]{1,0:T(8,128)S(1)}, s32[56,768]{1,0:T(8,128)S(1)}, u32[]{:S(2)}, u32[]{:S(2)}) collective-permute-start(s32[56,768]{1,0:T(8,128)S(1)} %constant_dynamic-update-slice_fusion.2.r0), channel_id=1, source_target_pairs={{4,0},{5,1},{6,2},{7,3},{0,4},{1,5},{2,6},{3,7},{12,8},{13,9},{14,... | collective-permute-start | bytes 516104 | tf_op jit(solution)/shard_map/ppermute | solution.py:243
  28.7 0.0 collective-permute-done.2
  28.8 0.0 collective-permute-done.9.yc
  28.8 1.6 %shard_map.37.rhs = f8e4m3fn[3072,1536]{1,0:T(32,128)(4,1)S(1)} custom-call(s32[96,768]{1,0:T(8,128)S(1)} %collective-permute-done.8.yy, s32[96,768]{1,0:T(8,128)S(1)} %collective-permute-done.9.yc), custom_call_target="tpu_custom_call" | custom-call | flops 1073741824 | bytes 1048576 | tf_op jit(solution)/shard_map/pallas_call | solution.py:228
  30.3 4.1 %collective-permute-done.5.rp = s32[56,768]{1,0:T(8,128)S(1)} collective-permute-done((s32[56,768]{1,0:T(8,128)S(1)}, s32[56,768]{1,0:T(8,128)S(1)}, u32[]{:S(2)}, u32[]{:S(2)}) %collective-permute-start.5) | collective-permute-done | bytes 172064 | tf_op jit(solution)/shard_map/ppermute | solution.py:243
  34.4 3.4 %collective-permute-done.6.rm = s32[56,768]{1,0:T(8,128)S(1)} collective-permute-done((s32[56,768]{1,0:T(8,128)S(1)}, s32[56,768]{1,0:T(8,128)S(1)}, u32[]{:S(2)}, u32[]{:S(2)}) %collective-permute-start.6) | collective-permute-done | bytes 172064 | tf_op jit(solution)/shard_map/ppermute | solution.py:243
  37.8 0.0 collective-permute-done.7.r2
  37.8 11.1 %shard_map.38 = f32[32,256]{1,0:T(8,128)S(1)} custom-call(s32[256,1]{1,0:T(8,128)S(1)} %reshape.10.idp, s32[96,768]{1,0:T(8,128)S(1)} %constant_dynamic-update-slice_fusion.pair, s32[16,768]{1,0:T(8,128)S(1)} %pad_add_fusion.hubs, s32[56,768]{1,0:T(8,128)S(1)} %constant_dynamic-update-slice_fusion.2.r0, s32[56,768]{1,0:T(8,128)S(1)} %collective-permute-done.5.rp, ...), custom_call_target="tpu_custom_call" | custom-call | flops 8589934592 | bytes 1048576 | tf_op jit(solution)/shard_map/pallas_call | solution.py:228
  49.0 14.3 %all_to_all.9 = f32[32,1,256]{2,1,0:T(1,128)S(1)} all-to-all(f32[32,1,256]{2,1,0:T(1,128)S(1)} %copy.8), channel_id=1, replica_groups=mesh['y'=4,'core'=2,'zh'=4,'x'=4,'zl'=2] {'zh','x','zl'}, dimensions={0} | all-to-all | bytes 65536 | tf_op jit(solution)/shard_map/all_to_all | solution.py:277
  63.3 0.1 reduce_sum.9
  63.4 0.5 add_divide_fusion
  (6 shorter events, 0.1 us)
Async XLA Ops:
  0.0 12.2 %collective-permute-start = (s32[48,768]{1,0:T(8,128)}, s32[48,768]{1,0:T(8,128)S(1)}, u32[]{:S(2)}, u32[]{:S(2)}) collective-permute-start(s32[48,768]{1,0:T(8,128)} %param.3), channel_id=1, source_target_pairs={{25,0},{8,1},{27,2},{10,3},{29,4},{12,5},{31,6},{14,7},{1,8},{16,9... | collective-permute-start | bytes 442376 | tf_op jit(solution)/shard_map/ppermute | solution.py:243
  5.9 17.7 %collective-permute-start.3 = (s32[48,768]{1,0:T(8,128)}, s32[48,768]{1,0:T(8,128)S(1)}, u32[]{:S(2)}, u32[]{:S(2)}) collective-permute-start(s32[48,768]{1,0:T(8,128)} %param.3), channel_id=1, source_target_pairs={{0,0},{25,1},{2,2},{27,3},{4,4},{29,5},{6,6},{31,7},{16,8},{9,9},{... | collective-permute-start | bytes 442376 | tf_op jit(solution)/shard_map/ppermute | solution.py:243
  7.8 8.1 %collective-permute-start.1 = (s32[4,768]{1,0:T(4,128)}, s32[4,768]{1,0:T(4,128)S(1)}, u32[]{:S(2)}, u32[]{:S(2)}) collective-permute-start(s32[4,768]{1,0:T(4,128)} %param.4), channel_id=1, source_target_pairs={{1,0},{0,1},{3,2},{2,3},{5,4},{4,5},{7,6},{6,7},{9,8},{8,9},{11,10... | collective-permute-start | bytes 36872 | tf_op jit(solution)/shard_map/ppermute | solution.py:243
  12.2 11.3 %collective-permute-start.8 = (s32[96,768]{1,0:T(8,128)S(1)}, s32[96,768]{1,0:T(8,128)S(1)}, u32[]{:S(2)}, u32[]{:S(2)}) collective-permute-start(s32[96,768]{1,0:T(8,128)S(1)} %constant_dynamic-update-slice_fusion.pair), channel_id=1, source_target_pairs={{0,0},{193,1},{2,2},{195,3},{4,4},{197,5},{6,6},{199,7},{136,8},{7... | collective-permute-start | bytes 884744 | tf_op jit(solution)/shard_map/ppermute | solution.py:243
  16.6 12.1 %collective-permute-start.2 = (s32[8,768]{1,0:T(8,128)S(1)}, s32[8,768]{1,0:T(8,128)S(1)}, u32[]{:S(2)}, u32[]{:S(2)}) collective-permute-start(s32[8,768]{1,0:T(8,128)S(1)} %pad_add_fusion.1), channel_id=1, source_target_pairs={{25,0},{8,1},{27,2},{10,3},{29,4},{12,5},{31,6},{14,7},{1,8},{16,9... | collective-permute-start | bytes 73736 | tf_op jit(solution)/shard_map/ppermute | solution.py:243
  16.8 6.9 %collective-permute-start.4 = (s32[8,768]{1,0:T(8,128)S(1)}, s32[8,768]{1,0:T(8,128)S(1)}, u32[]{:S(2)}, u32[]{:S(2)}) collective-permute-start(s32[8,768]{1,0:T(8,128)S(1)} %pad_add_fusion.1), channel_id=1, source_target_pairs={{0,0},{25,1},{2,2},{27,3},{4,4},{29,5},{6,6},{31,7},{16,8},{9,9},{... | collective-permute-start | bytes 73736 | tf_op jit(solution)/shard_map/ppermute | solution.py:243
  23.5 5.2 %collective-permute-start.9 = (s32[96,768]{1,0:T(8,128)S(1)}, s32[96,768]{1,0:T(8,128)S(1)}, u32[]{:S(2)}, u32[]{:S(2)}) collective-permute-start(s32[96,768]{1,0:T(8,128)S(1)} %collective-permute-done.8.yy), channel_id=1, source_target_pairs={{32,0},{33,1},{34,2},{35,3},{36,4},{37,5},{38,6},{39,7},{40,8},{41... | collective-permute-start | bytes 884744 | tf_op jit(solution)/shard_map/ppermute | solution.py:243
  23.7 10.7 %collective-permute-start.5 = (s32[56,768]{1,0:T(8,128)S(1)}, s32[56,768]{1,0:T(8,128)S(1)}, u32[]{:S(2)}, u32[]{:S(2)}) collective-permute-start(s32[56,768]{1,0:T(8,128)S(1)} %constant_dynamic-update-slice_fusion.2.r0), channel_id=1, source_target_pairs={{2,0},{3,1},{4,2},{5,3},{6,4},{7,5},{0,6},{1,7},{10,8},{11,9},{12,... | collective-permute-start | bytes 516104 | tf_op jit(solution)/shard_map/ppermute | solution.py:243
  26.4 11.4 %collective-permute-start.6 = (s32[56,768]{1,0:T(8,128)S(1)}, s32[56,768]{1,0:T(8,128)S(1)}, u32[]{:S(2)}, u32[]{:S(2)}) collective-permute-start(s32[56,768]{1,0:T(8,128)S(1)} %constant_dynamic-update-slice_fusion.2.r0), channel_id=1, source_target_pairs={{6,0},{7,1},{0,2},{1,3},{2,4},{3,5},{4,6},{5,7},{14,8},{15,9},{8,1... | collective-permute-start | bytes 516104 | tf_op jit(solution)/shard_map/ppermute | solution.py:243
  26.5 11.4 %collective-permute-start.7 = (s32[56,768]{1,0:T(8,128)S(1)}, s32[56,768]{1,0:T(8,128)S(1)}, u32[]{:S(2)}, u32[]{:S(2)}) collective-permute-start(s32[56,768]{1,0:T(8,128)S(1)} %constant_dynamic-update-slice_fusion.2.r0), channel_id=1, source_target_pairs={{4,0},{5,1},{6,2},{7,3},{0,4},{1,5},{2,6},{3,7},{12,8},{13,9},{14,... | collective-permute-start | bytes 516104 | tf_op jit(solution)/shard_map/ppermute | solution.py:243

commit v7 on v6

--- a/solution.py
+++ b/solution.py
@@ -71,10 +71,6 @@
     y, core = lax.axis_index("y"), lax.axis_index("core")
     zh, x, zl = lax.axis_index("zh"), lax.axis_index("x"), lax.axis_index("zl")
     return y, core, zh, x, zl
-
-
-def planes(words, bits):
-    return jnp.concatenate([jnp.right_shift(words, b) & 1 for b in bits], 0)
 
 
 def octets(words, at):
@@ -104,29 +100,49 @@
                 )
 
 
-def count_kernel(idp, pair, hubs, r0, rp, rm, r2, rhs, out, keep, lhs, near, turned, res):
+def prep_kernel(idp, pair, hubs, keep, mine, near, light, deg):
+    y, core, zh, x, zl = place()
+    row = 2 * y + core
+    ids = idp[...]
+    q = (lax.broadcasted_iota(I32, (256, 16), 1) == ids // 768).astype(BF16)
+    r = (lax.broadcasted_iota(I32, (256, 768), 1) == ids % 768).astype(BF16)
+    keep[...] = jnp.where(lax.dot_general(q, r, OUTER, preferred_element_type=F32) > 0.5, 0, -1)
+    wordhot = (lax.broadcasted_iota(I32, (256, 48), 1) + 48 * row == ids // 32).astype(BF16)
+    bithot = (lax.broadcasted_iota(I32, (256, 32), 1) == ids % 32).astype(BF16)
+    light[...] = 1.0 - lax.dot_general(wordhot, bithot, OUTER, preferred_element_type=F32)
+    own = pl.ds(4 * zh + x, 1)
+    side = pl.ds(4 * ((zh + 3 + 2 * zl) & 3) + x, 1)
+    left = pair[0:48, :] & keep[own, :]
+    mine[:, 0:768] = left
+    mine[:, 768:1536] = pair[48:96, :] & keep[side, :]
+    for part, line in enumerate((own, side)):
+        words = hubs[8 * part : 8 * part + 8, :] & keep[line, :]
+        for b in range(8):
+            bits = octets(words, (b, 8 + b, 16 + b, 24 + b)) & I8(1)
+            near[32 * b : 32 * b + 32, 768 * part : 768 * part + 768] = bits.astype(
+                BF16
+            ).astype(F8)
+    first = (zl == 0).astype(F32)
+    for at in range(32):
+        edge = (jnp.right_shift(left, at) & 1).astype(F32)
+        deg[:, at : at + 1] = jnp.sum(edge, axis=1, keepdims=True)
+    hub_deg = jnp.sum(near[:, 0:768].astype(F32), axis=1, keepdims=True)
+    hub_deg = lax.dot_general(
+        wordhot.astype(F32),
+        hub_deg * bithot.astype(F32),
+        OUTER,
+        precision=lax.Precision.HIGHEST,
+        preferred_element_type=F32,
+    )
+    deg[...] = first * (deg[...] * light[...] + hub_deg)
+
+
+def count_kernel(idp, keep, mine, near, light, deg, r0, rp, rm, r2, rhs, out, lhs, turned, res):
     y, core, zh, x, zl = place()
     row = 2 * y + core
     z = 2 * zh + zl
     group = (16 - y - z) & 3
     sources = ((r0, 0), (rp, 1), (rm, 3), (r2, 2))
-    ids = idp[...]
-    q = (lax.broadcasted_iota(I32, (256, 16), 1) == ids // 768).astype(BF16)
-    r = (lax.broadcasted_iota(I32, (256, 768), 1) == ids % 768).astype(BF16)
-    keep[...] = jnp.where(lax.dot_general(q, r, OUTER, preferred_element_type=F32) > 0.5, 0, -1)
-    wordhot = (lax.broadcasted_iota(I32, (256, 48), 1) + 48 * row == ids // 32).astype(F32)
-    bithot = (lax.broadcasted_iota(I32, (256, 32), 1) == ids % 32).astype(F32)
-    light = 1.0 - lax.dot_general(
-        wordhot.astype(BF16), bithot.astype(BF16), OUTER, preferred_element_type=F32
-    )
-    own = pl.ds(4 * zh + x, 1)
-    side = pl.ds(4 * ((zh + 3 + 2 * zl) & 3) + x, 1)
-    mine = jnp.concatenate([pair[0:48, :] & keep[own, :], pair[48:96, :] & keep[side, :]], 1)
-    hub_words = jnp.concatenate(
-        [hubs[0:8, :] & keep[own, :], hubs[8:16, :] & keep[side, :]], 1
-    )
-    hub_col = planes(hub_words, range(32)).astype(F32)
-    near[...] = hub_col.astype(F8)
     for side in range(2):
         xs = 2 * core + side
         words = jnp.zeros((8, 768), I32)
@@ -135,8 +151,8 @@
             words = jnp.where(hit, ref[48:56, :], words)
         words = words & keep[pl.ds(2 * row + side, 1), :]
         turned[768 * side : 768 * side + 768, :] = jnp.concatenate([words] * 16, 0).T
-    lane = lax.broadcasted_iota(I32, (48, 128), 1) // 8
-    first = (zl == 0).astype(F32)
+    lane = lax.broadcasted_iota(I32, (48, 128), 1)
+    lane = 8 * ((lane // 8) & 3) + lane // 32
     once = ((x == 0) & (z == ((16 - 2 * y) & 3))).astype(F32)
 
     def masked(ref, rel, rows):
@@ -163,7 +179,7 @@
                 words = octets(masked(ref, rel, slice(48, 56)), (0, 8, 16, 24))
                 for b in range(8):
                     lhs[0, 32 * b : 32 * b + 32, 768 * n : 768 * n + 768] = plane(words, b)
-        both = octets(mine, (16 * half, 16 * half + 8))
+        both = octets(mine[...], (16 * half, 16 * half + 8))
         edges = jnp.concatenate([plane(both, 4 * quarter + b) for b in range(4)], 0)
         reach = lax.dot_general(
             edges, near[...], (((1,), (1,)), ((), ())), preferred_element_type=F32
@@ -175,42 +191,31 @@
                 rows = slice(96 * b + 48 * k, 96 * b + 48 * k + 48)
                 words = turned[pl.ds(at, 48, stride=32), :]
                 low = (jnp.right_shift(words, lane) & 1).astype(F32)
-                high = (jnp.right_shift(words, lane + 16) & 1).astype(F32)
-                edge = (jnp.right_shift(mine, at) & 1).astype(F32)
+                high = (jnp.right_shift(words, lane + 4) & 1).astype(F32)
+                edge = (jnp.right_shift(mine[...], at) & 1).astype(F32)
                 closed = jnp.sum(paths[rows, :] * edge, axis=1, keepdims=True)
                 with_hub = jnp.sum(
                     reach[rows, :128] * low + reach[rows, 128:] * high, axis=1, keepdims=True
                 )
                 res[:, at : at + 1] = (0.5 * scale) * closed + scale * with_hub
-                res[:, 32 + at : 33 + at] = first * jnp.sum(
-                    edge[:, :768], axis=1, keepdims=True
-                ) + once * jnp.sum(low + high, axis=1, keepdims=True)
+                res[:, 32 + at : 33 + at] = once * jnp.sum(low + high, axis=1, keepdims=True)
     paths = jnp.dot(lhs[0, :256, :], rhs[...], preferred_element_type=F32)
-    tri = jnp.concatenate(
-        [
-            jnp.sum(
-                paths[32 * b + 8 * s : 32 * b + 8 * s + 8, :]
-                * hub_col[64 * s + 8 * b : 64 * s + 8 * b + 8, :],
-                axis=1,
-                keepdims=True,
-            )
-            for s in range(4)
-            for b in range(8)
-        ],
-        0,
-    )
-    bit = (lax.broadcasted_iota(I32, (256, 1), 0) // 8) & 7
+    bit = lax.broadcasted_iota(I32, (256, 1), 0) // 32
     unscale = jnp.right_shift(128, bit).astype(F32) * jnp.where(bit == 7, -0.5 / 128, 0.5 / 128)
-    hub_tri = unscale * tri
-    hub_deg = first * jnp.sum(hub_col[:, :768], axis=1, keepdims=True)
-    hub_part = lax.dot_general(
+    hub_tri = unscale * jnp.sum(paths * near[...].astype(F32), axis=1, keepdims=True)
+    ids = idp[...]
+    wordhot = (lax.broadcasted_iota(I32, (256, 48), 1) + 48 * row == ids // 32).astype(F32)
+    bithot = (lax.broadcasted_iota(I32, (256, 32), 1) == ids % 32).astype(F32)
+    hub_tri = lax.dot_general(
         wordhot,
-        jnp.concatenate([hub_tri * bithot, hub_deg * bithot], 1),
+        hub_tri * bithot,
         OUTER,
         precision=lax.Precision.HIGHEST,
         preferred_element_type=F32,
     )
-    total = res[...] * jnp.concatenate([light, light], 1) + hub_part
+    total = jnp.concatenate(
+        [res[:, 0:32] * light[...] + hub_tri, res[:, 32:64] * light[...] + deg[...]], 1
+    )
     for c in range(16):
         line = jnp.concatenate(
             [total[3 * c + k : 3 * c + k + 1, 0:32] for k in range(3)]
@@ -219,8 +224,7 @@
             + [jnp.zeros((1, 32), F32)],
             1,
         )
-        out[2 * c : 2 * c + 1, :] = line
-        out[2 * c + 1 : 2 * c + 2, :] = line
+        out[c : c + 1, :] = line
 
 
 def call(kernel, outs, scratch, args, flops, limit):
@@ -258,24 +262,27 @@
     hubs = jnp.concatenate([hub, hub_beside], 0)
     yy = send(pair, along_y)
     yc = send(yy, lambda y, core, zh, x, zl: (y, core ^ 1, zh, x, zl))
-    planed = hub_ids.reshape(8, 32).T.reshape(256, 1)
+    planed = hub_ids.reshape(8, 4, 8).transpose(2, 1, 0).reshape(256, 1)
+    ready = call(
+        prep_kernel,
+        [((16, 768), I32), ((48, 1536), I32), ((256, 1536), F8), ((48, 32), F32), ((48, 32), F32)],
+        [],
+        (planed, pair, hubs),
+        1 << 30,
+        8,
+    )
     (rhs,) = call(right_kernel, [((3072, 1536), F8)], [], (yy, yc), 1 << 30, 8)
     (table,) = call(
         count_kernel,
-        [((32, 256), F32)],
-        [
-            pltpu.VMEM((16, 768), I32),
-            pltpu.VMEM((2, 384, 3072), F8),
-            pltpu.VMEM((256, 1536), F8),
-            pltpu.VMEM((1536, 128), I32),
-            pltpu.VMEM((48, 64), F32),
-        ],
-        (planed, pair, hubs, rows, *ring, rhs),
+        [((16, 256), F32)],
+        [pltpu.VMEM((2, 384, 3072), F8), pltpu.VMEM((1536, 128), I32), pltpu.VMEM((48, 64), F32)],
+        (planed, *ready, rows, *ring, rhs),
         1 << 33,
         24,
     )
-    everyone = lax.all_to_all(table, ("zh", "x", "zl"), 0, 0, tiled=True)
-    total = jnp.sum(everyone, axis=0)
+    everyone = lax.all_to_all(table, ("zh", "x"), 0, 0, tiled=True)
+    total = jnp.sum(everyone, axis=0, keepdims=True)
+    total = (total + lax.ppermute(total, "zl", [(0, 1), (1, 0)]))[0]
     return total[:OUT] / (1.0 + total[128 : 128 + OUT])
 
 

time: 64.2 us -> 67.3 us (1.048)
  blocking collectives: 14.3 us -> 16.7 us
  waiting for transfers between devices: 9.28 us -> 7.11 us
  starting transfers between devices: 24.2 us -> 26.2 us
  Pallas kernels: 12.7 us -> 13.7 us
    ppermute x10, waiting for transfers between devices: 9.28 us -> 4.19 us  [send(): return lax.ppermute(value, AXES, perm=permutation(source))]
    ppermute x0 -> x1, waiting for transfers between devices: none -> 2.93 us  [clustering(): total = (total + lax.ppermute(total, 'zl', [(0, 1), (1, 0)]))[0]]
    all_to_all x1, blocking collectives: 14.3 us -> 16.7 us  [clustering(): everyone = lax.all_to_all(table, ('zh', 'x'), 0, 0, tiled=True)]
    ppermute x10, starting transfers between devices: 24.2 us -> 25.5 us  [send(): return lax.ppermute(value, AXES, perm=permutation(source))]
    pallas_call x2 -> x3, Pallas kernels: 12.7 us -> 13.7 us  [call(): pl.pallas_call(kernel, out_shape=[jax.ShapeDtypeStruct(*o) for o in outs]...]
    ppermute x0 -> x1, starting transfers between devices: none -> 0.73 us  [clustering(): total = (total + lax.ppermute(total, 'zl', [(0, 1), (1, 0)]))[0]]
  transfers between devices with their start and end apart: 10 -> 11, of which waited for: 4 -> 4; matrix products, arithmetic and copies ran while one was open for 4% -> 4% of each run, Pallas kernels for 2% -> 4%
where the time goes in v7:
time: 67.3 us; the launch traced here: 67.1 us
  starting transfers between devices  26.2 us (39%)
  blocking collectives  16.7 us (25%)
  Pallas kernels  13.7 us (20%)
  waiting for transfers between devices  7.11 us (11%)
  local copies, waits for them, and re-layouts  1.92 us (3%)
  other arithmetic  1.3 us (2%)
    ppermute x10, starting transfers between devices, send(): return lax.ppermute(value, AXES, perm=permutation(source))  25.5 us
    all_to_all x1, blocking collectives, clustering(): everyone = lax.all_to_all(table, ('zh', 'x'), 0, 0, tiled=True)  16.7 us
    pallas_call x3, Pallas kernels, call(): pl.pallas_call(kernel, out_shape=[jax.ShapeDtypeStruct(*o) for o in outs]...  13.7 us
    ppermute x10, waiting for transfers between devices, send(): return lax.ppermute(value, AXES, perm=permutation(source))  4.19 us
    ppermute x1, waiting for transfers between devices, clustering(): total = (total + lax.ppermute(total, 'zl', [(0, 1), (1, 0)]))[0]  2.93 us
  transfers between devices with their start and end apart: 11, of which 4 were waited for; matrix products, arithmetic and copies ran while one was open for 4% of the time, Pallas kernels for 4%

profile of v7, /device:TPU:8, one launch (start us, length us, event | category | flops | bytes accessed | tf_op | source)
XLA Modules:
  0.0 67.1 jit_solution(10750233612401752358)
XLA Ops:
  0.0 5.9 %collective-permute-start = (s32[48,768]{1,0:T(8,128)}, s32[48,768]{1,0:T(8,128)S(1)}, u32[]{:S(2)}, u32[]{:S(2)}) collective-permute-start(s32[48,768]{1,0:T(8,128)} %param.3), channel_id=1, source_target_pairs={{25,0},{8,1},{27,2},{10,3},{29,4},{12,5},{31,6},{14,7},{1,8},{16,9... | collective-permute-start | bytes 442376 | tf_op jit(solution)/shard_map/ppermute | solution.py:247
  5.9 1.9 %collective-permute-start.3 = (s32[48,768]{1,0:T(8,128)}, s32[48,768]{1,0:T(8,128)S(1)}, u32[]{:S(2)}, u32[]{:S(2)}) collective-permute-start(s32[48,768]{1,0:T(8,128)} %param.3), channel_id=1, source_target_pairs={{0,0},{25,1},{2,2},{27,3},{4,4},{29,5},{6,6},{31,7},{16,8},{9,9},{... | collective-permute-start | bytes 442376 | tf_op jit(solution)/shard_map/ppermute | solution.py:247
  7.8 2.5 %collective-permute-start.1 = (s32[4,768]{1,0:T(4,128)}, s32[4,768]{1,0:T(4,128)S(1)}, u32[]{:S(2)}, u32[]{:S(2)}) collective-permute-start(s32[4,768]{1,0:T(4,128)} %param.4), channel_id=1, source_target_pairs={{1,0},{0,1},{3,2},{2,3},{5,4},{4,5},{7,6},{6,7},{9,8},{8,9},{11,10... | collective-permute-start | bytes 36872 | tf_op jit(solution)/shard_map/ppermute | solution.py:247
  10.3 0.9 %constant_dynamic-update-slice_fusion.1 = s32[96,768]{1,0:T(8,128)S(1)} fusion(s32[48,768]{1,0:T(8,128)} %param.3), kind=kLoop, calls=%fused_computation.3 | loop fusion | bytes 294912
  11.2 0.0 collective-permute-done
  11.3 3.7 %collective-permute-start.8 = (s32[96,768]{1,0:T(8,128)S(1)}, s32[96,768]{1,0:T(8,128)S(1)}, u32[]{:S(2)}, u32[]{:S(2)}) collective-permute-start(s32[96,768]{1,0:T(8,128)S(1)} %constant_dynamic-update-slice_fusion.pair), channel_id=1, source_target_pairs={{0,0},{193,1},{2,2},{195,3},{4,4},{197,5},{6,6},{199,7},{136,8},{7... | collective-permute-start | bytes 884744 | tf_op jit(solution)/shard_map/ppermute | solution.py:247
  15.0 0.0 collective-permute-done.1
  15.0 0.7 %broadcast_select_fusion.1 = (s32[4,768]{1,0:T(4,128)S(1)}, s32[4,768]{1,0:T(4,128)S(1)}) fusion(s32[4,768]{1,0:T(4,128)} %param.4, s32[4,768]{1,0:T(4,128)S(1)} %collective-permute-done.1, pred[]{:T(512)S(6)} %eq.3), kind=kLoop, calls=%fused_computation.7 | loop fusion | flops 6144 | bytes 49153 | tf_op jit(solution)/shard_map/jit(_where)/select_n | solution.py:253
  15.7 1.0 %collective-permute-start.2 = (s32[8,768]{1,0:T(8,128)S(1)}, s32[8,768]{1,0:T(8,128)S(1)}, u32[]{:S(2)}, u32[]{:S(2)}) collective-permute-start(s32[8,768]{1,0:T(8,128)S(1)} %pad_add_fusion.1), channel_id=1, source_target_pairs={{25,0},{8,1},{27,2},{10,3},{29,4},{12,5},{31,6},{14,7},{1,8},{16,9... | collective-permute-start | bytes 73736 | tf_op jit(solution)/shard_map/ppermute | solution.py:247
  16.8 0.8 %reshape.13 = s32[8,4,8]{2,1,0:T(4,128)S(1)} reshape(s32[256]{0:T(256)} %param.5) | data formatting | bytes 2048 | tf_op jit(solution)/shard_map/reshape | solution.py:265
  17.5 0.1 copy.7
  17.6 0.1 reshape.15.idp
  17.7 4.2 %collective-permute-start.4 = (s32[8,768]{1,0:T(8,128)S(1)}, s32[8,768]{1,0:T(8,128)S(1)}, u32[]{:S(2)}, u32[]{:S(2)}) collective-permute-start(s32[8,768]{1,0:T(8,128)S(1)} %pad_add_fusion.1), channel_id=1, source_target_pairs={{0,0},{25,1},{2,2},{27,3},{4,4},{29,5},{6,6},{31,7},{16,8},{9,9},{... | collective-permute-start | bytes 73736 | tf_op jit(solution)/shard_map/ppermute | solution.py:247
  21.9 0.0 collective-permute-done.2
  22.0 0.6 collective-permute-done.8.yy
  22.6 0.0 collective-permute-start.9
  22.6 0.0 collective-permute-done.3
  22.6 2.1 %collective-permute-done.4 = s32[8,768]{1,0:T(8,128)S(1)} collective-permute-done((s32[8,768]{1,0:T(8,128)S(1)}, s32[8,768]{1,0:T(8,128)S(1)}, u32[]{:S(2)}, u32[]{:S(2)}) %collective-permute-start.4) | collective-permute-done | bytes 24608 | tf_op jit(solution)/shard_map/ppermute | solution.py:247
  24.7 3.0 %collective-permute-start.7 = (s32[56,768]{1,0:T(8,128)S(1)}, s32[56,768]{1,0:T(8,128)S(1)}, u32[]{:S(2)}, u32[]{:S(2)}) collective-permute-start(s32[56,768]{1,0:T(8,128)S(1)} %constant_dynamic-update-slice_fusion.2.r0), channel_id=1, source_target_pairs={{4,0},{5,1},{6,2},{7,3},{0,4},{1,5},{2,6},{3,7},{12,8},{13,9},{14,... | collective-permute-start | bytes 516104 | tf_op jit(solution)/shard_map/ppermute | solution.py:247
  27.7 0.6 collective-permute-start.6
  28.3 2.6 %collective-permute-start.5 = (s32[56,768]{1,0:T(8,128)S(1)}, s32[56,768]{1,0:T(8,128)S(1)}, u32[]{:S(2)}, u32[]{:S(2)}) collective-permute-start(s32[56,768]{1,0:T(8,128)S(1)} %constant_dynamic-update-slice_fusion.2.r0), channel_id=1, source_target_pairs={{2,0},{3,1},{4,2},{5,3},{6,4},{7,5},{0,6},{1,7},{10,8},{11,9},{12,... | collective-permute-start | bytes 516104 | tf_op jit(solution)/shard_map/ppermute | solution.py:247
  30.9 1.3 %shard_map.37 = (s32[16,768]{1,0:T(8,128)S(1)}, s32[48,1536]{1,0:T(8,128)S(1)}, f8e4m3fn[256,1536]{1,0:T(32,128)(4,1)S(1)}, f32[48,32]{1,0:T(8,128)S(1)}, f32[48,32]{1,0:T(8,128)S(1)}) custom-call(s32[256,1]{1,0:T(8,128)S(1)} %reshape.15.idp, s32[96,768]{1,0:T(8,128)S(1)} %constant_dynamic-update-slice_fusion.pair, s32[16,768]{1,0:T(8,128)S(1)} %pad_add_fusion.hubs), custom_call_target="tpu_custom_call" | custom-call | flops 1073741824 | bytes 1048576 | tf_op jit(solution)/shard_map/pallas_call | solution.py:232
  32.2 0.0 collective-permute-done.9.yc
  32.2 1.6 %shard_map.38.rhs = f8e4m3fn[3072,1536]{1,0:T(32,128)(4,1)S(1)} custom-call(s32[96,768]{1,0:T(8,128)S(1)} %collective-permute-done.8.yy, s32[96,768]{1,0:T(8,128)S(1)} %collective-permute-done.9.yc), custom_call_target="tpu_custom_call" | custom-call | flops 1073741824 | bytes 1048576 | tf_op jit(solution)/shard_map/pallas_call | solution.py:232
  33.8 0.0 collective-permute-done.7.r2
  33.8 1.5 %collective-permute-done.6.rm = s32[56,768]{1,0:T(8,128)S(1)} collective-permute-done((s32[56,768]{1,0:T(8,128)S(1)}, s32[56,768]{1,0:T(8,128)S(1)}, u32[]{:S(2)}, u32[]{:S(2)}) %collective-permute-start.6) | collective-permute-done | bytes 172064 | tf_op jit(solution)/shard_map/ppermute | solution.py:247
  35.3 0.0 collective-permute-done.5.rp
  35.3 10.9 %shard_map.39 = f32[16,256]{1,0:T(8,128)S(1)} custom-call(s32[256,1]{1,0:T(8,128)S(1)} %reshape.15.idp, s32[16,768]{1,0:T(8,128)S(1)} %get-tuple-element.10.keep, s32[48,1536]{1,0:T(8,128)S(1)} %get-tuple-element.11.mine, f8e4m3fn[256,1536]{1,0:T(32,128)(4,1)S(1)} %get-tuple-element.12.near, f32[48,32]{1,0:T(8,128)S(1)} %get-tuple-element.13.light, ...), custom_call_target="tpu_custom_call" | custom-call | flops 8589934592 | bytes 1048576 | tf_op jit(solution)/shard_map/pallas_call | solution.py:232
  46.2 16.7 %all_to_all.9 = f32[16,1,256]{2,1,0:T(1,128)S(1)} all-to-all(f32[16,1,256]{2,1,0:T(1,128)S(1)} %copy.10), channel_id=1, replica_groups=mesh['y'=4,'core'=2,'zh'=4,'x'=4,'zl'=2] {'zh','x'}, dimensions={0} | all-to-all | bytes 32768 | tf_op jit(solution)/shard_map/all_to_all | solution.py:283
  62.9 0.7 %collective-permute-start.10 = (f32[1,256]{1,0:T(1,128)S(1)}, f32[1,256]{1,0:T(1,128)S(1)}, u32[]{:S(2)}, u32[]{:S(2)}) collective-permute-start(f32[1,256]{1,0:T(1,128)S(1)} %bitcast.7), channel_id=1, source_target_pairs={{0,1},{1,0},{2,3},{3,2},{4,5},{5,4},{6,7},{7,6},{8,9},{9,8},{10,11... | collective-permute-start | bytes 3080 | tf_op jit(solution)/shard_map/ppermute | solution.py:285
  63.6 2.9 %collective-permute-done.10 = f32[1,256]{1,0:T(1,128)S(1)} collective-permute-done((f32[1,256]{1,0:T(1,128)S(1)}, f32[1,256]{1,0:T(1,128)S(1)}, u32[]{:S(2)}, u32[]{:S(2)}) %collective-permute-start.10) | collective-permute-done | bytes 1056 | tf_op jit(solution)/shard_map/ppermute | solution.py:285
  66.5 0.5 fusion.1
  (8 shorter events, 0.1 us)
Async XLA Ops:
  0.0 11.2 %collective-permute-start = (s32[48,768]{1,0:T(8,128)}, s32[48,768]{1,0:T(8,128)S(1)}, u32[]{:S(2)}, u32[]{:S(2)}) collective-permute-start(s32[48,768]{1,0:T(8,128)} %param.3), channel_id=1, source_target_pairs={{25,0},{8,1},{27,2},{10,3},{29,4},{12,5},{31,6},{14,7},{1,8},{16,9... | collective-permute-start | bytes 442376 | tf_op jit(solution)/shard_map/ppermute | solution.py:247
  5.9 16.7 %collective-permute-start.3 = (s32[48,768]{1,0:T(8,128)}, s32[48,768]{1,0:T(8,128)S(1)}, u32[]{:S(2)}, u32[]{:S(2)}) collective-permute-start(s32[48,768]{1,0:T(8,128)} %param.3), channel_id=1, source_target_pairs={{0,0},{25,1},{2,2},{27,3},{4,4},{29,5},{6,6},{31,7},{16,8},{9,9},{... | collective-permute-start | bytes 442376 | tf_op jit(solution)/shard_map/ppermute | solution.py:247
  7.8 7.2 %collective-permute-start.1 = (s32[4,768]{1,0:T(4,128)}, s32[4,768]{1,0:T(4,128)S(1)}, u32[]{:S(2)}, u32[]{:S(2)}) collective-permute-start(s32[4,768]{1,0:T(4,128)} %param.4), channel_id=1, source_target_pairs={{1,0},{0,1},{3,2},{2,3},{5,4},{4,5},{7,6},{6,7},{9,8},{8,9},{11,10... | collective-permute-start | bytes 36872 | tf_op jit(solution)/shard_map/ppermute | solution.py:247
  11.3 11.3 %collective-permute-start.8 = (s32[96,768]{1,0:T(8,128)S(1)}, s32[96,768]{1,0:T(8,128)S(1)}, u32[]{:S(2)}, u32[]{:S(2)}) collective-permute-start(s32[96,768]{1,0:T(8,128)S(1)} %constant_dynamic-update-slice_fusion.pair), channel_id=1, source_target_pairs={{0,0},{193,1},{2,2},{195,3},{4,4},{197,5},{6,6},{199,7},{136,8},{7... | collective-permute-start | bytes 884744 | tf_op jit(solution)/shard_map/ppermute | solution.py:247
  15.7 6.2 %collective-permute-start.2 = (s32[8,768]{1,0:T(8,128)S(1)}, s32[8,768]{1,0:T(8,128)S(1)}, u32[]{:S(2)}, u32[]{:S(2)}) collective-permute-start(s32[8,768]{1,0:T(8,128)S(1)} %pad_add_fusion.1), channel_id=1, source_target_pairs={{25,0},{8,1},{27,2},{10,3},{29,4},{12,5},{31,6},{14,7},{1,8},{16,9... | collective-permute-start | bytes 73736 | tf_op jit(solution)/shard_map/ppermute | solution.py:247
  17.7 6.9 %collective-permute-start.4 = (s32[8,768]{1,0:T(8,128)S(1)}, s32[8,768]{1,0:T(8,128)S(1)}, u32[]{:S(2)}, u32[]{:S(2)}) collective-permute-start(s32[8,768]{1,0:T(8,128)S(1)} %pad_add_fusion.1), channel_id=1, source_target_pairs={{0,0},{25,1},{2,2},{27,3},{4,4},{29,5},{6,6},{31,7},{16,8},{9,9},{... | collective-permute-start | bytes 73736 | tf_op jit(solution)/shard_map/ppermute | solution.py:247
  22.6 9.6 %collective-permute-start.9 = (s32[96,768]{1,0:T(8,128)S(1)}, s32[96,768]{1,0:T(8,128)S(1)}, u32[]{:S(2)}, u32[]{:S(2)}) collective-permute-start(s32[96,768]{1,0:T(8,128)S(1)} %collective-permute-done.8.yy), channel_id=1, source_target_pairs={{32,0},{33,1},{34,2},{35,3},{36,4},{37,5},{38,6},{39,7},{40,8},{41... | collective-permute-start | bytes 884744 | tf_op jit(solution)/shard_map/ppermute | solution.py:247
  24.7 9.1 %collective-permute-start.7 = (s32[56,768]{1,0:T(8,128)S(1)}, s32[56,768]{1,0:T(8,128)S(1)}, u32[]{:S(2)}, u32[]{:S(2)}) collective-permute-start(s32[56,768]{1,0:T(8,128)S(1)} %constant_dynamic-update-slice_fusion.2.r0), channel_id=1, source_target_pairs={{4,0},{5,1},{6,2},{7,3},{0,4},{1,5},{2,6},{3,7},{12,8},{13,9},{14,... | collective-permute-start | bytes 516104 | tf_op jit(solution)/shard_map/ppermute | solution.py:247
  27.7 7.6 %collective-permute-start.6 = (s32[56,768]{1,0:T(8,128)S(1)}, s32[56,768]{1,0:T(8,128)S(1)}, u32[]{:S(2)}, u32[]{:S(2)}) collective-permute-start(s32[56,768]{1,0:T(8,128)S(1)} %constant_dynamic-update-slice_fusion.2.r0), channel_id=1, source_target_pairs={{6,0},{7,1},{0,2},{1,3},{2,4},{3,5},{4,6},{5,7},{14,8},{15,9},{8,1... | collective-permute-start | bytes 516104 | tf_op jit(solution)/shard_map/ppermute | solution.py:247
  28.3 7.0 %collective-permute-start.5 = (s32[56,768]{1,0:T(8,128)S(1)}, s32[56,768]{1,0:T(8,128)S(1)}, u32[]{:S(2)}, u32[]{:S(2)}) collective-permute-start(s32[56,768]{1,0:T(8,128)S(1)} %constant_dynamic-update-slice_fusion.2.r0), channel_id=1, source_target_pairs={{2,0},{3,1},{4,2},{5,3},{6,4},{7,5},{0,6},{1,7},{10,8},{11,9},{12,... | collective-permute-start | bytes 516104 | tf_op jit(solution)/shard_map/ppermute | solution.py:247
  62.9 3.7 %collective-permute-start.10 = (f32[1,256]{1,0:T(1,128)S(1)}, f32[1,256]{1,0:T(1,128)S(1)}, u32[]{:S(2)}, u32[]{:S(2)}) collective-permute-start(f32[1,256]{1,0:T(1,128)S(1)} %bitcast.7), channel_id=1, source_target_pairs={{0,1},{1,0},{2,3},{3,2},{4,5},{5,4},{6,7},{7,6},{8,9},{9,8},{10,11... | collective-permute-start | bytes 3080 | tf_op jit(solution)/shard_map/ppermute | solution.py:285
